TPU v7x, 16 devices: a whole 2x2x2 slice. The times are simulated.
16 devices in a mesh: dp: 2 (over z), dap: 8 (over y, x, core).
Axes of the slice: x: 2, y: 2, z: 2, core: 2. Of those that a mesh axis runs over, the one named last changes fastest.
Arguments:
- z_pair: bfloat16 [2, 256, 256, 128], P('dp', 'dap')
- pair_mask: int32 [2, 256, 256], P('dp', 'dap')
- dz_out: bfloat16 [2, 256, 256, 128], P('dp', 'dap')
- ln_in: bfloat16 [2, 2, 128], replicated
- w_proj: bfloat16 [2, 128, 640], replicated
- b_proj: bfloat16 [2, 640], replicated
- ln_mid: bfloat16 [2, 2, 128], replicated
- w_out: bfloat16 [2, 128, 128], replicated
- b_out: bfloat16 [2, 128], replicated
Outputs:
- output 1: bfloat16 [2, 256, 256, 128], P('dp', 'dap')
- output 2: bfloat16 [2, 256, 256, 128], P('dp', 'dap')
- output 3: float32 [2, 2, 128], replicated
- output 4: float32 [2, 128, 640], replicated
- output 5: float32 [2, 640], replicated
- output 6: float32 [2, 2, 128], replicated
- output 7: float32 [2, 128, 128], replicated
- output 8: float32 [2, 128], replicated
All inputs are finite; a program needn't handle non-finite values.
Results may differ from a plain program's by a relative error of at most 0.0119678.
Values are sent between devices in bfloat16 or wider.
A program may use at most 1 GiB of HBM per device.

v0:
```python
import jax
import jax.numpy as jnp
import functools
from jax import lax
from jax.sharding import PartitionSpec as P, NamedSharding

LN_EPS = 1e-5


def layer_norm(values, ln_gain, ln_bias):
    mean_val = jnp.mean(values, axis=-1, keepdims=True)
    centered = values - mean_val
    variance = jnp.mean(centered * centered, axis=-1, keepdims=True)
    return centered * lax.rsqrt(variance + LN_EPS) * ln_gain + ln_bias


def norm_bf16(values, ln_gain, ln_bias):
    return layer_norm(values, ln_gain, ln_bias).astype(jnp.bfloat16)


def split_gates(proj_all, mask_f, hidden):
    a_side = (jax.nn.sigmoid(proj_all[..., :hidden]) * proj_all[..., hidden:2 * hidden] * mask_f).astype(jnp.bfloat16)
    b_side = (jax.nn.sigmoid(proj_all[..., 2 * hidden:3 * hidden]) * proj_all[..., 3 * hidden:4 * hidden] * mask_f).astype(jnp.bfloat16)
    g_side = jax.nn.sigmoid(proj_all[..., 4 * hidden:])
    return a_side, b_side, g_side


def pre_forward(z_in, mask_f, ln_pair, w_proj, b_proj):
    hidden = (w_proj.shape[1] - w_proj.shape[0]) // 4
    z_hat, ln_pull = jax.vjp(norm_bf16, z_in.astype(jnp.float32), ln_pair[0], ln_pair[1])
    proj_all = jnp.einsum("pijc,ck->pijk", z_hat, w_proj, preferred_element_type=jnp.float32) + b_proj
    (a_side, b_side, g_side), gate_pull = jax.vjp(functools.partial(split_gates, mask_f=mask_f, hidden=hidden), proj_all)
    return a_side, b_side, g_side, (z_hat, ln_pull, gate_pull)


def post_forward(tri_x, g_side, z_in, ln_pair, w_out, b_out):
    x_hat, mid_pull = jax.vjp(norm_bf16, tri_x, ln_pair[0], ln_pair[1])
    update = jnp.einsum("pijh,hc->pijc", x_hat, w_out, preferred_element_type=jnp.float32) + b_out
    z_new = (z_in.astype(jnp.float32) + g_side * update).astype(jnp.bfloat16)
    return z_new, (x_hat, mid_pull, update)


def post_backward(dz_new, g_side, w_out, saved_parts):
    x_hat, mid_pull, update = saved_parts
    dz_f32 = dz_new.astype(jnp.float32)
    d_gate = dz_f32 * update
    d_update = dz_f32 * g_side
    d_b_out = jnp.sum(d_update, axis=(0, 1, 2))
    d_upd_bf = d_update.astype(jnp.bfloat16)
    d_w_out = jnp.einsum("pijh,pijc->hc", x_hat, d_upd_bf, preferred_element_type=jnp.float32)
    value_a6 = jnp.einsum("pijc,hc->pijh", d_upd_bf, w_out, preferred_element_type=jnp.float32).astype(jnp.bfloat16)
    d_tri, d_mid_gain, d_mid_bias = mid_pull(value_a6)
    return d_tri, d_gate, dz_f32, (jnp.stack([d_mid_gain, d_mid_bias]), d_w_out, d_b_out)


def pre_backward(d_a_side, d_b_side, d_gate, w_proj, saved_parts):
    z_hat, ln_pull, gate_pull = saved_parts
    (d_proj,) = gate_pull((d_a_side, d_b_side, d_gate))
    d_b_proj = jnp.sum(d_proj, axis=(0, 1, 2))
    d_proj_bf = d_proj.astype(jnp.bfloat16)
    d_w_proj = jnp.einsum("pijc,pijk->ck", z_hat, d_proj_bf, preferred_element_type=jnp.float32)
    d_zhat = jnp.einsum("pijk,ck->pijc", d_proj_bf, w_proj, preferred_element_type=jnp.float32).astype(jnp.bfloat16)
    dz_norm, d_in_gain, d_in_bias = ln_pull(d_zhat)
    return dz_norm, (jnp.stack([d_in_gain, d_in_bias]), d_w_proj, d_b_proj)


def collect_grads(pre_first, post_first, pre_second, post_second):
    return (jnp.stack([pre_first[0], pre_second[0]]), jnp.stack([pre_first[1], pre_second[1]]), jnp.stack([pre_first[2], pre_second[2]]), jnp.stack([post_first[0], post_second[0]]), jnp.stack([post_first[1], post_second[1]]), jnp.stack([post_first[2], post_second[2]]))


def solution(mesh):
    def local_step(z_pair, pair_mask, dz_out, ln_in, w_proj, b_proj, ln_mid, w_out, b_out):
        mask_f = pair_mask.astype(jnp.float32)[..., None]
        ln_in32 = ln_in.astype(jnp.float32)
        b_proj32 = b_proj.astype(jnp.float32)
        ln_mid32 = ln_mid.astype(jnp.float32)
        b_out32 = b_out.astype(jnp.float32)
        a_rows0, b_rows0, g_rows0, keep_pre0 = pre_forward(z_pair, mask_f, ln_in32[0], w_proj[0], b_proj32[0])
        b_full0 = lax.all_gather(b_rows0, "dap", axis=1, tiled=True)
        tri_x0 = jnp.einsum("pikc,pjkc->pijc", a_rows0, b_full0, preferred_element_type=jnp.float32)
        z_mid, keep_post0 = post_forward(tri_x0, g_rows0, z_pair, ln_mid32[0], w_out[0], b_out32[0])
        a_rows1, b_rows1, g_rows1, keep_pre1 = pre_forward(z_mid, mask_f, ln_in32[1], w_proj[1], b_proj32[1])
        a_cols1 = lax.all_to_all(a_rows1, "dap", 2, 1, tiled=True)
        b_full1 = lax.all_gather(b_rows1, "dap", axis=1, tiled=True)
        tri_x1 = jnp.einsum("pkic,pkjc->pijc", a_cols1, b_full1, preferred_element_type=jnp.float32)
        z_new, keep_post1 = post_forward(tri_x1, g_rows1, z_mid, ln_mid32[1], w_out[1], b_out32[1])
        d_tri1, d_gate1, d_res1, grads_post1 = post_backward(dz_out, g_rows1, w_out[1], keep_post1)
        d_trib1 = d_tri1.astype(jnp.bfloat16)
        d_acols1 = jnp.einsum("pijc,pkjc->pkic", d_trib1, b_full1, preferred_element_type=jnp.float32).astype(jnp.bfloat16)
        d_arows1 = lax.all_to_all(d_acols1, "dap", 1, 2, tiled=True)
        d_bpart1 = jnp.einsum("pkic,pijc->pkjc", a_cols1, d_trib1, preferred_element_type=jnp.float32).astype(jnp.bfloat16)
        d_brows1 = lax.psum_scatter(d_bpart1, "dap", scatter_dimension=1, tiled=True)
        dz_norm1, grads_pre1 = pre_backward(d_arows1, d_brows1, d_gate1, w_proj[1], keep_pre1)
        dz_mid = (d_res1 + dz_norm1).astype(jnp.bfloat16)
        d_tri0, d_gate0, d_res0, grads_post0 = post_backward(dz_mid, g_rows0, w_out[0], keep_post0)
        d_trib0 = d_tri0.astype(jnp.bfloat16)
        d_arows0 = jnp.einsum("pijc,pjkc->pikc", d_trib0, b_full0, preferred_element_type=jnp.float32).astype(jnp.bfloat16)
        d_bpart0 = jnp.einsum("pijc,pikc->pjkc", d_trib0, a_rows0, preferred_element_type=jnp.float32).astype(jnp.bfloat16)
        d_brows0 = lax.psum_scatter(d_bpart0, "dap", scatter_dimension=1, tiled=True)
        dz_norm0, grads_pre0 = pre_backward(d_arows0, d_brows0, d_gate0, w_proj[0], keep_pre0)
        dz_pair = (d_res0 + dz_norm0).astype(jnp.bfloat16)
        grads_all = lax.psum(collect_grads(grads_pre0, grads_post0, grads_pre1, grads_post1), ("dp", "dap"))
        return (z_new, dz_pair) + grads_all

    row_spec = P("dp", "dap")
    return jax.shard_map(local_step, mesh=mesh, in_specs=(row_spec, row_spec, row_spec, P(), P(), P(), P(), P(), P()), out_specs=(row_spec, row_spec, P(), P(), P(), P(), P(), P()), check_vma=False)
```

profile of v0, /device:TPU:0, one launch (start us, length us, event | category | flops | bytes accessed | tf_op | source)
XLA Modules:
  0.0 804.5 jit_solution(6729829500885513188)
XLA Ops:
  19.0 5.5 fusion.104
  32.5 83.6 %all-gather.3.cloned.1.call-done = bf16[1,256,256,128]{3,2,0,1:T(8,128)(2,1)} async-done(((bf16[1,32,256,128]{3,2,0,1:T(8,128)(2,1)}), bf16[1,256,256,128]{3,2,0,1:T(8,128)(2,1)}) %all-gather.3.cloned.1.call-update) | async-done | bytes 16777232 | tf_op jit(solution)/shard_map/all_gather | solution.py:79
  116.1 21.9 %copy.119 = bf16[1,256,256,128]{2,1,3,0:T(8,128)(2,1)} copy(bf16[1,256,256,128]{3,2,0,1:T(8,128)(2,1)} %all-gather.3.cloned.1.call-done) | data formatting | bytes 33554432 | tf_op jit(solution)/shard_map/all_gather | solution.py:79
  138.0 9.9 %bitcast_reduce_fusion.1 = (f32[32,256]{1,0:T(8,128)S(1)}, f32[128,256,32]{1,2,0:T(8,128)S(1)}) fusion(bf16[32,256,128]{1,0,2:T(8,128)(2,1)} %copy.120, bf16[1,256,256,128]{2,1,3,0:T(8,128)(2,1)} %copy.119), kind=kOutput, calls=%fused_computation.147 | convolution fusion | flops 537911296 | bytes 23101440 | tf_op jit(solution)/shard_map/pikc,pjkc->pijc/dot_general | solution.py:80
  149.9 7.2 convert_reduce_fusion.4
  177.7 5.4 fusion.158
  186.5 39.8 %all-to-all-done = bf16[1,32,256,128]{3,1,0,2:T(8,128)(2,1)} async-done(((bf16[1,32,256,128]{3,1,0,2:T(8,128)(2,1)}), bf16[1,32,256,128]{3,1,0,2:T(8,128)(2,1)}, u32[]{:S(2)}, u32[]{:S(2)}) %all-to-all-start) | async-done | bytes 2097184 | tf_op jit(solution)/shard_map/all_to_all | solution.py:83
  235.4 43.1 %all-gather.5.cloned.1.call-done = bf16[1,256,256,128]{3,2,0,1:T(8,128)(2,1)} async-done(((bf16[1,32,256,128]{3,2,0,1:T(8,128)(2,1)}), bf16[1,256,256,128]{3,2,0,1:T(8,128)(2,1)}) %all-gather.5.cloned.1.call-update) | async-done | bytes 16777232 | tf_op jit(solution)/shard_map/all_gather | solution.py:84
  278.5 21.8 %copy.125 = bf16[1,256,256,128]{2,1,3,0:T(8,128)(2,1)} copy(bf16[1,256,256,128]{3,2,0,1:T(8,128)(2,1)} %all-gather.5.cloned.1.call-done) | data formatting | bytes 33554432 | tf_op jit(solution)/shard_map/all_gather | solution.py:84
  300.3 9.4 %bitcast_reduce_fusion = (f32[32,256]{1,0:T(8,128)S(1)}, f32[128,256,32]{1,2,0:T(8,128)S(1)}) fusion(bf16[256,32,128]{0,1,2:T(8,128)(2,1)} %copy.129, bf16[1,256,256,128]{2,1,3,0:T(8,128)(2,1)} %copy.125), kind=kOutput, calls=%fused_computation.144 | convolution fusion | flops 537911296 | bytes 23101440 | tf_op jit(solution)/shard_map/pkic,pkjc->pijc/dot_general | solution.py:85
  317.1 12.6 %fusion.179 = bf16[128,256,256]{2,1,0:T(8,128)(2,1)} fusion(bf16[32,256,128]{1,0,2:T(8,128)(2,1)} %get-tuple-element.58, bf16[256,32,128]{0,1,2:T(8,128)(2,1)} %copy.129), kind=kOutput, calls=%fused_computation.258 | convolution fusion | flops 536870912 | bytes 20971520 | tf_op jit(solution)/shard_map/pkic,pijc->pkjc/dot_general | solution.py:91
  329.7 24.4 %copy.133 = bf16[128,256,256]{0,1,2:T(8,128)(2,1)} copy(bf16[128,256,256]{2,1,0:T(8,128)(2,1)} %fusion.179) | data formatting | bytes 33554432 | tf_op jit(solution)/shard_map/pkic,pijc->pkjc/dot_general | solution.py:91
  354.1 11.0 %convert_bitcast_fusion.8 = bf16[1,256,32,128]{1,2,3,0:T(8,128)(2,1)} fusion(bf16[32,256,128]{1,0,2:T(8,128)(2,1)} %get-tuple-element.58, bf16[1,256,256,128]{2,1,3,0:T(8,128)(2,1)} %copy.125), kind=kOutput, calls=%fused_computation.180 | convolution fusion | flops 537919488 | bytes 20971520 | tf_op jit(solution)/shard_map/pijc,pkjc->pkic/dot_general | solution.py:89
  370.2 42.1 %all_to_all.24 = bf16[1,256,32,128]{3,2,0,1:T(8,128)(2,1)S(1)} all-to-all(bf16[1,256,32,128]{3,2,0,1:T(8,128)(2,1)} %copy.134), channel_id=1, replica_groups=mesh['dp'=2,'dap'=8] {'dap'}, dimensions={1} | all-to-all | bytes 4194304 | tf_op jit(solution)/shard_map/all_to_all | solution.py:90
  415.4 59.9 %reduce-scatter.3.cloned.1.call-done = bf16[1,32,256,128]{3,2,1,0:T(8,128)(2,1)} async-done(((bf16[1,256,256,128]{3,2,1,0:T(8,128)(2,1)}), bf16[1,32,256,128]{3,2,1,0:T(8,128)(2,1)}) %reduce-scatter.3.cloned.1.call-update) | async-done | bytes 2097168 | tf_op jit(solution)/shard_map/reduce_scatter | solution.py:92
  475.3 20.3 %fusion.60 = (f32[1,32,256,128]{3,2,1,0:T(8,128)}, bf16[1,32,256,128]{3,2,1,0:T(8,128)(2,1)}, f32[128]{0:T(128)S(1)}, f32[1,32,256,128]{3,2,1,0:T(8,128)}, f32[1...) fusion(bf16[1,32,256,128]{3,2,1,0:T(8,128)(2,1)} %param.11, ...), kind=kOutput, calls=%fused_computation.100 | convolution fusion | flops 304086912 | bytes 56689664 | tf_op jit(solution)/shard_map/pijh,hc->pijc/dot_general | solution.py:38
  495.7 9.2 %fusion.16 = (f32[640]{0:T(1024)S(1)}, bf16[1,32,256,640]{3,2,1,0:T(8,128)(2,1)S(1)}) fusion(f32[1,32,256,128]{3,2,1,0:T(8,128)} %get-tuple-element.55, f32[1,32,256,128]{3,2,1,0:T(8,128)} %get-tuple-element.54, f32[1,32,256,128]{3,2,1,0:T(8,128)} %get-tuple-element.56, f32[1,32,256,128]{3,2,1,0:T(8,128)} %get-tuple-element.57, ...), kind=kLoop, calls=%fused_computation.22 | loop fusion | flops 31456640 | bytes 31459840 | tf_op jit(solution)/shard_map/reduce_sum | solution.py:59
  508.9 6.2 fusion.42
  515.1 7.6 fusion.98
  543.8 12.5 %fusion.180 = bf16[128,256,256]{2,1,0:T(8,128)(2,1)} fusion(bf16[32,256,128]{1,0,2:T(8,128)(2,1)} %copy.120, bf16[32,256,128]{1,0,2:T(8,128)(2,1)} %fusion.110), kind=kOutput, calls=%fused_computation.259 | convolution fusion | flops 536870912 | bytes 20971520 | tf_op jit(solution)/shard_map/pijc,pikc->pjkc/dot_general | solution.py:98
  556.3 24.3 %copy.140 = bf16[128,256,256]{0,1,2:T(8,128)(2,1)} copy(bf16[128,256,256]{2,1,0:T(8,128)(2,1)} %fusion.180) | data formatting | bytes 33554432 | tf_op jit(solution)/shard_map/pijc,pikc->pjkc/dot_general | solution.py:98
  581.7 5.6 fusion.140
  587.3 10.1 %fusion.4 = bf16[128,256,32]{1,2,0:T(8,128)(2,1)} fusion(bf16[32,256,128]{1,0,2:T(8,128)(2,1)S(1)} %copy-done.11, bf16[1,256,256,128]{2,1,3,0:T(8,128)(2,1)} %copy.119), kind=kOutput, calls=%fused_computation.8 | convolution fusion | flops 536870912 | bytes 20971520 | tf_op jit(solution)/shard_map/pijc,pjkc->pikc/dot_general | solution.py:97
  603.4 5.6 fusion.137
  610.8 7.6 fusion.131
  618.4 72.1 %reduce-scatter.5.cloned.1.call-done = bf16[1,32,256,128]{3,2,1,0:T(8,128)(2,1)} async-done(((bf16[1,256,256,128]{3,2,1,0:T(8,128)(2,1)}), bf16[1,32,256,128]{3,2,1,0:T(8,128)(2,1)}) %reduce-scatter.5.cloned.1.call-update) | async-done | bytes 2097168 | tf_op jit(solution)/shard_map/reduce_scatter | solution.py:99
  690.5 11.1 %fusion.93 = (f32[1,32,256,128]{3,2,1,0:T(8,128)S(1)}, f32[1,32,256,128]{3,2,1,0:T(8,128)S(1)}, f32[1,32,256,128]{3,2,1,0:T(8,128)S(1)}, f32[1,32,256,128]{3,2,1,0:T(8,128)S(1)}, f32[1,32,256,128]{3,2,1,0:T(8,128)S(1)}) fusion(bf16[1,32,256,128]{3,2,1,0:T(8,128)(2,1)} %reduce-scatter.5.cloned.1.call-done, f32[32,256]{1,0:T(8,128)S(1)} %convert_bitcast_fusion.9, ...), kind=kLoop, calls=%fused_computation.149 | loop fusion | flops 30408704 | bytes 52462080 | tf_op jit(solution)/shard_map/transpose(jvp())/mul | solution.py:23
  712.9 6.1 fusion.55
  720.3 6.2 fusion.45
  727.5 32.2 %all-reduce.10 = (f32[2,2,128]{2,1,0:T(2,128)}, f32[2,640]{1,0:T(2,128)}, f32[2,2,128]{2,1,0:T(2,128)}, f32[2,128]{1,0:T(2,128)}) all-reduce(f32[2,2,128]{2,1,0:T(2,128)S(1)} %pad_maximum_fusion.3, f32[2,640]{1,0:T(2,128)S(1)} %pad_maximum_fusion.2, ...), channel_id=1, replica_groups=mesh['dp'=2,'dap'=8] {'dp','dap'}, use_global_device_ids=true, to_apply=%region_22.0 | all-reduce | flops 2560 | bytes 20480 | tf_op jit(solution)/shard_map/psum | solution.py:102
  759.7 8.4 %fusion.67 = bf16[1,32,256,128]{3,2,1,0:T(8,128)(2,1)} fusion(bf16[1,32,256,128]{3,2,1,0:T(8,128)(2,1)} %copy-done.12, bf16[1,32,256,128]{3,2,1,0:T(8,128)(2,1)S(1)} %copy-done.5, bf16[32,256,128]{2,1,0:T(8,128)(2,1)} %copy-done.16, f32[32,256]{1,0:T(8,128)S(1)} %negate_multiply_fusion, f32[32,256]{1,0:T(8,128)S(1)} %multiply_multiply_fusion, ...), kind=kLoop, calls=%fused_computation.107 | loop fusion | flops 12582912 | bytes 8520192 | tf_op jit(solution)/shard_map/convert_element_type | solution.py:101
  768.1 26.1 %all-reduce.14.cloned.1.call-done = (f32[2,128,640]{2,1,0:T(8,128)}, f32[2,128,128]{2,1,0:T(8,128)}) async-done(((f32[2,128,640]{2,1,0:T(8,128)}, f32[2,128,128]{2,1,0:T(8,128)}), (f32[2,128,640]{2,1,0:T(8,128)}, f32[2,128,128]{2,1,0:T(8,128)})) %all-reduce.14.cloned.1.call-update) | async-done | bytes 786448 | tf_op jit(solution)/shard_map/psum | solution.py:102
  (166 shorter events, 121.0 us)
Async XLA Ops:
  7.2 8.3 %copy-start.4 = (bf16[1,32,256,128]{3,2,1,0:T(8,128)(2,1)S(1)}, bf16[1,32,256,128]{3,2,1,0:T(8,128)(2,1)}, u32[]{:S(2)}) copy-start(bf16[1,32,256,128]{3,2,1,0:T(8,128)(2,1)} %param.9) | copy-start | bytes 6291460
  7.2 8.3 %copy-start.27 = (bf16[2,128,640]{2,1,0:T(8,128)(2,1)S(1)}, bf16[2,128,640]{2,1,0:T(8,128)(2,1)}, u32[]{:S(2)}) copy-start(bf16[2,128,640]{2,1,0:T(8,128)(2,1)} %param.13) | copy-start | bytes 983044
  7.2 108.9 %all-gather.3.cloned.1.call-start = ((), (), s32[]{:S(2)}) async-start(), calls=%async_computation.4 | async-start | bytes 18874368 | tf_op jit(solution)/shard_map/all_gather | solution.py:79
  8.1 10.9 %copy-start.32 = (f32[128]{0:T(128)}, f32[128]{0:T(128)S(1)}, u32[]{:S(2)}) copy-start(f32[128]{0:T(128)S(1)} %get-tuple-element.69) | copy-start | bytes 1540
  8.1 10.9 %copy-start.34 = (f32[128]{0:T(128)}, f32[128]{0:T(128)S(1)}, u32[]{:S(2)}) copy-start(f32[128]{0:T(128)S(1)} %get-tuple-element.68) | copy-start | bytes 1540
  8.1 151.4 %copy-start.36 = (f32[128]{0:T(128)}, f32[128]{0:T(128)S(1)}, u32[]{:S(2)}) copy-start(f32[128]{0:T(128)S(1)} %get-tuple-element.67) | copy-start | bytes 1540
  11.8 7.2 copy-start.21
  19.0 8.2 %copy-start.2 = (f32[1,32,256,640]{3,2,1,0:T(8,128)}, f32[1,32,256,640]{3,2,1,0:T(8,128)S(1)}, u32[]{:S(2)}) copy-start(f32[1,32,256,640]{3,2,1,0:T(8,128)S(1)} %add_bitcast_fusion.1) | copy-start | bytes 62914564
  19.0 8.8 %copy-start.42 = (bf16[2,128]{1,0:T(2,128)(2,1)S(1)}, bf16[2,128]{1,0:T(2,128)(2,1)}, u32[]{:S(2)}) copy-start(bf16[2,128]{1,0:T(2,128)(2,1)} %param.17) | copy-start | bytes 1540
  19.0 8.8 %copy-start.40 = (bf16[2,2,128]{2,1,0:T(2,128)(2,1)S(1)}, bf16[2,2,128]{2,1,0:T(2,128)(2,1)}, u32[]{:S(2)}) copy-start(bf16[2,2,128]{2,1,0:T(2,128)(2,1)} %param.15) | copy-start | bytes 3076
  27.2 251.3 %all-gather.5.cloned.1.call-start = ((), (), s32[]{:S(2)}) async-start(), calls=%async_computation.5 | async-start | bytes 18874368 | tf_op jit(solution)/shard_map/all_gather | solution.py:84
  32.5 117.4 %copy-start.38 = (f32[128]{0:T(128)}, f32[128]{0:T(128)S(1)}, u32[]{:S(2)}) copy-start(f32[128]{0:T(128)S(1)} %get-tuple-element.71) | copy-start | bytes 1540
  148.4 8.6 %copy-start.30 = (f32[32,256]{1,0:T(8,128)}, f32[32,256]{1,0:T(8,128)S(1)}, u32[]{:S(2)}) copy-start(f32[32,256]{1,0:T(8,128)S(1)} %multiply_reduce_fusion.1) | copy-start | bytes 98308
  148.5 8.6 %copy-start.25 = (f32[32,256]{1,0:T(8,128)}, f32[32,256]{1,0:T(8,128)S(1)}, u32[]{:S(2)}) copy-start(f32[32,256]{1,0:T(8,128)S(1)} %fusion.162) | copy-start | bytes 98308
  149.9 7.2 copy-start.20
  163.0 7.6 copy-start.3
  173.3 53.0 %all-to-all-start = ((bf16[1,32,256,128]{3,1,0,2:T(8,128)(2,1)}), bf16[1,32,256,128]{3,1,0,2:T(8,128)(2,1)}, u32[]{:S(2)}, u32[]{:S(2)}) async-start(bf16[1,32,256,128]{3,1,0,2:T(8,128)(2,1)} %copy.126), calls=%async_computation | async-start | bytes 4194304 | tf_op jit(solution)/shard_map/all_to_all | solution.py:83
  177.7 297.6 %reduce-scatter.3.cloned.1.call-start = ((), (), s32[]{:S(2)}) async-start(), calls=%async_computation.6 | async-start | bytes 18874368 | tf_op jit(solution)/shard_map/reduce_scatter | solution.py:92
  354.1 336.4 %reduce-scatter.5.cloned.1.call-start = ((), (), s32[]{:S(2)}) async-start(), calls=%async_computation.7 | async-start | bytes 18874368 | tf_op jit(solution)/shard_map/reduce_scatter | solution.py:99
  495.7 9.2 %copy-start.9 = (bf16[1,32,256,128]{3,2,1,0:T(8,128)(2,1)S(1)}, bf16[1,32,256,128]{3,2,1,0:T(8,128)(2,1)}, u32[]{:S(2)}) copy-start(bf16[1,32,256,128]{3,2,1,0:T(8,128)(2,1)} %copy-done.8) | copy-start | bytes 6291460
  508.9 13.8 %copy-start.14 = (bf16[32,256,128]{2,1,0:T(8,128)(2,1)}, bf16[32,256,128]{2,1,0:T(8,128)(2,1)S(1)}, u32[]{:S(2)}) copy-start(bf16[32,256,128]{2,1,0:T(8,128)(2,1)S(1)} %get-tuple-element.78) | copy-start | bytes 6291460
  580.6 213.5 %all-reduce.14.cloned.1.call-start = ((), (), s32[]{:S(2)}) async-start(), calls=%async_computation.8 | async-start | bytes 1572864 | tf_op jit(solution)/shard_map/psum | solution.py:102
  603.4 6.3 copy-start.15
  603.4 7.4 copy-start.10
  603.4 7.4 copy-start.37
  610.8 79.7 %copy-start.13 = (bf16[1,32,256,128]{3,2,1,0:T(8,128)(2,1)S(1)}, bf16[1,32,256,128]{3,2,1,0:T(8,128)(2,1)}, u32[]{:S(2)}) copy-start(bf16[1,32,256,128]{3,2,1,0:T(8,128)(2,1)} %copy-done.12) | copy-start | bytes 6291460
  610.8 79.7 %copy-start.39 = (f32[128]{0:T(128)S(1)}, f32[128]{0:T(128)}, u32[]{:S(2)}) copy-start(f32[128]{0:T(128)} %copy-done.38) | copy-start | bytes 1540
  701.6 7.4 copy-start.5
  701.6 7.3 copy-start.22
  701.6 7.3 copy-start.24
  701.6 7.3 copy-start.33
  701.7 7.3 copy-start.35
  (17 other events, 67.0 us)
Sparse Core Ops, SparseCore 0:
  27.4 88.6 all-gather.2
  170.7 107.7 all-gather.4
  354.2 121.0 reduce-scatter.2
  580.8 109.6 reduce-scatter.4
  727.6 66.5 all-reduce.13
where the time goes:
time: 813 us; the launch traced here: 804 us
  waiting for transfers between devices  325 us (40%)
  local copies, waits for them, and re-layouts  145 us (18%)
  matrix products  143 us (18%)
  other arithmetic  97.8 us (12%)
  blocking collectives  74.3 us (9%)
  between operations  14.9 us (2%)
    all_gather x1, waiting for transfers between devices, local_step(): b_full0 = lax.all_gather(b_rows0, 'dap', axis=1, tiled=True)  83.6 us
    reduce_scatter x1, waiting for transfers between devices, local_step(): lax.psum_scatter(d_bpart0, 'dap', scatter_dimension=1, tiled=True)  72.1 us
    reduce_scatter x1, waiting for transfers between devices, local_step(): lax.psum_scatter(d_bpart1, 'dap', scatter_dimension=1, tiled=True)  59.9 us
    all_gather x1, waiting for transfers between devices, local_step(): b_full1 = lax.all_gather(b_rows1, 'dap', axis=1, tiled=True)  43.1 us
    all_to_all x1, blocking collectives, local_step(): d_arows1 = lax.all_to_all(d_acols1, 'dap', 1, 2, tiled=True)  42.1 us
    all_to_all x1, waiting for transfers between devices, local_step(): a_cols1 = lax.all_to_all(a_rows1, 'dap', 2, 1, tiled=True)  39.8 us
    psum x1, blocking collectives, local_step(): lax.psum(collect_grads(grads_pre0, grads_post0, grads_pre1, grads_post1),...  32.2 us
    dot_general x2, matrix products, post_forward(): jnp.einsum('pijh,hc->pijc', x_hat, w_out, preferred_element_type=jnp.floa...  27.5 us
  transfers between devices with their start and end apart: 6, of which 6 were waited for; matrix products, arithmetic and copies ran while one was open for 11% of the time, Pallas kernels for 0%

commit v1 on v0

v1 whole, which is shorter than its diff:
```python
import functools

import jax
import jax.numpy as jnp
from jax import lax
from jax.experimental import pallas as pl
from jax.experimental.pallas import tpu as pltpu
from jax.sharding import PartitionSpec as P

LN_EPS = 1e-5
N = 256
C = 128
GROUP = 8
ROWS = N // GROUP
CH = C // GROUP
STEP = 8
SEND = 16
STEPS = ROWS // STEP
F32 = jnp.float32
BF16 = jnp.bfloat16
VMEM_LIMIT = 62 * 1024 * 1024


def dot(lhs, rhs, lhs_dim, rhs_dim):
    return lax.dot_general(lhs, rhs, (((lhs_dim,), (rhs_dim,)), ((), ())), preferred_element_type=F32)


def norm(values):
    mean = jnp.mean(values, axis=0, keepdims=True)
    cen = values - mean
    inv = lax.rsqrt(jnp.mean(cen * cen, axis=0, keepdims=True) + LN_EPS)
    return cen * inv, inv


def norm_back(d_hat, unit, inv, gain):
    d_unit = d_hat * gain
    mean_d = jnp.mean(d_unit, axis=0, keepdims=True)
    mean_du = jnp.mean(d_unit * unit, axis=0, keepdims=True)
    return inv * (d_unit - mean_d - unit * mean_du)


def fold(values):
    return values[:, :C] + values[:, C:]


def row_sums(acc):
    return jnp.sum(acc.T, axis=0, keepdims=True)


def sigmoid(values):
    return 0.5 * jnp.tanh(0.5 * values) + 0.5


def project(z_t, ln, w_t, bias):
    unit, inv = norm(z_t)
    z_hat = (unit * ln[0] + ln[1]).astype(BF16)
    return unit, inv, z_hat, dot(w_t, z_hat, 1, 0) + bias


def place():
    me = lax.axis_index("dap")
    return me, me // 4, (me // 2) % 2, me % 2


def enter():
    me = lax.axis_index("dap")
    sem = pltpu.get_barrier_semaphore()
    for k in range(1, GROUP):
        pl.semaphore_signal(sem, inc=1, device_id={"dap": (me + k) % GROUP}, device_id_type=pl.DeviceIdType.MESH)
    pl.semaphore_wait(sem, GROUP - 1)


def peers():
    me, cy, cx, core = place()
    out = []
    for dy, dx in ((1, 1), (1, 0), (0, 1), (0, 0)):
        for dc in (1, 0):
            out.append((((cy + dy) % 2) * 2 + (cx + dx) % 2) * 2 + (core + dc) % 2)
    return me, out


def spread(ref, value, row):
    for h in range(2):
        ref[pl.ds(h * C * STEP + row, C, stride=STEP), :] = value[:, h * C:(h + 1) * C]


def pack_rows(lo_ref, hi_ref, send_ref, slot):
    for h in range(2):
        for q in range(4):
            at = pl.ds((h * C + q * 32) * STEP, 32 * STEP)
            lo = lo_ref[at, :].reshape(32, STEP, C)
            hi = hi_ref[at, :].reshape(32, STEP, C)
            send_ref[slot, q * 32:(q + 1) * 32, :, h * C:(h + 1) * C] = jnp.concatenate([lo, hi], axis=1).astype(BF16)


def move(src_ref, dst_ref, send_sem, recv_sem, dest, own):
    if own:
        return pltpu.make_async_copy(src_ref, dst_ref, recv_sem)
    return pltpu.make_async_remote_copy(src_ref, dst_ref, send_sem, recv_sem, device_id={"dap": dest}, device_id_type=pl.DeviceIdType.MESH)


def wait_sends(copies):
    for copy in copies:
        if copy.is_remote:
            copy.wait_send()


def row_copies(send_ref, out_ref, send_sem, recv_sem, slot):
    me, dests = peers()
    start = pl.multiple_of(me * ROWS + slot * SEND, SEND)
    return [
        move(send_ref.at[slot, pl.ds(pl.multiple_of(dest * CH, CH), CH)], out_ref.at[:, pl.ds(start, SEND), :],
             send_sem.at[slot, k], recv_sem, dest, k == GROUP - 1)
        for k, dest in enumerate(dests)
    ]


def send_rows(step, jobs):
    for slot in range(ROWS // SEND):
        @pl.when(step == 2 * slot + 1)
        def _():
            for stage, send_ref, out_ref, send_sem, recv_sem in jobs:
                pack_rows(stage.at[0], stage.at[1], send_ref, slot)
                for copy in row_copies(send_ref, out_ref, send_sem, recv_sem, slot):
                    copy.start()

    @pl.when(step == STEPS - 1)
    def _():
        for stage, send_ref, out_ref, send_sem, recv_sem in jobs:
            for slot in range(ROWS // SEND):
                wait_sends(row_copies(send_ref, out_ref, send_sem, recv_sem, slot))
            pltpu.make_async_copy(out_ref, out_ref, recv_sem).wait()


def pre_row(r, z_t, mask_ref, ln_ref, w_t_ref, bias_ref, g_ref, a_stage, b_stage):
    _, _, _, p = project(z_t, ln_ref, w_t_ref[...], bias_ref[...])
    m = mask_ref[0, pl.ds(r, 1), :].astype(F32)
    spread(a_stage, sigmoid(p[:C]) * p[C:2 * C] * m, r)
    spread(b_stage, sigmoid(p[2 * C:3 * C]) * p[3 * C:4 * C] * m, r)
    g_ref[r] = sigmoid(p[4 * C:])


def pre_kernel(z_ref, mask_ref, ln_ref, w_t_ref, bias_ref, eye_ref, a_ref, b_ref, g_ref, a_st, b_st, a_send, b_send, a_ss, b_ss, rs):
    step = pl.program_id(0)
    pl.when(step == 0)(enter)
    half = step % 2

    def body(r, carry):
        z_t = dot(eye_ref[...], z_ref[r], 1, 1)
        pre_row(r, z_t, mask_ref, ln_ref, w_t_ref, bias_ref, g_ref, a_st.at[half], b_st.at[half])
        return carry

    lax.fori_loop(0, STEP, body, 0)
    send_rows(step, [(a_st, a_send, a_ref, a_ss, rs.at[0]), (b_st, b_send, b_ref, b_ss, rs.at[1])])


def mid_kernel(x_ref, z_ref, g0_ref, mask_ref, mln_ref, wo_t_ref, bo_ref, ln_ref, w_t_ref, bias_ref, eye_ref,
               a_ref, b_ref, g_ref, zm_ref, a_st, b_st, a_send, b_send, a_ss, b_ss, rs):
    step = pl.program_id(0)
    pl.when(step == 0)(enter)
    half = step % 2

    def body(r, carry):
        unit, _ = norm(x_ref[r].astype(F32))
        x_hat = (unit * mln_ref[0] + mln_ref[1]).astype(BF16)
        update = dot(wo_t_ref[...], x_hat, 1, 0) + bo_ref[...]
        z_new = (dot(eye_ref[...], z_ref[r], 1, 1) + g0_ref[r] * update).astype(BF16)
        zm_ref[r] = z_new
        pre_row(r, z_new.astype(F32), mask_ref, ln_ref, w_t_ref, bias_ref, g_ref, a_st.at[half], b_st.at[half])
        return carry

    lax.fori_loop(0, STEP, body, 0)
    send_rows(step, [(a_st, a_send, a_ref, a_ss, rs.at[0]), (b_st, b_send, b_ref, b_ss, rs.at[1])])


def post_back_row(x_t, g, dz, mln_ref, wo_t_ref, wo_ref, bo_ref, acc_ref):
    unit, inv = norm(x_t)
    x_hat = (unit * mln_ref[0] + mln_ref[1]).astype(BF16)
    update = dot(wo_t_ref[...], x_hat, 1, 0) + bo_ref[...]
    d_up = dz * g
    d_up_bf = d_up.astype(BF16)
    acc_ref[0] += dot(x_hat, d_up_bf, 1, 1)
    acc_ref[3] += fold(d_up)
    d_hat = dot(wo_ref[...], d_up_bf, 1, 0).astype(BF16).astype(F32)
    acc_ref[1] += fold(d_hat * unit)
    acc_ref[2] += fold(d_hat)
    dx = norm_back(d_hat, unit, inv, mln_ref[0])
    return update, dx, dz * update * g * (1.0 - g)


def put_post(grad_ref, acc_ref):
    grad_ref[0:C, :] = acc_ref[0]
    grad_ref[C:C + 8, :] = jnp.concatenate([row_sums(acc_ref[1]), row_sums(acc_ref[2]), row_sums(acc_ref[3]), jnp.zeros((5, C), F32)], axis=0)


def turn_kernel(x_ref, zm_ref, g_ref, dz_ref, mln_ref, wo_t_ref, wo_ref, bo_ref, eye_ref,
                dx_ref, z_out_ref, dpg_ref, grad_ref, d_st, d_send, acc_ref, d_ss, rs):
    step = pl.program_id(0)

    @pl.when(step == 0)
    def _():
        enter()
        acc_ref[...] = jnp.zeros_like(acc_ref)

    half = step % 2

    def body(r, carry):
        dz = dot(eye_ref[...], dz_ref[r], 1, 1)
        g = g_ref[r]
        update, dx, d_pg = post_back_row(x_ref[r].astype(F32), g, dz, mln_ref, wo_t_ref, wo_ref, bo_ref, acc_ref)
        dpg_ref[r] = d_pg
        z_out_ref[r] = (zm_ref[r].astype(F32) + g * update).T.astype(BF16)
        spread(d_st.at[half], dx, r)
        return carry

    lax.fori_loop(0, STEP, body, 0)

    @pl.when(step == STEPS - 1)
    def _():
        put_post(grad_ref, acc_ref)

    send_rows(step, [(d_st, d_send, dx_ref, d_ss, rs.at[0])])


def pre_back_row(r, z_t, da, db, d_pg, mask_ref, ln_ref, w_t_ref, w_ref, bias_ref, w_acc, b_acc, l_acc):
    unit, inv, z_hat, p = project(z_t, ln_ref, w_t_ref[...], bias_ref[...])
    m = mask_ref[0, pl.ds(r, 1), :].astype(F32)
    parts = []
    for side, d_side in ((0, da), (1, db)):
        s = sigmoid(p[2 * side * C:(2 * side + 1) * C])
        v = p[(2 * side + 1) * C:(2 * side + 2) * C]
        d_v = d_side * m * s
        parts += [d_v * v * (1.0 - s), d_v]
    parts.append(d_pg)
    for k, part in enumerate(parts):
        b_acc[k * C:(k + 1) * C, :] += fold(part)
    d_p = jnp.concatenate([part.astype(BF16) for part in parts], axis=0)
    w_acc[...] += dot(d_p, z_hat, 1, 1)
    d_hat = dot(w_ref[...], d_p, 1, 0).astype(BF16).astype(F32)
    l_acc[0] += fold(d_hat * unit)
    l_acc[1] += fold(d_hat)
    return norm_back(d_hat, unit, inv, ln_ref[0])


def put_pre(grad_ref, w_acc, b_acc, l_acc):
    grad_ref[0:5 * C, :] = w_acc[...]
    rows = [row_sums(b_acc[k * C:(k + 1) * C, :]) for k in range(5)]
    rows += [row_sums(l_acc[0]), row_sums(l_acc[1]), jnp.zeros((1, C), F32)]
    grad_ref[5 * C:5 * C + 8, :] = jnp.concatenate(rows, axis=0)


def back_kernel(da_ref, db_ref, dpg1_ref, zm_ref, mask_ref, dz_ref, x_ref, g_ref, ln_ref, w_t_ref, w_ref, bias_ref,
                mln_ref, wo_t_ref, wo_ref, bo_ref, eye_ref,
                dx_ref, dzm_ref, dpg_ref, grad1_ref, grad0_ref, d_st, d_send, w_acc, b_acc, l_acc, acc_ref, d_ss, rs):
    step = pl.program_id(0)

    @pl.when(step == 0)
    def _():
        enter()
        for ref in (w_acc, b_acc, l_acc, acc_ref):
            ref[...] = jnp.zeros_like(ref)

    half = step % 2

    def body(r, carry):
        dzn = pre_back_row(r, zm_ref[r].astype(F32), da_ref[r].astype(F32), db_ref[r].astype(F32), dpg1_ref[r], mask_ref,
                           ln_ref, w_t_ref, w_ref, bias_ref, w_acc, b_acc, l_acc)
        dzm = (dot(eye_ref[...], dz_ref[r], 1, 1) + dzn).astype(BF16)
        dzm_ref[r] = dzm
        _, dx, d_pg = post_back_row(x_ref[r].astype(F32), g_ref[r], dzm.astype(F32), mln_ref, wo_t_ref, wo_ref, bo_ref, acc_ref)
        dpg_ref[r] = d_pg
        spread(d_st.at[half], dx, r)
        return carry

    lax.fori_loop(0, STEP, body, 0)

    @pl.when(step == STEPS - 1)
    def _():
        put_pre(grad1_ref, w_acc, b_acc, l_acc)
        put_post(grad0_ref, acc_ref)

    send_rows(step, [(d_st, d_send, dx_ref, d_ss, rs.at[0])])


def last_kernel(da_ref, db_ref, dpg_ref, z_ref, mask_ref, dzm_ref, ln_ref, w_t_ref, w_ref, bias_ref, eye_ref,
                dz_ref, grad_ref, w_acc, b_acc, l_acc):
    step = pl.program_id(0)

    @pl.when(step == 0)
    def _():
        for ref in (w_acc, b_acc, l_acc):
            ref[...] = jnp.zeros_like(ref)

    def body(r, carry):
        z_t = dot(eye_ref[...], z_ref[r], 1, 1)
        dzn = pre_back_row(r, z_t, da_ref[r].astype(F32), db_ref[r].astype(F32), dpg_ref[r], mask_ref,
                           ln_ref, w_t_ref, w_ref, bias_ref, w_acc, b_acc, l_acc)
        dz_ref[r] = (dzm_ref[r].astype(F32) + dzn).T.astype(BF16)
        return carry

    lax.fori_loop(0, STEP, body, 0)

    @pl.when(step == STEPS - 1)
    def _():
        put_pre(grad_ref, w_acc, b_acc, l_acc)


HALF = N // 2


def spread_channel(stage, value, c):
    for h in range(2):
        stage[pl.ds((h * 2 + c // 8) * HALF * 8 + c % 8, HALF, stride=8), :] = value[:, h * C:(h + 1) * C]


def pack_channels(stage, send_ref, slot):
    for h in range(2):
        for q in range(4):
            lo = stage[pl.ds((h * 2) * HALF * 8 + q * 256, 256), :].reshape(32, 8, C)
            hi = stage[pl.ds((h * 2 + 1) * HALF * 8 + q * 256, 256), :].reshape(32, 8, C)
            send_ref[slot, q * 32:(q + 1) * 32, :, h * C:(h + 1) * C] = jnp.concatenate([lo, hi], axis=1).astype(BF16)


def channel_copies(send_ref, out_ref, send_sem, recv_sem, slot, top):
    me, cy, cx, core = place()
    out = []
    k = 0
    for dx in (1, 0):
        for dc in (1, 0):
            within = ((cx + dx) % 2) * 2 + (core + dc) % 2
            out.append(move(send_ref.at[slot, pl.ds(pl.multiple_of(within * ROWS, ROWS), ROWS)],
                            out_ref.at[:, pl.ds(pl.multiple_of(me * CH, CH), CH), :],
                            send_sem.at[slot, k], recv_sem, top * 4 + within, slot == 1 and k == 3))
            k += 1
    return out


def channel_kernel(products, n_in, n_out, *refs):
    ins, outs = refs[:n_in], refs[n_in:n_in + n_out]
    stages = refs[n_in + n_out:n_in + 2 * n_out]
    sends = refs[n_in + 2 * n_out:n_in + 3 * n_out]
    sems = refs[n_in + 3 * n_out:n_in + 4 * n_out]
    rs = refs[-1]
    step = pl.program_id(0)
    pl.when(step == 0)(enter)
    _, cy, _, _ = place()
    top = (cy + 1 + step) % 2
    rows = pl.ds(pl.multiple_of(top * HALF, HALF), HALF)
    for j in range(n_out):
        for c in range(CH):
            spread_channel(stages[j], products[j](ins, c, rows), c)
        for slot in range(2):
            @pl.when(step == slot)
            def _():
                pack_channels(stages[j], sends[j], slot)
                for copy in channel_copies(sends[j], outs[j], sems[j], rs.at[j], slot, top):
                    copy.start()

    @pl.when(step == 1)
    def _():
        for j in range(n_out):
            for slot in range(2):
                wait_sends(channel_copies(sends[j], outs[j], sems[j], rs.at[j], slot, (cy + 1 + slot) % 2))
            pltpu.make_async_copy(outs[j], outs[j], rs.at[j]).wait()


OUT_FWD = (lambda r, c, rows: dot(r[0][c, rows, :], r[1][c], 1, 1),)
IN_FWD = (lambda r, c, rows: dot(r[0][c, :, rows], r[1][c], 0, 0),)
IN_BWD = (lambda r, c, rows: dot(r[1][c, rows, :], r[2][c], 1, 1), lambda r, c, rows: dot(r[0][c, rows, :], r[2][c], 1, 0))
OUT_BWD = (lambda r, c, rows: dot(r[2][c, rows, :], r[1][c], 1, 0), lambda r, c, rows: dot(r[2][c, :, rows], r[0][c], 0, 0))

ANY = pl.BlockSpec(memory_space=pl.ANY)
TRI = jax.ShapeDtypeStruct((CH, N, N), BF16)
ROW = jax.ShapeDtypeStruct((ROWS, C, N), BF16)
ROW32 = jax.ShapeDtypeStruct((ROWS, C, N), F32)
NATIVE = jax.ShapeDtypeStruct((ROWS, N, C), BF16)
POST = jax.ShapeDtypeStruct((C + 8, C), F32)
PRE = jax.ShapeDtypeStruct((5 * C + 8, C), F32)


def by_row(array):
    tail = array.shape[1:]
    return pl.BlockSpec((array.shape[0] // STEPS,) + tail, lambda t: (t,) + (0,) * len(tail))


def whole(array):
    zeros = (0,) * len(array.shape)
    return pl.BlockSpec(array.shape, lambda t: zeros)


def params(collective_id):
    if collective_id is None:
        return pltpu.CompilerParams(dimension_semantics=("arbitrary",), vmem_limit_bytes=VMEM_LIMIT)
    return pltpu.CompilerParams(dimension_semantics=("arbitrary",), vmem_limit_bytes=VMEM_LIMIT, collective_id=collective_id, has_side_effects=True)


def row_call(kernel, name, collective_id, ins, consts, outs, specs, n_send, scratch):
    sent = [pltpu.VMEM((2, 2 * C * STEP, C), F32)] * n_send + [pltpu.VMEM((ROWS // SEND, C, SEND, N), BF16)] * n_send
    sems = [pltpu.SemaphoreType.DMA((ROWS // SEND, GROUP))] * n_send + ([pltpu.SemaphoreType.DMA((n_send,))] if n_send else [])
    return pl.pallas_call(
        kernel,
        grid=(STEPS,),
        in_specs=[by_row(x) for x in ins] + [whole(x) for x in consts],
        out_specs=specs,
        out_shape=outs,
        scratch_shapes=sent + scratch + sems,
        compiler_params=params(collective_id),
        name=name,
    )(*ins, *consts)


def channel_call(products, name, collective_id, ins, n_out):
    return pl.pallas_call(
        functools.partial(channel_kernel, products, len(ins), n_out),
        grid=(2,),
        in_specs=[whole(x) for x in ins],
        out_specs=[ANY] * n_out,
        out_shape=[ROW] * n_out,
        scratch_shapes=[pltpu.VMEM((4 * HALF * 8, C), F32)] * n_out + [pltpu.VMEM((2, HALF, CH, N), BF16)] * n_out
        + [pltpu.SemaphoreType.DMA((2, 4))] * n_out + [pltpu.SemaphoreType.DMA((n_out,))],
        compiler_params=params(collective_id),
        name=name,
    )(*ins)


def local_step(z_pair, pair_mask, dz_out, ln_in, w_proj, b_proj, ln_mid, w_out, b_out):
    z, dz = z_pair[0], dz_out[0]
    mask = pair_mask.reshape(STEPS, STEP, N)
    eye = jnp.eye(C, dtype=BF16)
    ln = jnp.broadcast_to(ln_in.astype(F32)[..., None], (2, 2, C, N))
    mln = jnp.broadcast_to(ln_mid.astype(F32)[..., None], (2, 2, C, N))
    bias = jnp.broadcast_to(b_proj.astype(F32)[..., None], (2, 5 * C, N))
    bo = jnp.broadcast_to(b_out.astype(F32)[..., None], (2, C, N))
    w_t = jnp.swapaxes(w_proj, 1, 2)
    wo_t = jnp.swapaxes(w_out, 1, 2)
    pre = [(ln[k], w_t[k], bias[k]) for k in range(2)]
    post = [(mln[k], wo_t[k], bo[k]) for k in range(2)]

    a0, b0, g0 = row_call(pre_kernel, "pre0", 0, [z, mask], [*pre[0], eye], [TRI, TRI, ROW32], [ANY, ANY, by_row(ROW32)], 2, [])
    x0, = channel_call(OUT_FWD, "tri0", 1, [a0, b0], 1)
    a1, b1, g1, zm = row_call(mid_kernel, "mid", 2, [x0, z, g0, mask], [*post[0], *pre[1], eye], [TRI, TRI, ROW32, ROW],
                              [ANY, ANY, by_row(ROW32), by_row(ROW)], 2, [])
    x1, = channel_call(IN_FWD, "tri1", 3, [a1, b1], 1)
    post_acc = [pltpu.VMEM((4, C, C), F32)]
    pre_acc = [pltpu.VMEM((5 * C, C), F32), pltpu.VMEM((5 * C, C), F32), pltpu.VMEM((2, C, C), F32)]
    dx1, z_new, dpg1, post_g1 = row_call(turn_kernel, "turn", 4, [x1, zm, g1, dz], [mln[1], wo_t[1], w_out[1], bo[1], eye],
                                         [TRI, NATIVE, ROW32, POST], [ANY, by_row(NATIVE), by_row(ROW32), whole(POST)], 1, post_acc)
    da1, db1 = channel_call(IN_BWD, "trib1", 5, [a1, b1, dx1], 2)
    dx0, dzm, dpg0, pre_g1, post_g0 = row_call(
        back_kernel, "back", 6, [da1, db1, dpg1, zm, mask, dz, x0, g0],
        [ln[1], w_t[1], w_proj[1], bias[1], mln[0], wo_t[0], w_out[0], bo[0], eye],
        [TRI, ROW, ROW32, PRE, POST], [ANY, by_row(ROW), by_row(ROW32), whole(PRE), whole(POST)], 1, pre_acc + post_acc)
    da0, db0 = channel_call(OUT_BWD, "trib0", 7, [a0, b0, dx0], 2)
    dz_new, pre_g0 = row_call(last_kernel, "last", None, [da0, db0, dpg0, z, mask, dzm], [ln[0], w_t[0], w_proj[0], bias[0], eye],
                              [NATIVE, PRE], [by_row(NATIVE), whole(PRE)], 0, pre_acc)

    total = lax.psum(jnp.concatenate([pre_g0, pre_g1, post_g0, post_g1]), ("dp", "dap"))
    pre_g = [total[:5 * C + 8], total[5 * C + 8:2 * (5 * C + 8)]]
    post_g = [total[2 * (5 * C + 8):2 * (5 * C + 8) + C + 8], total[2 * (5 * C + 8) + C + 8:]]
    d_w_proj = jnp.stack([g[:5 * C].T for g in pre_g])
    d_b_proj = jnp.stack([g[5 * C:5 * C + 5].reshape(5 * C) for g in pre_g])
    d_ln_in = jnp.stack([g[5 * C + 5:5 * C + 7] for g in pre_g])
    d_w_out = jnp.stack([g[:C] for g in post_g])
    d_ln_mid = jnp.stack([g[C:C + 2] for g in post_g])
    d_b_out = jnp.stack([g[C + 2] for g in post_g])
    return z_new[None], dz_new[None], d_ln_in, d_w_proj, d_b_proj, d_ln_mid, d_w_out, d_b_out


def solution(mesh):
    row_spec = P("dp", "dap")
    return jax.shard_map(local_step, mesh=mesh, in_specs=(row_spec,) * 3 + (P(),) * 6,
                         out_specs=(row_spec,) * 2 + (P(),) * 6, check_vma=False)
```

time: 813 us -> 510 us (0.63)
  Pallas kernels: 0 us -> 402 us
  waiting for transfers between devices: 325 us -> 67.1 us
  matrix products: 143 us -> 0 us
  local copies, waits for them, and re-layouts: 145 us -> 18.6 us
  other arithmetic: 97.8 us -> 6.95 us
  blocking collectives: 74.3 us -> 0 us
    pallas_call x0 -> x9, Pallas kernels: none -> 402 us  [the longest x5 238 us: row_call(): pl.pallas_call(kernel, grid=(STEPS,), in_specs=[by_row(x) for x in ins] +...]
    dot_general x18 -> x0, matrix products: 143 us -> none  [the longest x2 27.5 us: post_forward(): jnp.einsum('pijh,hc->pijc', x_hat, w_out, preferred_element_type=jnp.floa...]
    reduce_scatter x2 -> x0, waiting for transfers between devices: 132 us -> none  [the longest x1 72.1 us: local_step(): lax.psum_scatter(d_bpart0, 'dap', scatter_dimension=1, tiled=True)]
    all_gather x2 -> x0, waiting for transfers between devices: 127 us -> none  [the longest x1 83.6 us: local_step(): b_full0 = lax.all_gather(b_rows0, 'dap', axis=1, tiled=True)]
    dot_general x5 -> x0, local copies, waits for them, and re-layouts: 61.5 us -> none  [the longest x1 24.4 us: local_step(): jnp.einsum('pkic,pijc->pkjc', a_cols1, d_trib1, preferred_element_type=jn...]
    reduce_sum x17 -> x0, other arithmetic: 56 us -> none  [the longest x10 27.3 us: layer_norm(): return centered * lax.rsqrt(variance + LN_EPS) * ln_gain + ln_bias]
    all_gather x2 -> x0, local copies, waits for them, and re-layouts: 43.7 us -> none  [the longest x1 21.9 us: local_step(): b_full0 = lax.all_gather(b_rows0, 'dap', axis=1, tiled=True)]
    all_to_all x1 -> x0, blocking collectives: 42.1 us -> none  [local_step(): d_arows1 = lax.all_to_all(d_acols1, 'dap', 1, 2, tiled=True)]
  transfers between devices with their start and end apart: 6 -> 1, of which waited for: 6 -> 1; matrix products, arithmetic and copies ran while one was open for 11% -> 0% of each run, Pallas kernels for 0% -> 0%
where the time goes in v1:
time: 510 us; the launch traced here: 509 us
  Pallas kernels  402 us (79%)
  waiting for transfers between devices  67.1 us (13%)
  local copies, waits for them, and re-layouts  18.6 us (4%)
  between operations  14.2 us (3%)
  other arithmetic  6.95 us (1%)
    pallas_call x5, Pallas kernels, row_call(): pl.pallas_call(kernel, grid=(STEPS,), in_specs=[by_row(x) for x in ins] +...  238 us
    pallas_call x4, Pallas kernels, channel_call(): pl.pallas_call(functools.partial(channel_kernel, products, len(ins), n_ou...  164 us
    psum x1, waiting for transfers between devices, local_step(): lax.psum(jnp.concatenate([pre_g0, pre_g1, post_g0, post_g1]), ('dp', 'dap'))  67.1 us
  transfers between devices with their start and end apart: 1, of which 1 were waited for; matrix products, arithmetic and copies ran while one was open for 0% of the time, Pallas kernels for 0%

profile of v1, /device:TPU:0, one launch (start us, length us, event | category | flops | bytes accessed | tf_op | source)
XLA Modules:
  0.0 509.2 jit_solution(17587048903412732994)
XLA Ops:
  7.9 1.2 copy.17
  9.0 1.8 slice_bitcast_fusion.4
  10.8 0.7 convert_element_type.24
  11.5 0.8 slice_bitcast_fusion.2
  12.3 0.7 convert_element_type.23
  13.0 0.9 copy.18
  14.6 1.0 broadcast_in_dim.57.bias_ref
  15.6 0.8 broadcast_in_dim.55.ln_ref
  16.4 62.0 %pre0.1 = (bf16[16,256,256]{2,1,0:T(8,128)(2,1)}, bf16[16,256,256]{2,1,0:T(8,128)(2,1)}, f32[32,128,256]{2,1,0:T(8,128)}) custom-call(bf16[32,256,128]{2,1,0:T(8,128)(2,1)} %bitcast.67, s32[4,8,256]{2,1,0:T(8,128)} %bitcast.74, f32[2,128,256]{2,1,0:T(8,128)} %broadcast_in_dim.55.ln_ref, bf16[640,128]{1,0:T(8,128)(2,1)} %get-tuple-element.77.w_t_ref, ...), custom_call_target="tpu_custom_call" | custom-call | tf_op jit(solution)/shard_map/pre0/pallas_call | solution.py:400
  78.4 29.4 %tri0.1.x_ref = bf16[32,128,256]{2,1,0:T(8,128)(2,1)} custom-call(bf16[16,256,256]{2,1,0:T(8,128)(2,1)} %get-tuple-element.30.refs_0_, bf16[16,256,256]{2,1,0:T(8,128)(2,1)} %get-tuple-element.31.refs_1_), custom_call_target="tpu_custom_call" | custom-call | tf_op jit(solution)/shard_map/tri0/pallas_call | solution.py:413
  107.9 1.0 broadcast_in_dim.65.bias_ref
  108.8 0.8 broadcast_in_dim.59.mln_ref
  109.6 0.8 broadcast_in_dim.63.ln_ref
  110.4 0.7 broadcast_in_dim.61.bo_ref
  111.2 61.3 %mid.1 = (bf16[16,256,256]{2,1,0:T(8,128)(2,1)}, bf16[16,256,256]{2,1,0:T(8,128)(2,1)}, f32[32,128,256]{2,1,0:T(8,128)}, bf16[32,128,256]{2,1,0:T(8,128)(2,1)}) custom-call(bf16[32,128,256]{2,1,0:T(8,128)(2,1)} %tri0.1.x_ref, bf16[32,256,128]{2,1,0:T(8,128)(2,1)} %bitcast.68, f32[32,128,256]{2,1,0:T(8,128)} %get-tuple-element.32.g0_ref.g_ref, ...), custom_call_target="tpu_custom_call" | custom-call | tf_op jit(solution)/shard_map/mid/pallas_call | solution.py:400
  172.5 29.3 %tri1.1.x_ref = bf16[32,128,256]{2,1,0:T(8,128)(2,1)} custom-call(bf16[16,256,256]{2,1,0:T(8,128)(2,1)} %get-tuple-element.33.refs_0_, bf16[16,256,256]{2,1,0:T(8,128)(2,1)} %get-tuple-element.34.refs_1_), custom_call_target="tpu_custom_call" | custom-call | tf_op jit(solution)/shard_map/tri1/pallas_call | solution.py:413
  201.7 0.8 broadcast_in_dim.67.mln_ref
  202.5 0.7 broadcast_in_dim.69.bo_ref
  203.3 35.9 %turn.1 = (bf16[16,256,256]{2,1,0:T(8,128)(2,1)}, bf16[32,256,128]{2,1,0:T(8,128)(2,1)}, f32[32,128,256]{2,1,0:T(8,128)}, f32[136,128]{1,0:T(8,128)}) custom-call(bf16[32,128,256]{2,1,0:T(8,128)(2,1)} %tri1.1.x_ref, bf16[32,128,256]{2,1,0:T(8,128)(2,1)} %get-tuple-element.35.zm_ref, f32[32,128,256]{2,1,0:T(8,128)} %get-tuple-element.36.g_ref, ...), custom_call_target="tpu_custom_call" | custom-call | tf_op jit(solution)/shard_map/turn/pallas_call | solution.py:400
  239.1 52.7 %trib1.1 = (bf16[32,128,256]{2,1,0:T(8,128)(2,1)}, bf16[32,128,256]{2,1,0:T(8,128)(2,1)}) custom-call(bf16[16,256,256]{2,1,0:T(8,128)(2,1)} %get-tuple-element.33.refs_0_, bf16[16,256,256]{2,1,0:T(8,128)(2,1)} %get-tuple-element.34.refs_1_, bf16[16,256,256]{2,1,0:T(8,128)(2,1)} %get-tuple-element.38.refs_2_), custom_call_target="tpu_custom_call" | custom-call | tf_op jit(solution)/shard_map/trib1/pallas_call | solution.py:413
  291.8 47.7 %back.1 = (bf16[16,256,256]{2,1,0:T(8,128)(2,1)}, bf16[32,128,256]{2,1,0:T(8,128)(2,1)}, f32[32,128,256]{2,1,0:T(8,128)}, f32[648,128]{1,0:T(8,128)}, f32[136,128]{1,0:T(8,128)}) custom-call(bf16[32,128,256]{2,1,0:T(8,128)(2,1)} %get-tuple-element.39.da_ref, bf16[32,128,256]{2,1,0:T(8,128)(2,1)} %get-tuple-element.40.db_ref, ...), custom_call_target="tpu_custom_call" | custom-call | tf_op jit(solution)/shard_map/back/pallas_call | solution.py:400
  339.6 52.4 %trib0.1 = (bf16[32,128,256]{2,1,0:T(8,128)(2,1)}, bf16[32,128,256]{2,1,0:T(8,128)(2,1)}) custom-call(bf16[16,256,256]{2,1,0:T(8,128)(2,1)} %get-tuple-element.30.refs_0_, bf16[16,256,256]{2,1,0:T(8,128)(2,1)} %get-tuple-element.31.refs_1_, bf16[16,256,256]{2,1,0:T(8,128)(2,1)} %get-tuple-element.42.refs_2_), custom_call_target="tpu_custom_call" | custom-call | tf_op jit(solution)/shard_map/trib0/pallas_call | solution.py:413
  392.1 31.5 %last.1 = (bf16[32,256,128]{2,1,0:T(8,128)(2,1)}, f32[648,128]{1,0:T(8,128)}) custom-call(bf16[32,128,256]{2,1,0:T(8,128)(2,1)} %get-tuple-element.43.da_ref, bf16[32,128,256]{2,1,0:T(8,128)(2,1)} %get-tuple-element.44.db_ref, f32[32,128,256]{2,1,0:T(8,128)} %get-tuple-element.45.dpg_ref, bf16[32,256,128]{2,1,0:T(8,128)(2,1)} %bitcast.69, ...), custom_call_target="tpu_custom_call" | custom-call | tf_op jit(solution)/shard_map/last/pallas_call | solution.py:400
  423.6 1.9 pad_maximum_fusion
  425.6 67.1 %all-reduce.2.cloned.1.call-done = f32[1568,128]{1,0:T(8,128)} async-done(((f32[1568,128]{1,0:T(8,128)}), f32[1568,128]{1,0:T(8,128)}) %all-reduce.2.cloned.1.call-update) | async-done | bytes 802832 | tf_op jit(solution)/shard_map/psum | solution.py:457
  492.6 0.7 slice_bitcast_fusion.13
  493.3 1.3 slice_bitcast_fusion.1
  494.6 1.1 copy.19
  495.7 0.7 fusion.1
  497.0 0.9 slice_bitcast_fusion.7
  498.5 0.7 slice_bitcast_fusion.15
  501.0 1.3 copy.28
  (32 shorter events, 4.5 us)
Async XLA Ops:
  7.2 6.7 %copy-start.2 = (bf16[2,128,128]{2,1,0:T(8,128)(2,1)S(1)}, bf16[2,128,128]{2,1,0:T(8,128)(2,1)}, u32[]{:S(2)}) copy-start(bf16[2,128,128]{2,1,0:T(8,128)(2,1)} %param.16) | copy-start | bytes 196612
  7.2 7.4 %copy-start.5 = (bf16[2,2,128]{2,1,0:T(2,128)(2,1)S(1)}, bf16[2,2,128]{2,1,0:T(2,128)(2,1)}, u32[]{:S(2)}) copy-start(bf16[2,2,128]{2,1,0:T(2,128)(2,1)} %param.15) | copy-start | bytes 3076
  7.2 7.4 %copy-start.6 = (bf16[2,128]{1,0:T(2,128)(2,1)S(1)}, bf16[2,128]{1,0:T(2,128)(2,1)}, u32[]{:S(2)}) copy-start(bf16[2,128]{1,0:T(2,128)(2,1)} %param.17) | copy-start | bytes 1540
  7.2 485.4 %all-reduce.2.cloned.1.call-start = ((), (), s32[]{:S(2)}) async-start(), calls=%async_computation | async-start | bytes 1605632 | tf_op jit(solution)/shard_map/psum | solution.py:457
  392.0 31.6 %copy-start.1 = (f32[648,128]{1,0:T(8,128)S(1)}, f32[648,128]{1,0:T(8,128)}, u32[]{:S(2)}) copy-start(f32[648,128]{1,0:T(8,128)} %get-tuple-element.49) | copy-start | bytes 995332
  392.0 31.6 %copy-start.3 = (f32[136,128]{1,0:T(8,128)S(1)}, f32[136,128]{1,0:T(8,128)}, u32[]{:S(2)}) copy-start(f32[136,128]{1,0:T(8,128)} %get-tuple-element.51) | copy-start | bytes 208900
  392.1 31.6 %copy-start.4 = (f32[136,128]{1,0:T(8,128)S(1)}, f32[136,128]{1,0:T(8,128)}, u32[]{:S(2)}) copy-start(f32[136,128]{1,0:T(8,128)} %get-tuple-element.50) | copy-start | bytes 208900
  493.3 7.7 %copy-start = (bf16[32,256,128]{2,1,0:T(8,128)(2,1)S(1)}, bf16[32,256,128]{2,1,0:T(8,128)(2,1)}, u32[]{:S(2)}) copy-start(bf16[32,256,128]{2,1,0:T(8,128)(2,1)} %get-tuple-element.37) | copy-start | bytes 6291460
Sparse Core Ops, SparseCore 0:
  425.7 66.8 all-reduce.1

commit v2 on v1

--- a/solution.py
+++ b/solution.py
@@ -54,7 +54,34 @@
 def project(z_t, ln, w_t, bias):
     unit, inv = norm(z_t)
     z_hat = (unit * ln[0] + ln[1]).astype(BF16)
-    return unit, inv, z_hat, dot(w_t, z_hat, 1, 0) + bias
+    return unit, inv, z_hat, dot(w_t[...], z_hat, 1, 0) + bias[...]
+
+
+def set_eye(eye):
+    same = lax.broadcasted_iota(jnp.int32, (C, C), 0) == lax.broadcasted_iota(jnp.int32, (C, C), 1)
+    eye[...] = jnp.where(same, 1.0, 0.0).astype(BF16)
+
+
+def set_column(ref, row):
+    column = jnp.broadcast_to(row.astype(F32), (C, C)).T
+    ref[:, :C] = column
+    ref[:, C:] = column
+
+
+def set_pre(block, ln_in, w_proj, b_proj, ln, w_t, bias):
+    for k in range(2):
+        set_column(ln.at[k], ln_in[block, k:k + 1, :])
+    for k in range(5):
+        cols = slice(k * C, (k + 1) * C)
+        set_column(bias.at[cols], b_proj[block:block + 1, cols])
+        w_t[cols, :] = w_proj[block, :, cols].astype(F32).T.astype(BF16)
+
+
+def set_post(block, ln_mid, w_out, b_out, mln, wo_t, bo):
+    for k in range(2):
+        set_column(mln.at[k], ln_mid[block, k:k + 1, :])
+    set_column(bo, b_out[block:block + 1, :])
+    wo_t[...] = w_out[block].astype(F32).T.astype(BF16)
 
 
 def place():
@@ -73,7 +100,7 @@
 def peers():
     me, cy, cx, core = place()
     out = []
-    for dy, dx in ((1, 1), (1, 0), (0, 1), (0, 0)):
+    for dy, dx in ((1, 0), (0, 1), (1, 1), (0, 0)):
         for dc in (1, 0):
             out.append((((cy + dy) % 2) * 2 + (cx + dx) % 2) * 2 + (core + dc) % 2)
     return me, out
@@ -121,8 +148,13 @@
         def _():
             for stage, send_ref, out_ref, send_sem, recv_sem in jobs:
                 pack_rows(stage.at[0], stage.at[1], send_ref, slot)
-                for copy in row_copies(send_ref, out_ref, send_sem, recv_sem, slot):
+                for copy in row_copies(send_ref, out_ref, send_sem, recv_sem, slot)[:4]:
                     copy.start()
+            if slot == ROWS // SEND - 1:
+                for stage, send_ref, out_ref, send_sem, recv_sem in jobs:
+                    for past in range(ROWS // SEND):
+                        for copy in row_copies(send_ref, out_ref, send_sem, recv_sem, past)[4:]:
+                            copy.start()
 
     @pl.when(step == STEPS - 1)
     def _():
@@ -133,16 +165,23 @@
 
 
 def pre_row(r, z_t, mask_ref, ln_ref, w_t_ref, bias_ref, g_ref, a_stage, b_stage):
-    _, _, _, p = project(z_t, ln_ref, w_t_ref[...], bias_ref[...])
+    _, _, _, p = project(z_t, ln_ref, w_t_ref, bias_ref)
     m = mask_ref[0, pl.ds(r, 1), :].astype(F32)
     spread(a_stage, sigmoid(p[:C]) * p[C:2 * C] * m, r)
     spread(b_stage, sigmoid(p[2 * C:3 * C]) * p[3 * C:4 * C] * m, r)
     g_ref[r] = sigmoid(p[4 * C:])
 
 
-def pre_kernel(z_ref, mask_ref, ln_ref, w_t_ref, bias_ref, eye_ref, a_ref, b_ref, g_ref, a_st, b_st, a_send, b_send, a_ss, b_ss, rs):
+def pre_kernel(z_ref, mask_ref, ln_in, w_proj, b_proj, a_ref, b_ref, g_ref, a_st, b_st, a_send, b_send,
+               eye_ref, ln_ref, w_t_ref, bias_ref, a_ss, b_ss, rs):
     step = pl.program_id(0)
-    pl.when(step == 0)(enter)
+
+    @pl.when(step == 0)
+    def _():
+        enter()
+        set_eye(eye_ref)
+        set_pre(0, ln_in, w_proj, b_proj, ln_ref, w_t_ref, bias_ref)
+
     half = step % 2
 
     def body(r, carry):
@@ -154,10 +193,18 @@
     send_rows(step, [(a_st, a_send, a_ref, a_ss, rs.at[0]), (b_st, b_send, b_ref, b_ss, rs.at[1])])
 
 
-def mid_kernel(x_ref, z_ref, g0_ref, mask_ref, mln_ref, wo_t_ref, bo_ref, ln_ref, w_t_ref, bias_ref, eye_ref,
-               a_ref, b_ref, g_ref, zm_ref, a_st, b_st, a_send, b_send, a_ss, b_ss, rs):
+def mid_kernel(x_ref, z_ref, g0_ref, mask_ref, ln_mid, w_out, b_out, ln_in, w_proj, b_proj,
+               a_ref, b_ref, g_ref, zm_ref, a_st, b_st, a_send, b_send,
+               eye_ref, ln_ref, w_t_ref, bias_ref, mln_ref, wo_t_ref, bo_ref, a_ss, b_ss, rs):
     step = pl.program_id(0)
-    pl.when(step == 0)(enter)
+
+    @pl.when(step == 0)
+    def _():
+        enter()
+        set_eye(eye_ref)
+        set_pre(1, ln_in, w_proj, b_proj, ln_ref, w_t_ref, bias_ref)
+        set_post(0, ln_mid, w_out, b_out, mln_ref, wo_t_ref, bo_ref)
+
     half = step % 2
 
     def body(r, carry):
@@ -191,15 +238,19 @@
 def put_post(grad_ref, acc_ref):
     grad_ref[0:C, :] = acc_ref[0]
     grad_ref[C:C + 8, :] = jnp.concatenate([row_sums(acc_ref[1]), row_sums(acc_ref[2]), row_sums(acc_ref[3]), jnp.zeros((5, C), F32)], axis=0)
-
-
-def turn_kernel(x_ref, zm_ref, g_ref, dz_ref, mln_ref, wo_t_ref, wo_ref, bo_ref, eye_ref,
-                dx_ref, z_out_ref, dpg_ref, grad_ref, d_st, d_send, acc_ref, d_ss, rs):
+    grad_ref[C + 8:C + 16, :] = jnp.zeros((8, C), F32)
+
+
+def turn_kernel(x_ref, zm_ref, g_ref, dz_ref, ln_mid, w_out, b_out,
+                dx_ref, z_out_ref, dpg_ref, grad_ref, d_st, d_send, eye_ref, mln_ref, wo_t_ref, bo_ref, acc_ref, d_ss, rs):
     step = pl.program_id(0)
+    wo_ref = w_out.at[1]
 
     @pl.when(step == 0)
     def _():
         enter()
+        set_eye(eye_ref)
+        set_post(1, ln_mid, w_out, b_out, mln_ref, wo_t_ref, bo_ref)
         acc_ref[...] = jnp.zeros_like(acc_ref)
 
     half = step % 2
@@ -223,7 +274,7 @@
 
 
 def pre_back_row(r, z_t, da, db, d_pg, mask_ref, ln_ref, w_t_ref, w_ref, bias_ref, w_acc, b_acc, l_acc):
-    unit, inv, z_hat, p = project(z_t, ln_ref, w_t_ref[...], bias_ref[...])
+    unit, inv, z_hat, p = project(z_t, ln_ref, w_t_ref, bias_ref)
     m = mask_ref[0, pl.ds(r, 1), :].astype(F32)
     parts = []
     for side, d_side in ((0, da), (1, db)):
@@ -247,16 +298,21 @@
     rows = [row_sums(b_acc[k * C:(k + 1) * C, :]) for k in range(5)]
     rows += [row_sums(l_acc[0]), row_sums(l_acc[1]), jnp.zeros((1, C), F32)]
     grad_ref[5 * C:5 * C + 8, :] = jnp.concatenate(rows, axis=0)
-
-
-def back_kernel(da_ref, db_ref, dpg1_ref, zm_ref, mask_ref, dz_ref, x_ref, g_ref, ln_ref, w_t_ref, w_ref, bias_ref,
-                mln_ref, wo_t_ref, wo_ref, bo_ref, eye_ref,
-                dx_ref, dzm_ref, dpg_ref, grad1_ref, grad0_ref, d_st, d_send, w_acc, b_acc, l_acc, acc_ref, d_ss, rs):
+    grad_ref[5 * C + 8:5 * C + 16, :] = jnp.zeros((8, C), F32)
+
+
+def back_kernel(da_ref, db_ref, dpg1_ref, zm_ref, mask_ref, dz_ref, x_ref, g_ref, ln_in, w_proj, b_proj, ln_mid, w_out, b_out,
+                dx_ref, dzm_ref, dpg_ref, grad1_ref, grad0_ref, d_st, d_send,
+                eye_ref, ln_ref, w_t_ref, bias_ref, mln_ref, wo_t_ref, bo_ref, w_acc, b_acc, l_acc, acc_ref, d_ss, rs):
     step = pl.program_id(0)
+    w_ref, wo_ref = w_proj.at[1], w_out.at[0]
 
     @pl.when(step == 0)
     def _():
         enter()
+        set_eye(eye_ref)
+        set_pre(1, ln_in, w_proj, b_proj, ln_ref, w_t_ref, bias_ref)
+        set_post(0, ln_mid, w_out, b_out, mln_ref, wo_t_ref, bo_ref)
         for ref in (w_acc, b_acc, l_acc, acc_ref):
             ref[...] = jnp.zeros_like(ref)
 
@@ -282,12 +338,15 @@
     send_rows(step, [(d_st, d_send, dx_ref, d_ss, rs.at[0])])
 
 
-def last_kernel(da_ref, db_ref, dpg_ref, z_ref, mask_ref, dzm_ref, ln_ref, w_t_ref, w_ref, bias_ref, eye_ref,
-                dz_ref, grad_ref, w_acc, b_acc, l_acc):
+def last_kernel(da_ref, db_ref, dpg_ref, z_ref, mask_ref, dzm_ref, ln_in, w_proj, b_proj,
+                dz_ref, grad_ref, eye_ref, ln_ref, w_t_ref, bias_ref, w_acc, b_acc, l_acc):
     step = pl.program_id(0)
+    w_ref = w_proj.at[0]
 
     @pl.when(step == 0)
     def _():
+        set_eye(eye_ref)
+        set_pre(0, ln_in, w_proj, b_proj, ln_ref, w_t_ref, bias_ref)
         for ref in (w_acc, b_acc, l_acc):
             ref[...] = jnp.zeros_like(ref)
 
@@ -353,11 +412,15 @@
             @pl.when(step == slot)
             def _():
                 pack_channels(stages[j], sends[j], slot)
-                for copy in channel_copies(sends[j], outs[j], sems[j], rs.at[j], slot, top):
+                for copy in channel_copies(sends[j], outs[j], sems[j], rs.at[j], slot, top)[2 - 2 * slot:4 - 2 * slot]:
                     copy.start()
 
     @pl.when(step == 1)
     def _():
+        for slot in range(2):
+            for j in range(n_out):
+                for copy in channel_copies(sends[j], outs[j], sems[j], rs.at[j], slot, (cy + 1 + slot) % 2)[2 * slot:2 + 2 * slot]:
+                    copy.start()
         for j in range(n_out):
             for slot in range(2):
                 wait_sends(channel_copies(sends[j], outs[j], sems[j], rs.at[j], slot, (cy + 1 + slot) % 2))
@@ -368,14 +431,100 @@
 IN_FWD = (lambda r, c, rows: dot(r[0][c, :, rows], r[1][c], 0, 0),)
 IN_BWD = (lambda r, c, rows: dot(r[1][c, rows, :], r[2][c], 1, 1), lambda r, c, rows: dot(r[0][c, rows, :], r[2][c], 1, 0))
 OUT_BWD = (lambda r, c, rows: dot(r[2][c, rows, :], r[1][c], 1, 0), lambda r, c, rows: dot(r[2][c, :, rows], r[0][c], 0, 0))
+
+ALL = 16
+SHARE = 112
+PACKS = (C + 16, C + 16, 5 * C + 16, 5 * C + 16)
+
+
+def share(k):
+    return pl.ds(pl.multiple_of(k * SHARE, SHARE), SHARE)
+
+
+def sum_kernel(p0, p1, p2, p3, tot_ref, send_ref, got_ref, part_ref, ss, rs, ss2, rs2):
+    dp, dap = lax.axis_index("dp"), lax.axis_index("dap")
+    me = dp * GROUP + dap
+    others = [(me + k) % ALL for k in range(1, ALL)]
+    ids = [{"dp": o // GROUP, "dap": o % GROUP} for o in others]
+    sem = pltpu.get_barrier_semaphore()
+    for to in ids:
+        pl.semaphore_signal(sem, inc=1, device_id=to, device_id_type=pl.DeviceIdType.MESH)
+    at = 0
+    for ref, rows in zip((p0, p1, p2, p3), PACKS):
+        send_ref[at:at + rows, :] = ref[...].astype(BF16)
+        at += rows
+    send_ref[at:, :] = jnp.zeros((ALL * SHARE - at, C), BF16)
+    pl.semaphore_wait(sem, ALL - 1)
+
+    def first(to, k, frm):
+        return pltpu.make_async_remote_copy(send_ref.at[share(others[k])], got_ref.at[frm], ss.at[k], rs.at[frm], device_id=to, device_id_type=pl.DeviceIdType.MESH)
+
+    def second(to, k, frm):
+        return pltpu.make_async_remote_copy(part_ref, tot_ref.at[share(frm)], ss2.at[k], rs2.at[frm], device_id=to, device_id_type=pl.DeviceIdType.MESH)
+
+    for k, to in enumerate(ids):
+        first(to, k, me).start()
+    got_ref[me] = send_ref[share(me), :]
+    for k, to in enumerate(ids):
+        first(to, k, others[k]).wait_recv()
+    total = got_ref[0].astype(F32)
+    for k in range(1, ALL):
+        total = total + got_ref[k].astype(F32)
+    part_ref[...] = total
+    for k, to in enumerate(ids):
+        second(to, k, me).start()
+    tot_ref[share(me), :] = total
+    for k, to in enumerate(ids):
+        second(to, k, others[k]).wait_recv()
+    for k, to in enumerate(ids):
+        first(to, k, me).wait_send()
+        second(to, k, me).wait_send()
+
+
+def split_kernel(tot, d_ln_in, d_w_proj, d_b_proj, d_ln_mid, d_w_out, d_b_out):
+    at = 0
+    for k in range(2):
+        d_w_out[k] = tot[at:at + C, :]
+        d_ln_mid[k] = tot[at + C:at + C + 2, :]
+        d_b_out[k:k + 1, :] = tot[at + C + 2:at + C + 3, :]
+        at += C + 16
+    for k in range(2):
+        for j in range(5):
+            d_w_proj[k, :, j * C:(j + 1) * C] = tot[at + j * C:at + (j + 1) * C, :].T
+            d_b_proj[k:k + 1, j * C:(j + 1) * C] = tot[at + 5 * C + j:at + 5 * C + j + 1, :]
+        d_ln_in[k] = tot[at + 5 * C + 5:at + 5 * C + 7, :]
+        at += 5 * C + 16
+
+
+def sum_grads(packs):
+    vmem = pl.BlockSpec(memory_space=pltpu.VMEM)
+    dma = pltpu.SemaphoreType.DMA((ALL,))
+    total = pl.pallas_call(
+        sum_kernel,
+        in_specs=[vmem] * 4,
+        out_specs=vmem,
+        out_shape=jax.ShapeDtypeStruct((ALL * SHARE, C), F32),
+        scratch_shapes=[pltpu.VMEM((ALL * SHARE, C), BF16), pltpu.VMEM((ALL, SHARE, C), BF16), pltpu.VMEM((SHARE, C), F32), dma, dma, dma, dma],
+        compiler_params=pltpu.CompilerParams(vmem_limit_bytes=VMEM_LIMIT, collective_id=8, has_side_effects=True),
+        name="sum",
+    )(*packs)
+    shapes = ((2, 2, C), (2, C, 5 * C), (2, 5 * C), (2, 2, C), (2, C, C), (2, C))
+    return pl.pallas_call(
+        split_kernel,
+        in_specs=[vmem],
+        out_specs=[vmem] * 6,
+        out_shape=[jax.ShapeDtypeStruct(shape, F32) for shape in shapes],
+        name="split",
+    )(total)
+
 
 ANY = pl.BlockSpec(memory_space=pl.ANY)
 TRI = jax.ShapeDtypeStruct((CH, N, N), BF16)
 ROW = jax.ShapeDtypeStruct((ROWS, C, N), BF16)
 ROW32 = jax.ShapeDtypeStruct((ROWS, C, N), F32)
 NATIVE = jax.ShapeDtypeStruct((ROWS, N, C), BF16)
-POST = jax.ShapeDtypeStruct((C + 8, C), F32)
-PRE = jax.ShapeDtypeStruct((5 * C + 8, C), F32)
+POST = jax.ShapeDtypeStruct((C + 16, C), F32)
+PRE = jax.ShapeDtypeStruct((5 * C + 16, C), F32)
 
 
 def by_row(array):
@@ -426,44 +575,28 @@
 def local_step(z_pair, pair_mask, dz_out, ln_in, w_proj, b_proj, ln_mid, w_out, b_out):
     z, dz = z_pair[0], dz_out[0]
     mask = pair_mask.reshape(STEPS, STEP, N)
-    eye = jnp.eye(C, dtype=BF16)
-    ln = jnp.broadcast_to(ln_in.astype(F32)[..., None], (2, 2, C, N))
-    mln = jnp.broadcast_to(ln_mid.astype(F32)[..., None], (2, 2, C, N))
-    bias = jnp.broadcast_to(b_proj.astype(F32)[..., None], (2, 5 * C, N))
-    bo = jnp.broadcast_to(b_out.astype(F32)[..., None], (2, C, N))
-    w_t = jnp.swapaxes(w_proj, 1, 2)
-    wo_t = jnp.swapaxes(w_out, 1, 2)
-    pre = [(ln[k], w_t[k], bias[k]) for k in range(2)]
-    post = [(mln[k], wo_t[k], bo[k]) for k in range(2)]
-
-    a0, b0, g0 = row_call(pre_kernel, "pre0", 0, [z, mask], [*pre[0], eye], [TRI, TRI, ROW32], [ANY, ANY, by_row(ROW32)], 2, [])
-    x0, = channel_call(OUT_FWD, "tri0", 1, [a0, b0], 1)
-    a1, b1, g1, zm = row_call(mid_kernel, "mid", 2, [x0, z, g0, mask], [*post[0], *pre[1], eye], [TRI, TRI, ROW32, ROW],
-                              [ANY, ANY, by_row(ROW32), by_row(ROW)], 2, [])
-    x1, = channel_call(IN_FWD, "tri1", 3, [a1, b1], 1)
+    pre, post = [ln_in, w_proj, b_proj], [ln_mid, w_out, b_out]
+    eye = [pltpu.VMEM((C, C), BF16)]
+    pre_c = [pltpu.VMEM((2, C, N), F32), pltpu.VMEM((5 * C, C), BF16), pltpu.VMEM((5 * C, N), F32)]
+    post_c = [pltpu.VMEM((2, C, N), F32), pltpu.VMEM((C, C), BF16), pltpu.VMEM((C, N), F32)]
     post_acc = [pltpu.VMEM((4, C, C), F32)]
     pre_acc = [pltpu.VMEM((5 * C, C), F32), pltpu.VMEM((5 * C, C), F32), pltpu.VMEM((2, C, C), F32)]
-    dx1, z_new, dpg1, post_g1 = row_call(turn_kernel, "turn", 4, [x1, zm, g1, dz], [mln[1], wo_t[1], w_out[1], bo[1], eye],
-                                         [TRI, NATIVE, ROW32, POST], [ANY, by_row(NATIVE), by_row(ROW32), whole(POST)], 1, post_acc)
+
+    a0, b0, g0 = row_call(pre_kernel, "pre0", 0, [z, mask], pre, [TRI, TRI, ROW32], [ANY, ANY, by_row(ROW32)], 2, eye + pre_c)
+    x0, = channel_call(OUT_FWD, "tri0", 1, [a0, b0], 1)
+    a1, b1, g1, zm = row_call(mid_kernel, "mid", 2, [x0, z, g0, mask], post + pre, [TRI, TRI, ROW32, ROW],
+                              [ANY, ANY, by_row(ROW32), by_row(ROW)], 2, eye + pre_c + post_c)
+    x1, = channel_call(IN_FWD, "tri1", 3, [a1, b1], 1)
+    dx1, z_new, dpg1, post_g1 = row_call(turn_kernel, "turn", 4, [x1, zm, g1, dz], post, [TRI, NATIVE, ROW32, POST],
+                                         [ANY, by_row(NATIVE), by_row(ROW32), whole(POST)], 1, eye + post_c + post_acc)
     da1, db1 = channel_call(IN_BWD, "trib1", 5, [a1, b1, dx1], 2)
     dx0, dzm, dpg0, pre_g1, post_g0 = row_call(
-        back_kernel, "back", 6, [da1, db1, dpg1, zm, mask, dz, x0, g0],
-        [ln[1], w_t[1], w_proj[1], bias[1], mln[0], wo_t[0], w_out[0], bo[0], eye],
-        [TRI, ROW, ROW32, PRE, POST], [ANY, by_row(ROW), by_row(ROW32), whole(PRE), whole(POST)], 1, pre_acc + post_acc)
+        back_kernel, "back", 6, [da1, db1, dpg1, zm, mask, dz, x0, g0], pre + post, [TRI, ROW, ROW32, PRE, POST],
+        [ANY, by_row(ROW), by_row(ROW32), whole(PRE), whole(POST)], 1, eye + pre_c + post_c + pre_acc + post_acc)
     da0, db0 = channel_call(OUT_BWD, "trib0", 7, [a0, b0, dx0], 2)
-    dz_new, pre_g0 = row_call(last_kernel, "last", None, [da0, db0, dpg0, z, mask, dzm], [ln[0], w_t[0], w_proj[0], bias[0], eye],
-                              [NATIVE, PRE], [by_row(NATIVE), whole(PRE)], 0, pre_acc)
-
-    total = lax.psum(jnp.concatenate([pre_g0, pre_g1, post_g0, post_g1]), ("dp", "dap"))
-    pre_g = [total[:5 * C + 8], total[5 * C + 8:2 * (5 * C + 8)]]
-    post_g = [total[2 * (5 * C + 8):2 * (5 * C + 8) + C + 8], total[2 * (5 * C + 8) + C + 8:]]
-    d_w_proj = jnp.stack([g[:5 * C].T for g in pre_g])
-    d_b_proj = jnp.stack([g[5 * C:5 * C + 5].reshape(5 * C) for g in pre_g])
-    d_ln_in = jnp.stack([g[5 * C + 5:5 * C + 7] for g in pre_g])
-    d_w_out = jnp.stack([g[:C] for g in post_g])
-    d_ln_mid = jnp.stack([g[C:C + 2] for g in post_g])
-    d_b_out = jnp.stack([g[C + 2] for g in post_g])
-    return z_new[None], dz_new[None], d_ln_in, d_w_proj, d_b_proj, d_ln_mid, d_w_out, d_b_out
+    dz_new, pre_g0 = row_call(last_kernel, "last", None, [da0, db0, dpg0, z, mask, dzm], pre, [NATIVE, PRE],
+                              [by_row(NATIVE), whole(PRE)], 0, eye + pre_c + pre_acc)
+    return (z_new[None], dz_new[None], *sum_grads([post_g0, post_g1, pre_g0, pre_g1]))
 
 
 def solution(mesh):

time: 510 us -> 451 us (0.88)
  waiting for transfers between devices: 67.1 us -> 0 us
  Pallas kernels: 402 us -> 447 us
  local copies, waits for them, and re-layouts: 18.6 us -> 3.14 us
  between operations: 14.2 us -> 0.71 us
  other arithmetic: 6.95 us -> 0 us
    psum x1 -> x0, waiting for transfers between devices: 67.1 us -> none  [local_step(): lax.psum(jnp.concatenate([pre_g0, pre_g1, post_g0, post_g1]), ('dp', 'dap'))]
    pallas_call x0 -> x2, Pallas kernels: none -> 28.5 us  [the longest x1 26.2 us: sum_grads(): pl.pallas_call(sum_kernel, in_specs=[vmem] * 4, out_specs=vmem, out_shape...]
    pallas_call x5, Pallas kernels: 238 us -> 247 us  [row_call(): pl.pallas_call(kernel, grid=(STEPS,), in_specs=[by_row(x) for x in ins] +...]
    pallas_call x4, Pallas kernels: 164 us -> 171 us  [channel_call(): pl.pallas_call(functools.partial(channel_kernel, products, len(ins), n_ou...]
    broadcast_in_dim x11 -> x0, local copies, waits for them, and re-layouts: 6.65 us -> none  [the longest x2 1.98 us: local_step(): bias = jnp.broadcast_to(b_proj.astype(F32)[..., None], (2, 5 * C, N))]
  transfers between devices with their start and end apart: 1 -> 0, of which waited for: 1 -> 0; matrix products, arithmetic and copies ran while one was open for 0% -> 0% of each run, Pallas kernels for 0% -> 0%
where the time goes in v2:
time: 451 us; the launch traced here: 450 us
  Pallas kernels  447 us (99%)
    pallas_call x5, Pallas kernels, row_call(): pl.pallas_call(kernel, grid=(STEPS,), in_specs=[by_row(x) for x in ins] +...  247 us
    pallas_call x4, Pallas kernels, channel_call(): pl.pallas_call(functools.partial(channel_kernel, products, len(ins), n_ou...  171 us
    pallas_call x1, Pallas kernels, sum_grads(): pl.pallas_call(sum_kernel, in_specs=[vmem] * 4, out_specs=vmem, out_shape...  26.2 us

profile of v2, /device:TPU:0, one launch (start us, length us, event | category | flops | bytes accessed | tf_op | source)
XLA Modules:
  0.0 450.4 jit_solution(15219589242404708844)
XLA Ops:
  0.6 62.2 %pre0.1 = (bf16[16,256,256]{2,1,0:T(8,128)(2,1)}, bf16[16,256,256]{2,1,0:T(8,128)(2,1)}, f32[32,128,256]{2,1,0:T(8,128)}) custom-call(bf16[32,256,128]{2,1,0:T(8,128)(2,1)} %bitcast.5, s32[4,8,256]{2,1,0:T(8,128)} %bitcast.11, bf16[2,2,128]{2,1,0:T(2,128)(2,1)} %ln_in.7, bf16[2,128,640]{2,1,0:T(8,128)(2,1)} %w_proj.7, bf16[2,640]{1,0:T(2,128)(2,1)} %b_proj.7), custom_call_target="tpu_custom_call" | custom-call | tf_op jit(solution)/shard_map/pre0/pallas_call | solution.py:549
  62.8 30.9 %tri0.1.x_ref = bf16[32,128,256]{2,1,0:T(8,128)(2,1)} custom-call(bf16[16,256,256]{2,1,0:T(8,128)(2,1)} %get-tuple-element.36.refs_0_, bf16[16,256,256]{2,1,0:T(8,128)(2,1)} %get-tuple-element.37.refs_1_), custom_call_target="tpu_custom_call" | custom-call | tf_op jit(solution)/shard_map/tri0/pallas_call | solution.py:562
  93.7 62.1 %mid.1 = (bf16[16,256,256]{2,1,0:T(8,128)(2,1)}, bf16[16,256,256]{2,1,0:T(8,128)(2,1)}, f32[32,128,256]{2,1,0:T(8,128)}, bf16[32,128,256]{2,1,0:T(8,128)(2,1)}) custom-call(bf16[32,128,256]{2,1,0:T(8,128)(2,1)} %tri0.1.x_ref, bf16[32,256,128]{2,1,0:T(8,128)(2,1)} %bitcast.6, f32[32,128,256]{2,1,0:T(8,128)} %get-tuple-element.38.g0_ref.g_ref, ...), custom_call_target="tpu_custom_call" | custom-call | tf_op jit(solution)/shard_map/mid/pallas_call | solution.py:549
  155.8 30.6 %tri1.1.x_ref = bf16[32,128,256]{2,1,0:T(8,128)(2,1)} custom-call(bf16[16,256,256]{2,1,0:T(8,128)(2,1)} %get-tuple-element.39.refs_0_, bf16[16,256,256]{2,1,0:T(8,128)(2,1)} %get-tuple-element.40.refs_1_), custom_call_target="tpu_custom_call" | custom-call | tf_op jit(solution)/shard_map/tri1/pallas_call | solution.py:562
  186.4 38.0 %turn.1 = (bf16[16,256,256]{2,1,0:T(8,128)(2,1)}, bf16[32,256,128]{2,1,0:T(8,128)(2,1)}, f32[32,128,256]{2,1,0:T(8,128)}, f32[144,128]{1,0:T(8,128)}) custom-call(bf16[32,128,256]{2,1,0:T(8,128)(2,1)} %tri1.1.x_ref, bf16[32,128,256]{2,1,0:T(8,128)(2,1)} %get-tuple-element.41.zm_ref, f32[32,128,256]{2,1,0:T(8,128)} %get-tuple-element.42.g_ref, ...), custom_call_target="tpu_custom_call" | custom-call | tf_op jit(solution)/shard_map/turn/pallas_call | solution.py:549
  224.4 54.8 %trib1.1 = (bf16[32,128,256]{2,1,0:T(8,128)(2,1)}, bf16[32,128,256]{2,1,0:T(8,128)(2,1)}) custom-call(bf16[16,256,256]{2,1,0:T(8,128)(2,1)} %get-tuple-element.39.refs_0_, bf16[16,256,256]{2,1,0:T(8,128)(2,1)} %get-tuple-element.40.refs_1_, bf16[16,256,256]{2,1,0:T(8,128)(2,1)} %get-tuple-element.44.refs_2_), custom_call_target="tpu_custom_call" | custom-call | tf_op jit(solution)/shard_map/trib1/pallas_call | solution.py:562
  279.2 54.0 %back.1 = (bf16[16,256,256]{2,1,0:T(8,128)(2,1)}, bf16[32,128,256]{2,1,0:T(8,128)(2,1)}, f32[32,128,256]{2,1,0:T(8,128)}, f32[656,128]{1,0:T(8,128)}, f32[144,128]{1,0:T(8,128)}) custom-call(bf16[32,128,256]{2,1,0:T(8,128)(2,1)} %get-tuple-element.45.da_ref, bf16[32,128,256]{2,1,0:T(8,128)(2,1)} %get-tuple-element.46.db_ref, ...), custom_call_target="tpu_custom_call" | custom-call | tf_op jit(solution)/shard_map/back/pallas_call | solution.py:549
  333.2 54.4 %trib0.1 = (bf16[32,128,256]{2,1,0:T(8,128)(2,1)}, bf16[32,128,256]{2,1,0:T(8,128)(2,1)}) custom-call(bf16[16,256,256]{2,1,0:T(8,128)(2,1)} %get-tuple-element.36.refs_0_, bf16[16,256,256]{2,1,0:T(8,128)(2,1)} %get-tuple-element.37.refs_1_, bf16[16,256,256]{2,1,0:T(8,128)(2,1)} %get-tuple-element.48.refs_2_), custom_call_target="tpu_custom_call" | custom-call | tf_op jit(solution)/shard_map/trib0/pallas_call | solution.py:562
  387.6 31.2 %last.1 = (bf16[32,256,128]{2,1,0:T(8,128)(2,1)}, f32[656,128]{1,0:T(8,128)}) custom-call(bf16[32,128,256]{2,1,0:T(8,128)(2,1)} %get-tuple-element.49.da_ref, bf16[32,128,256]{2,1,0:T(8,128)(2,1)} %get-tuple-element.50.db_ref, f32[32,128,256]{2,1,0:T(8,128)} %get-tuple-element.51.dpg_ref, bf16[32,256,128]{2,1,0:T(8,128)(2,1)} %bitcast.7, ...), custom_call_target="tpu_custom_call" | custom-call | tf_op jit(solution)/shard_map/last/pallas_call | solution.py:549
  418.8 26.2 %sum.1.tot = f32[1792,128]{1,0:T(8,128)} custom-call(f32[144,128]{1,0:T(8,128)} %get-tuple-element.54.p0, f32[144,128]{1,0:T(8,128)} %get-tuple-element.55.p1, f32[656,128]{1,0:T(8,128)} %get-tuple-element.56.p2, f32[656,128]{1,0:T(8,128)} %get-tuple-element.57.p3), custom_call_target="tpu_custom_call" | custom-call | tf_op jit(solution)/shard_map/sum/pallas_call | solution.py:502
  445.0 2.3 split.1
  447.3 3.1 copy.18

commit v3 on v2

--- a/solution.py
+++ b/solution.py
@@ -14,7 +14,7 @@
 ROWS = N // GROUP
 CH = C // GROUP
 STEP = 8
-SEND = 16
+UNROLL = 4
 STEPS = ROWS // STEP
 F32 = jnp.float32
 BF16 = jnp.bfloat16
@@ -94,13 +94,16 @@
     sem = pltpu.get_barrier_semaphore()
     for k in range(1, GROUP):
         pl.semaphore_signal(sem, inc=1, device_id={"dap": (me + k) % GROUP}, device_id_type=pl.DeviceIdType.MESH)
-    pl.semaphore_wait(sem, GROUP - 1)
+
+
+def all_in():
+    pl.semaphore_wait(pltpu.get_barrier_semaphore(), GROUP - 1)
 
 
 def peers():
     me, cy, cx, core = place()
     out = []
-    for dy, dx in ((1, 0), (0, 1), (1, 1), (0, 0)):
+    for dy, dx in ((1, 1), (1, 0), (0, 1), (0, 0)):
         for dc in (1, 0):
             out.append((((cy + dy) % 2) * 2 + (cx + dx) % 2) * 2 + (core + dc) % 2)
     return me, out
@@ -111,13 +114,11 @@
         ref[pl.ds(h * C * STEP + row, C, stride=STEP), :] = value[:, h * C:(h + 1) * C]
 
 
-def pack_rows(lo_ref, hi_ref, send_ref, slot):
+def pack_rows(stage, send_ref, slot):
     for h in range(2):
         for q in range(4):
-            at = pl.ds((h * C + q * 32) * STEP, 32 * STEP)
-            lo = lo_ref[at, :].reshape(32, STEP, C)
-            hi = hi_ref[at, :].reshape(32, STEP, C)
-            send_ref[slot, q * 32:(q + 1) * 32, :, h * C:(h + 1) * C] = jnp.concatenate([lo, hi], axis=1).astype(BF16)
+            rows = stage[pl.ds((h * C + q * 32) * STEP, 32 * STEP), :].reshape(32, STEP, C)
+            send_ref[slot, q * 32:(q + 1) * 32, :, h * C:(h + 1) * C] = rows.astype(BF16)
 
 
 def move(src_ref, dst_ref, send_sem, recv_sem, dest, own):
@@ -134,45 +135,53 @@
 
 def row_copies(send_ref, out_ref, send_sem, recv_sem, slot):
     me, dests = peers()
-    start = pl.multiple_of(me * ROWS + slot * SEND, SEND)
+    start = pl.multiple_of(me * ROWS + slot * STEP, STEP)
     return [
-        move(send_ref.at[slot, pl.ds(pl.multiple_of(dest * CH, CH), CH)], out_ref.at[:, pl.ds(start, SEND), :],
+        move(send_ref.at[slot, pl.ds(pl.multiple_of(dest * CH, CH), CH)], out_ref.at[:, pl.ds(start, STEP), :],
              send_sem.at[slot, k], recv_sem, dest, k == GROUP - 1)
         for k, dest in enumerate(dests)
     ]
 
 
 def send_rows(step, jobs):
-    for slot in range(ROWS // SEND):
-        @pl.when(step == 2 * slot + 1)
-        def _():
-            for stage, send_ref, out_ref, send_sem, recv_sem in jobs:
-                pack_rows(stage.at[0], stage.at[1], send_ref, slot)
-                for copy in row_copies(send_ref, out_ref, send_sem, recv_sem, slot)[:4]:
-                    copy.start()
-            if slot == ROWS // SEND - 1:
-                for stage, send_ref, out_ref, send_sem, recv_sem in jobs:
-                    for past in range(ROWS // SEND):
-                        for copy in row_copies(send_ref, out_ref, send_sem, recv_sem, past)[4:]:
-                            copy.start()
+    pl.when(step == 0)(all_in)
+    for stage, send_ref, out_ref, send_sem, recv_sem in jobs:
+        pack_rows(stage, send_ref, step)
+        for copy in row_copies(send_ref, out_ref, send_sem, recv_sem, step):
+            copy.start()
 
     @pl.when(step == STEPS - 1)
     def _():
         for stage, send_ref, out_ref, send_sem, recv_sem in jobs:
-            for slot in range(ROWS // SEND):
+            for slot in range(STEPS):
                 wait_sends(row_copies(send_ref, out_ref, send_sem, recv_sem, slot))
             pltpu.make_async_copy(out_ref, out_ref, recv_sem).wait()
 
 
-def pre_row(r, z_t, mask_ref, ln_ref, w_t_ref, bias_ref, g_ref, a_stage, b_stage):
-    _, _, _, p = project(z_t, ln_ref, w_t_ref, bias_ref)
+def rows_loop(body):
+    def step(r, carry):
+        body(r)
+        return carry
+
+    lax.fori_loop(0, STEP, step, 0, unroll=UNROLL)
+
+
+def pre_row(r, z_t, mask_ref, ln_ref, w_t_ref, bias_ref, g_ref, keep_ref, unit_ref, inv_ref, a_stage, b_stage):
+    unit, inv, _, p = project(z_t, ln_ref, w_t_ref, bias_ref)
+    unit_ref[r] = unit
+    inv_ref[0, pl.ds(r, 1), :] = inv
     m = mask_ref[0, pl.ds(r, 1), :].astype(F32)
-    spread(a_stage, sigmoid(p[:C]) * p[C:2 * C] * m, r)
-    spread(b_stage, sigmoid(p[2 * C:3 * C]) * p[3 * C:4 * C] * m, r)
+    for side, stage in ((0, a_stage), (1, b_stage)):
+        s = sigmoid(p[2 * side * C:(2 * side + 1) * C])
+        v = p[(2 * side + 1) * C:(2 * side + 2) * C]
+        sm = s * m
+        spread(stage, sm * v, r)
+        keep_ref[r, 2 * side] = sm
+        keep_ref[r, 2 * side + 1] = v * (1.0 - s)
     g_ref[r] = sigmoid(p[4 * C:])
 
 
-def pre_kernel(z_ref, mask_ref, ln_in, w_proj, b_proj, a_ref, b_ref, g_ref, a_st, b_st, a_send, b_send,
+def pre_kernel(z_ref, mask_ref, ln_in, w_proj, b_proj, a_ref, b_ref, g_ref, keep_ref, unit_ref, inv_ref, a_st, b_st, a_send, b_send,
                eye_ref, ln_ref, w_t_ref, bias_ref, a_ss, b_ss, rs):
     step = pl.program_id(0)
 
@@ -182,19 +191,16 @@
         set_eye(eye_ref)
         set_pre(0, ln_in, w_proj, b_proj, ln_ref, w_t_ref, bias_ref)
 
-    half = step % 2
-
-    def body(r, carry):
+    @rows_loop
+    def _(r):
         z_t = dot(eye_ref[...], z_ref[r], 1, 1)
-        pre_row(r, z_t, mask_ref, ln_ref, w_t_ref, bias_ref, g_ref, a_st.at[half], b_st.at[half])
-        return carry
-
-    lax.fori_loop(0, STEP, body, 0)
+        pre_row(r, z_t, mask_ref, ln_ref, w_t_ref, bias_ref, g_ref, keep_ref, unit_ref, inv_ref, a_st, b_st)
+
     send_rows(step, [(a_st, a_send, a_ref, a_ss, rs.at[0]), (b_st, b_send, b_ref, b_ss, rs.at[1])])
 
 
 def mid_kernel(x_ref, z_ref, g0_ref, mask_ref, ln_mid, w_out, b_out, ln_in, w_proj, b_proj,
-               a_ref, b_ref, g_ref, zm_ref, a_st, b_st, a_send, b_send,
+               a_ref, b_ref, g_ref, keep_ref, unit_ref, inv_ref, zm_ref, gu_ref, munit_ref, minv_ref, a_st, b_st, a_send, b_send,
                eye_ref, ln_ref, w_t_ref, bias_ref, mln_ref, wo_t_ref, bo_ref, a_ss, b_ss, rs):
     step = pl.program_id(0)
 
@@ -205,25 +211,26 @@
         set_pre(1, ln_in, w_proj, b_proj, ln_ref, w_t_ref, bias_ref)
         set_post(0, ln_mid, w_out, b_out, mln_ref, wo_t_ref, bo_ref)
 
-    half = step % 2
-
-    def body(r, carry):
-        unit, _ = norm(x_ref[r].astype(F32))
+    @rows_loop
+    def _(r):
+        unit, inv = norm(x_ref[r].astype(F32))
+        munit_ref[r] = unit
+        minv_ref[0, pl.ds(r, 1), :] = inv
         x_hat = (unit * mln_ref[0] + mln_ref[1]).astype(BF16)
         update = dot(wo_t_ref[...], x_hat, 1, 0) + bo_ref[...]
-        z_new = (dot(eye_ref[...], z_ref[r], 1, 1) + g0_ref[r] * update).astype(BF16)
+        g = g0_ref[r]
+        change = g * update
+        gu_ref[r] = change * (1.0 - g)
+        z_new = (dot(eye_ref[...], z_ref[r], 1, 1) + change).astype(BF16)
         zm_ref[r] = z_new
-        pre_row(r, z_new.astype(F32), mask_ref, ln_ref, w_t_ref, bias_ref, g_ref, a_st.at[half], b_st.at[half])
-        return carry
-
-    lax.fori_loop(0, STEP, body, 0)
+        pre_row(r, z_new.astype(F32), mask_ref, ln_ref, w_t_ref, bias_ref, g_ref, keep_ref, unit_ref, inv_ref, a_st, b_st)
+
     send_rows(step, [(a_st, a_send, a_ref, a_ss, rs.at[0]), (b_st, b_send, b_ref, b_ss, rs.at[1])])
 
 
-def post_back_row(x_t, g, dz, mln_ref, wo_t_ref, wo_ref, bo_ref, acc_ref):
-    unit, inv = norm(x_t)
-    x_hat = (unit * mln_ref[0] + mln_ref[1]).astype(BF16)
-    update = dot(wo_t_ref[...], x_hat, 1, 0) + bo_ref[...]
+def post_back_row(unit, inv, g, dz, mln_ref, wo_ref, acc_ref, x_hat=None):
+    if x_hat is None:
+        x_hat = (unit * mln_ref[0] + mln_ref[1]).astype(BF16)
     d_up = dz * g
     d_up_bf = d_up.astype(BF16)
     acc_ref[0] += dot(x_hat, d_up_bf, 1, 1)
@@ -231,8 +238,7 @@
     d_hat = dot(wo_ref[...], d_up_bf, 1, 0).astype(BF16).astype(F32)
     acc_ref[1] += fold(d_hat * unit)
     acc_ref[2] += fold(d_hat)
-    dx = norm_back(d_hat, unit, inv, mln_ref[0])
-    return update, dx, dz * update * g * (1.0 - g)
+    return norm_back(d_hat, unit, inv, mln_ref[0])
 
 
 def put_post(grad_ref, acc_ref):
@@ -253,18 +259,16 @@
         set_post(1, ln_mid, w_out, b_out, mln_ref, wo_t_ref, bo_ref)
         acc_ref[...] = jnp.zeros_like(acc_ref)
 
-    half = step % 2
-
-    def body(r, carry):
+    @rows_loop
+    def _(r):
         dz = dot(eye_ref[...], dz_ref[r], 1, 1)
         g = g_ref[r]
-        update, dx, d_pg = post_back_row(x_ref[r].astype(F32), g, dz, mln_ref, wo_t_ref, wo_ref, bo_ref, acc_ref)
-        dpg_ref[r] = d_pg
-        z_out_ref[r] = (zm_ref[r].astype(F32) + g * update).T.astype(BF16)
-        spread(d_st.at[half], dx, r)
-        return carry
-
-    lax.fori_loop(0, STEP, body, 0)
+        unit, inv = norm(x_ref[r].astype(F32))
+        x_hat = (unit * mln_ref[0] + mln_ref[1]).astype(BF16)
+        change = g * (dot(wo_t_ref[...], x_hat, 1, 0) + bo_ref[...])
+        dpg_ref[r] = dz * change * (1.0 - g)
+        z_out_ref[r] = (zm_ref[r].astype(F32) + change).T.astype(BF16)
+        spread(d_st, post_back_row(unit, inv, g, dz, mln_ref, wo_ref, acc_ref, x_hat), r)
 
     @pl.when(step == STEPS - 1)
     def _():
@@ -273,15 +277,12 @@
     send_rows(step, [(d_st, d_send, dx_ref, d_ss, rs.at[0])])
 
 
-def pre_back_row(r, z_t, da, db, d_pg, mask_ref, ln_ref, w_t_ref, w_ref, bias_ref, w_acc, b_acc, l_acc):
-    unit, inv, z_hat, p = project(z_t, ln_ref, w_t_ref, bias_ref)
-    m = mask_ref[0, pl.ds(r, 1), :].astype(F32)
+def pre_back_row(unit, inv, keep, da, db, d_pg, ln_ref, w_ref, w_acc, b_acc, l_acc):
+    z_hat = (unit * ln_ref[0] + ln_ref[1]).astype(BF16)
     parts = []
     for side, d_side in ((0, da), (1, db)):
-        s = sigmoid(p[2 * side * C:(2 * side + 1) * C])
-        v = p[(2 * side + 1) * C:(2 * side + 2) * C]
-        d_v = d_side * m * s
-        parts += [d_v * v * (1.0 - s), d_v]
+        d_v = d_side * keep[2 * side]
+        parts += [d_v * keep[2 * side + 1], d_v]
     parts.append(d_pg)
     for k, part in enumerate(parts):
         b_acc[k * C:(k + 1) * C, :] += fold(part)
@@ -301,9 +302,14 @@
     grad_ref[5 * C + 8:5 * C + 16, :] = jnp.zeros((8, C), F32)
 
 
-def back_kernel(da_ref, db_ref, dpg1_ref, zm_ref, mask_ref, dz_ref, x_ref, g_ref, ln_in, w_proj, b_proj, ln_mid, w_out, b_out,
+def set_gains(ref, ln, block):
+    for k in range(2):
+        set_column(ref.at[k], ln[block, k:k + 1, :])
+
+
+def back_kernel(da_ref, db_ref, dpg1_ref, keep_ref, unit_ref, inv_ref, dz_ref, munit_ref, minv_ref, g_ref, gu_ref, ln_in, w_proj, ln_mid, w_out,
                 dx_ref, dzm_ref, dpg_ref, grad1_ref, grad0_ref, d_st, d_send,
-                eye_ref, ln_ref, w_t_ref, bias_ref, mln_ref, wo_t_ref, bo_ref, w_acc, b_acc, l_acc, acc_ref, d_ss, rs):
+                eye_ref, ln_ref, mln_ref, w_acc, b_acc, l_acc, acc_ref, d_ss, rs):
     step = pl.program_id(0)
     w_ref, wo_ref = w_proj.at[1], w_out.at[0]
 
@@ -311,24 +317,21 @@
     def _():
         enter()
         set_eye(eye_ref)
-        set_pre(1, ln_in, w_proj, b_proj, ln_ref, w_t_ref, bias_ref)
-        set_post(0, ln_mid, w_out, b_out, mln_ref, wo_t_ref, bo_ref)
+        set_gains(ln_ref, ln_in, 1)
+        set_gains(mln_ref, ln_mid, 0)
         for ref in (w_acc, b_acc, l_acc, acc_ref):
             ref[...] = jnp.zeros_like(ref)
 
-    half = step % 2
-
-    def body(r, carry):
-        dzn = pre_back_row(r, zm_ref[r].astype(F32), da_ref[r].astype(F32), db_ref[r].astype(F32), dpg1_ref[r], mask_ref,
-                           ln_ref, w_t_ref, w_ref, bias_ref, w_acc, b_acc, l_acc)
+    @rows_loop
+    def _(r):
+        at = pl.ds(r, 1)
+        dzn = pre_back_row(unit_ref[r], inv_ref[0, at, :], keep_ref.at[r], da_ref[r].astype(F32), db_ref[r].astype(F32), dpg1_ref[r],
+                           ln_ref, w_ref, w_acc, b_acc, l_acc)
         dzm = (dot(eye_ref[...], dz_ref[r], 1, 1) + dzn).astype(BF16)
         dzm_ref[r] = dzm
-        _, dx, d_pg = post_back_row(x_ref[r].astype(F32), g_ref[r], dzm.astype(F32), mln_ref, wo_t_ref, wo_ref, bo_ref, acc_ref)
-        dpg_ref[r] = d_pg
-        spread(d_st.at[half], dx, r)
-        return carry
-
-    lax.fori_loop(0, STEP, body, 0)
+        dzm = dzm.astype(F32)
+        dpg_ref[r] = dzm * gu_ref[r]
+        spread(d_st, post_back_row(munit_ref[r], minv_ref[0, at, :], g_ref[r], dzm, mln_ref, wo_ref, acc_ref), r)
 
     @pl.when(step == STEPS - 1)
     def _():
@@ -338,26 +341,22 @@
     send_rows(step, [(d_st, d_send, dx_ref, d_ss, rs.at[0])])
 
 
-def last_kernel(da_ref, db_ref, dpg_ref, z_ref, mask_ref, dzm_ref, ln_in, w_proj, b_proj,
-                dz_ref, grad_ref, eye_ref, ln_ref, w_t_ref, bias_ref, w_acc, b_acc, l_acc):
+def last_kernel(da_ref, db_ref, dpg_ref, keep_ref, unit_ref, inv_ref, dzm_ref, ln_in, w_proj,
+                dz_ref, grad_ref, ln_ref, w_acc, b_acc, l_acc):
     step = pl.program_id(0)
     w_ref = w_proj.at[0]
 
     @pl.when(step == 0)
     def _():
-        set_eye(eye_ref)
-        set_pre(0, ln_in, w_proj, b_proj, ln_ref, w_t_ref, bias_ref)
+        set_gains(ln_ref, ln_in, 0)
         for ref in (w_acc, b_acc, l_acc):
             ref[...] = jnp.zeros_like(ref)
 
-    def body(r, carry):
-        z_t = dot(eye_ref[...], z_ref[r], 1, 1)
-        dzn = pre_back_row(r, z_t, da_ref[r].astype(F32), db_ref[r].astype(F32), dpg_ref[r], mask_ref,
-                           ln_ref, w_t_ref, w_ref, bias_ref, w_acc, b_acc, l_acc)
+    @rows_loop
+    def _(r):
+        dzn = pre_back_row(unit_ref[r], inv_ref[0, pl.ds(r, 1), :], keep_ref.at[r], da_ref[r].astype(F32), db_ref[r].astype(F32), dpg_ref[r],
+                           ln_ref, w_ref, w_acc, b_acc, l_acc)
         dz_ref[r] = (dzm_ref[r].astype(F32) + dzn).T.astype(BF16)
-        return carry
-
-    lax.fori_loop(0, STEP, body, 0)
 
     @pl.when(step == STEPS - 1)
     def _():
@@ -412,15 +411,13 @@
             @pl.when(step == slot)
             def _():
                 pack_channels(stages[j], sends[j], slot)
-                for copy in channel_copies(sends[j], outs[j], sems[j], rs.at[j], slot, top)[2 - 2 * slot:4 - 2 * slot]:
+                if slot == 0 and j == 0:
+                    all_in()
+                for copy in channel_copies(sends[j], outs[j], sems[j], rs.at[j], slot, top):
                     copy.start()
 
     @pl.when(step == 1)
     def _():
-        for slot in range(2):
-            for j in range(n_out):
-                for copy in channel_copies(sends[j], outs[j], sems[j], rs.at[j], slot, (cy + 1 + slot) % 2)[2 * slot:2 + 2 * slot]:
-                    copy.start()
         for j in range(n_out):
             for slot in range(2):
                 wait_sends(channel_copies(sends[j], outs[j], sems[j], rs.at[j], slot, (cy + 1 + slot) % 2))
@@ -525,6 +522,8 @@
 NATIVE = jax.ShapeDtypeStruct((ROWS, N, C), BF16)
 POST = jax.ShapeDtypeStruct((C + 16, C), F32)
 PRE = jax.ShapeDtypeStruct((5 * C + 16, C), F32)
+KEEP = jax.ShapeDtypeStruct((ROWS, 4, C, N), F32)
+INV = jax.ShapeDtypeStruct((STEPS, STEP, N), F32)
 
 
 def by_row(array):
@@ -544,8 +543,8 @@
 
 
 def row_call(kernel, name, collective_id, ins, consts, outs, specs, n_send, scratch):
-    sent = [pltpu.VMEM((2, 2 * C * STEP, C), F32)] * n_send + [pltpu.VMEM((ROWS // SEND, C, SEND, N), BF16)] * n_send
-    sems = [pltpu.SemaphoreType.DMA((ROWS // SEND, GROUP))] * n_send + ([pltpu.SemaphoreType.DMA((n_send,))] if n_send else [])
+    sent = [pltpu.VMEM((2 * C * STEP, C), F32)] * n_send + [pltpu.VMEM((STEPS, C, STEP, N), BF16)] * n_send
+    sems = [pltpu.SemaphoreType.DMA((STEPS, GROUP))] * n_send + ([pltpu.SemaphoreType.DMA((n_send,))] if n_send else [])
     return pl.pallas_call(
         kernel,
         grid=(STEPS,),
@@ -582,20 +581,24 @@
     post_acc = [pltpu.VMEM((4, C, C), F32)]
     pre_acc = [pltpu.VMEM((5 * C, C), F32), pltpu.VMEM((5 * C, C), F32), pltpu.VMEM((2, C, C), F32)]
 
-    a0, b0, g0 = row_call(pre_kernel, "pre0", 0, [z, mask], pre, [TRI, TRI, ROW32], [ANY, ANY, by_row(ROW32)], 2, eye + pre_c)
+    kept = [by_row(ROW32), by_row(KEEP), by_row(ROW32), by_row(INV)]
+    a0, b0, g0, keep0, unit0, inv0 = row_call(pre_kernel, "pre0", 0, [z, mask], pre, [TRI, TRI, ROW32, KEEP, ROW32, INV],
+                                              [ANY, ANY, *kept], 2, eye + pre_c)
     x0, = channel_call(OUT_FWD, "tri0", 1, [a0, b0], 1)
-    a1, b1, g1, zm = row_call(mid_kernel, "mid", 2, [x0, z, g0, mask], post + pre, [TRI, TRI, ROW32, ROW],
-                              [ANY, ANY, by_row(ROW32), by_row(ROW)], 2, eye + pre_c + post_c)
+    a1, b1, g1, keep1, unit1, inv1, zm, gu0, munit0, minv0 = row_call(
+        mid_kernel, "mid", 2, [x0, z, g0, mask], post + pre, [TRI, TRI, ROW32, KEEP, ROW32, INV, ROW, ROW32, ROW32, INV],
+        [ANY, ANY, *kept, by_row(ROW), by_row(ROW32), by_row(ROW32), by_row(INV)], 2, eye + pre_c + post_c)
     x1, = channel_call(IN_FWD, "tri1", 3, [a1, b1], 1)
     dx1, z_new, dpg1, post_g1 = row_call(turn_kernel, "turn", 4, [x1, zm, g1, dz], post, [TRI, NATIVE, ROW32, POST],
                                          [ANY, by_row(NATIVE), by_row(ROW32), whole(POST)], 1, eye + post_c + post_acc)
     da1, db1 = channel_call(IN_BWD, "trib1", 5, [a1, b1, dx1], 2)
+    gains = [pltpu.VMEM((2, C, N), F32)]
     dx0, dzm, dpg0, pre_g1, post_g0 = row_call(
-        back_kernel, "back", 6, [da1, db1, dpg1, zm, mask, dz, x0, g0], pre + post, [TRI, ROW, ROW32, PRE, POST],
-        [ANY, by_row(ROW), by_row(ROW32), whole(PRE), whole(POST)], 1, eye + pre_c + post_c + pre_acc + post_acc)
+        back_kernel, "back", 6, [da1, db1, dpg1, keep1, unit1, inv1, dz, munit0, minv0, g0, gu0], [ln_in, w_proj, ln_mid, w_out],
+        [TRI, ROW, ROW32, PRE, POST], [ANY, by_row(ROW), by_row(ROW32), whole(PRE), whole(POST)], 1, eye + gains * 2 + pre_acc + post_acc)
     da0, db0 = channel_call(OUT_BWD, "trib0", 7, [a0, b0, dx0], 2)
-    dz_new, pre_g0 = row_call(last_kernel, "last", None, [da0, db0, dpg0, z, mask, dzm], pre, [NATIVE, PRE],
-                              [by_row(NATIVE), whole(PRE)], 0, eye + pre_c + pre_acc)
+    dz_new, pre_g0 = row_call(last_kernel, "last", None, [da0, db0, dpg0, keep0, unit0, inv0, dzm], [ln_in, w_proj], [NATIVE, PRE],
+                              [by_row(NATIVE), whole(PRE)], 0, gains + pre_acc)
     return (z_new[None], dz_new[None], *sum_grads([post_g0, post_g1, pre_g0, pre_g1]))
 
 

time: 451 us -> 385 us (0.85)
  Pallas kernels: 447 us -> 381 us
    pallas_call x5, Pallas kernels: 247 us -> 191 us  [row_call(): pl.pallas_call(kernel, grid=(STEPS,), in_specs=[by_row(x) for x in ins] +...]
    pallas_call x4, Pallas kernels: 171 us -> 162 us  [channel_call(): pl.pallas_call(functools.partial(channel_kernel, products, len(ins), n_ou...]
where the time goes in v3:
time: 385 us
  Pallas kernels  381 us (99%)
    pallas_call x5, Pallas kernels, row_call(): pl.pallas_call(kernel, grid=(STEPS,), in_specs=[by_row(x) for x in ins] +...  191 us
    pallas_call x4, Pallas kernels, channel_call(): pl.pallas_call(functools.partial(channel_kernel, products, len(ins), n_ou...  162 us
    pallas_call x1, Pallas kernels, sum_grads(): pl.pallas_call(sum_kernel, in_specs=[vmem] * 4, out_specs=vmem, out_shape...  25.7 us

profile of v3, /device:TPU:0, one launch (start us, length us, event | category | flops | bytes accessed | tf_op | source)
XLA Modules:
  0.0 384.7 jit_solution(9768119428579100127)
XLA Ops:
  0.6 55.9 %pre0.1 = (bf16[16,256,256]{2,1,0:T(8,128)(2,1)}, bf16[16,256,256]{2,1,0:T(8,128)(2,1)}, f32[32,128,256]{2,1,0:T(8,128)}, f32[32,4,128,256]{3,2,1,0:T(8,128)}, f...) custom-call(bf16[32,256,128]{2,1,0:T(8,128)(2,1)} %bitcast.7, s32[4,8,256]{2,1,0:T(8,128)} %bitcast.10, ...), custom_call_target="tpu_custom_call" | custom-call | tf_op jit(solution)/shard_map/pre0/pallas_call | solution.py:548
  56.6 28.8 %tri0.1.x_ref = bf16[32,128,256]{2,1,0:T(8,128)(2,1)} custom-call(bf16[16,256,256]{2,1,0:T(8,128)(2,1)} %get-tuple-element.45.refs_0_, bf16[16,256,256]{2,1,0:T(8,128)(2,1)} %get-tuple-element.46.refs_1_), custom_call_target="tpu_custom_call" | custom-call | tf_op jit(solution)/shard_map/tri0/pallas_call | solution.py:561
  85.4 55.1 %mid.1 = (bf16[16,256,256]{2,1,0:T(8,128)(2,1)}, bf16[16,256,256]{2,1,0:T(8,128)(2,1)}, f32[32,128,256]{2,1,0:T(8,128)}, f32[32,4,128,256]{3,2,1,0:T(8,128)}, f3...) custom-call(bf16[32,128,256]{2,1,0:T(8,128)(2,1)} %tri0.1.x_ref, ...), custom_call_target="tpu_custom_call" | custom-call | tf_op jit(solution)/shard_map/mid/pallas_call | solution.py:548
  140.5 28.8 %tri1.1.x_ref = bf16[32,128,256]{2,1,0:T(8,128)(2,1)} custom-call(bf16[16,256,256]{2,1,0:T(8,128)(2,1)} %get-tuple-element.48.refs_0_, bf16[16,256,256]{2,1,0:T(8,128)(2,1)} %get-tuple-element.49.refs_1_), custom_call_target="tpu_custom_call" | custom-call | tf_op jit(solution)/shard_map/tri1/pallas_call | solution.py:561
  169.4 29.3 %turn.1 = (bf16[16,256,256]{2,1,0:T(8,128)(2,1)}, bf16[32,256,128]{2,1,0:T(8,128)(2,1)}, f32[32,128,256]{2,1,0:T(8,128)}, f32[144,128]{1,0:T(8,128)}) custom-call(bf16[32,128,256]{2,1,0:T(8,128)(2,1)} %tri1.1.x_ref, bf16[32,128,256]{2,1,0:T(8,128)(2,1)} %get-tuple-element.50.zm_ref, f32[32,128,256]{2,1,0:T(8,128)} %get-tuple-element.51.g_ref, ...), custom_call_target="tpu_custom_call" | custom-call | tf_op jit(solution)/shard_map/turn/pallas_call | solution.py:548
  198.7 52.1 %trib1.1 = (bf16[32,128,256]{2,1,0:T(8,128)(2,1)}, bf16[32,128,256]{2,1,0:T(8,128)(2,1)}) custom-call(bf16[16,256,256]{2,1,0:T(8,128)(2,1)} %get-tuple-element.48.refs_0_, bf16[16,256,256]{2,1,0:T(8,128)(2,1)} %get-tuple-element.49.refs_1_, bf16[16,256,256]{2,1,0:T(8,128)(2,1)} %get-tuple-element.53.refs_2_), custom_call_target="tpu_custom_call" | custom-call | tf_op jit(solution)/shard_map/trib1/pallas_call | solution.py:561
  250.7 35.0 %back.1 = (bf16[16,256,256]{2,1,0:T(8,128)(2,1)}, bf16[32,128,256]{2,1,0:T(8,128)(2,1)}, f32[32,128,256]{2,1,0:T(8,128)}, f32[656,128]{1,0:T(8,128)}, f32[144,128]{1,0:T(8,128)}) custom-call(bf16[32,128,256]{2,1,0:T(8,128)(2,1)} %get-tuple-element.54.da_ref, bf16[32,128,256]{2,1,0:T(8,128)(2,1)} %get-tuple-element.55.db_ref, ...), custom_call_target="tpu_custom_call" | custom-call | tf_op jit(solution)/shard_map/back/pallas_call | solution.py:548
  285.8 52.2 %trib0.1 = (bf16[32,128,256]{2,1,0:T(8,128)(2,1)}, bf16[32,128,256]{2,1,0:T(8,128)(2,1)}) custom-call(bf16[16,256,256]{2,1,0:T(8,128)(2,1)} %get-tuple-element.45.refs_0_, bf16[16,256,256]{2,1,0:T(8,128)(2,1)} %get-tuple-element.46.refs_1_, bf16[16,256,256]{2,1,0:T(8,128)(2,1)} %get-tuple-element.63.refs_2_), custom_call_target="tpu_custom_call" | custom-call | tf_op jit(solution)/shard_map/trib0/pallas_call | solution.py:561
  338.0 15.6 %last.1 = (bf16[32,256,128]{2,1,0:T(8,128)(2,1)}, f32[656,128]{1,0:T(8,128)}) custom-call(bf16[32,128,256]{2,1,0:T(8,128)(2,1)} %get-tuple-element.64.da_ref, bf16[32,128,256]{2,1,0:T(8,128)(2,1)} %get-tuple-element.65.db_ref, f32[32,128,256]{2,1,0:T(8,128)} %get-tuple-element.66.dpg_ref, f32[32,4,128,256]{3,2,1,0:T(8,128)} %get-tuple-element.67.keep_ref, ...), custom_call_target="tpu_custom_call" | custom-call | tf_op jit(solution)/shard_map/last/pallas_call | solution.py:548
  353.6 25.7 %sum.1.tot = f32[1792,128]{1,0:T(8,128)} custom-call(f32[144,128]{1,0:T(8,128)} %get-tuple-element.72.p0, f32[144,128]{1,0:T(8,128)} %get-tuple-element.73.p1, f32[656,128]{1,0:T(8,128)} %get-tuple-element.74.p2, f32[656,128]{1,0:T(8,128)} %get-tuple-element.75.p3), custom_call_target="tpu_custom_call" | custom-call | tf_op jit(solution)/shard_map/sum/pallas_call | solution.py:499
  379.3 2.3 split.1
  381.6 3.1 copy.18

commit v4 on v3

--- a/solution.py
+++ b/solution.py
@@ -144,7 +144,6 @@
 
 
 def send_rows(step, jobs):
-    pl.when(step == 0)(all_in)
     for stage, send_ref, out_ref, send_sem, recv_sem in jobs:
         pack_rows(stage, send_ref, step)
         for copy in row_copies(send_ref, out_ref, send_sem, recv_sem, step):
@@ -156,6 +155,58 @@
             for slot in range(STEPS):
                 wait_sends(row_copies(send_ref, out_ref, send_sem, recv_sem, slot))
             pltpu.make_async_copy(out_ref, out_ref, recv_sem).wait()
+
+
+OUT_FWD = (lambda r, c: dot(r[0][c], r[1][c], 1, 1),)
+IN_FWD = (lambda r, c: dot(r[0][c], r[1][c], 0, 0),)
+IN_BWD = (lambda r, c: dot(r[1][c], r[2][c], 1, 1), lambda r, c: dot(r[0][c], r[2][c], 1, 0))
+OUT_BWD = (lambda r, c: dot(r[2][c], r[1][c], 1, 0), lambda r, c: dot(r[2][c], r[0][c], 0, 0))
+
+
+def back_copy(job, t, k, dest, frm):
+    stage, send_ref, land_ref, send_sem, recv_sem = job
+    return pltpu.make_async_remote_copy(
+        send_ref.at[t, dest], land_ref.at[t, :, pl.ds(pl.multiple_of(frm * CH, CH), CH), :], send_sem.at[t, k], recv_sem.at[t, frm],
+        device_id={"dap": dest}, device_id_type=pl.DeviceIdType.MESH)
+
+
+def channel_part(products, ins, jobs):
+    for product, job in zip(products, jobs):
+        def body(c, carry):
+            value = product(ins, c)
+            for h in range(2):
+                job[0][pl.ds((h * 2 + c // 8) * N * 8 + c % 8, N, stride=8), :] = value[:, h * C:(h + 1) * C]
+            return carry
+
+        lax.fori_loop(0, CH, body, 0, unroll=4)
+    all_in()
+    me, dests = peers()
+    for t in range(STEPS):
+        for job in jobs:
+            stage, send_ref, land_ref = job[:3]
+            for dest in range(GROUP):
+                for h in range(2):
+                    at = h * 2 * N * 8 + (dest * ROWS + t * STEP) * 8
+                    lo = stage[pl.ds(at, 64), :].reshape(STEP, 8, C)
+                    hi = stage[pl.ds(at + N * 8, 64), :].reshape(STEP, 8, C)
+                    send_ref[t, dest, :, :, h * C:(h + 1) * C] = jnp.concatenate([lo, hi], axis=1).astype(BF16)
+            for k, dest in enumerate(dests[:-1]):
+                back_copy(job, t, k, dest, me).start()
+            land_ref[t, :, pl.ds(pl.multiple_of(me * CH, CH), CH), :] = send_ref[t, me]
+
+
+def arrive(t, jobs):
+    me, dests = peers()
+    for job in jobs:
+        for k, frm in enumerate(dests[:-1]):
+            back_copy(job, t, k, frm, frm).wait_recv()
+
+    @pl.when(t == STEPS - 1)
+    def _():
+        for job in jobs:
+            for slot in range(STEPS):
+                for k, dest in enumerate(dests[:-1]):
+                    back_copy(job, slot, k, dest, me).wait_send()
 
 
 def rows_loop(body):
@@ -196,13 +247,16 @@
         z_t = dot(eye_ref[...], z_ref[r], 1, 1)
         pre_row(r, z_t, mask_ref, ln_ref, w_t_ref, bias_ref, g_ref, keep_ref, unit_ref, inv_ref, a_st, b_st)
 
+    pl.when(step == 0)(all_in)
     send_rows(step, [(a_st, a_send, a_ref, a_ss, rs.at[0]), (b_st, b_send, b_ref, b_ss, rs.at[1])])
 
 
-def mid_kernel(x_ref, z_ref, g0_ref, mask_ref, ln_mid, w_out, b_out, ln_in, w_proj, b_proj,
+def mid_kernel(a_in, b_in, z_ref, g0_ref, mask_ref, ln_mid, w_out, b_out, ln_in, w_proj, b_proj,
                a_ref, b_ref, g_ref, keep_ref, unit_ref, inv_ref, zm_ref, gu_ref, munit_ref, minv_ref, a_st, b_st, a_send, b_send,
-               eye_ref, ln_ref, w_t_ref, bias_ref, mln_ref, wo_t_ref, bo_ref, a_ss, b_ss, rs):
+               eye_ref, ln_ref, w_t_ref, bias_ref, mln_ref, wo_t_ref, bo_ref, a_ss, b_ss, rs,
+               st0, se0, la0, ss0, rv0):
     step = pl.program_id(0)
+    jobs = [(st0, se0, la0, ss0, rv0)]
 
     @pl.when(step == 0)
     def _():
@@ -210,22 +264,29 @@
         set_eye(eye_ref)
         set_pre(1, ln_in, w_proj, b_proj, ln_ref, w_t_ref, bias_ref)
         set_post(0, ln_mid, w_out, b_out, mln_ref, wo_t_ref, bo_ref)
-
-    @rows_loop
-    def _(r):
-        unit, inv = norm(x_ref[r].astype(F32))
-        munit_ref[r] = unit
-        minv_ref[0, pl.ds(r, 1), :] = inv
-        x_hat = (unit * mln_ref[0] + mln_ref[1]).astype(BF16)
-        update = dot(wo_t_ref[...], x_hat, 1, 0) + bo_ref[...]
-        g = g0_ref[r]
-        change = g * update
-        gu_ref[r] = change * (1.0 - g)
-        z_new = (dot(eye_ref[...], z_ref[r], 1, 1) + change).astype(BF16)
-        zm_ref[r] = z_new
-        pre_row(r, z_new.astype(F32), mask_ref, ln_ref, w_t_ref, bias_ref, g_ref, keep_ref, unit_ref, inv_ref, a_st, b_st)
-
-    send_rows(step, [(a_st, a_send, a_ref, a_ss, rs.at[0]), (b_st, b_send, b_ref, b_ss, rs.at[1])])
+        channel_part(OUT_FWD, (a_in, b_in), jobs)
+
+    @pl.when(step > 0)
+    def _():
+        t = step - 1
+        arrive(t, jobs)
+        x_ref = la0.at[t]
+
+        @rows_loop
+        def _(r):
+            unit, inv = norm(x_ref[r].astype(F32))
+            munit_ref[r] = unit
+            minv_ref[0, pl.ds(r, 1), :] = inv
+            x_hat = (unit * mln_ref[0] + mln_ref[1]).astype(BF16)
+            update = dot(wo_t_ref[...], x_hat, 1, 0) + bo_ref[...]
+            g = g0_ref[r]
+            change = g * update
+            gu_ref[r] = change * (1.0 - g)
+            z_new = (dot(eye_ref[...], z_ref[r], 1, 1) + change).astype(BF16)
+            zm_ref[r] = z_new
+            pre_row(r, z_new.astype(F32), mask_ref, ln_ref, w_t_ref, bias_ref, g_ref, keep_ref, unit_ref, inv_ref, a_st, b_st)
+
+        send_rows(t, [(a_st, a_send, a_ref, a_ss, rs.at[0]), (b_st, b_send, b_ref, b_ss, rs.at[1])])
 
 
 def post_back_row(unit, inv, g, dz, mln_ref, wo_ref, acc_ref, x_hat=None):
@@ -247,9 +308,11 @@
     grad_ref[C + 8:C + 16, :] = jnp.zeros((8, C), F32)
 
 
-def turn_kernel(x_ref, zm_ref, g_ref, dz_ref, ln_mid, w_out, b_out,
-                dx_ref, z_out_ref, dpg_ref, grad_ref, d_st, d_send, eye_ref, mln_ref, wo_t_ref, bo_ref, acc_ref, d_ss, rs):
+def turn_kernel(a_in, b_in, zm_ref, g_ref, dz_ref, ln_mid, w_out, b_out,
+                dx_ref, z_out_ref, dpg_ref, grad_ref, d_st, d_send, eye_ref, mln_ref, wo_t_ref, bo_ref, acc_ref, d_ss, rs,
+               st0, se0, la0, ss0, rv0):
     step = pl.program_id(0)
+    jobs = [(st0, se0, la0, ss0, rv0)]
     wo_ref = w_out.at[1]
 
     @pl.when(step == 0)
@@ -258,23 +321,30 @@
         set_eye(eye_ref)
         set_post(1, ln_mid, w_out, b_out, mln_ref, wo_t_ref, bo_ref)
         acc_ref[...] = jnp.zeros_like(acc_ref)
-
-    @rows_loop
-    def _(r):
-        dz = dot(eye_ref[...], dz_ref[r], 1, 1)
-        g = g_ref[r]
-        unit, inv = norm(x_ref[r].astype(F32))
-        x_hat = (unit * mln_ref[0] + mln_ref[1]).astype(BF16)
-        change = g * (dot(wo_t_ref[...], x_hat, 1, 0) + bo_ref[...])
-        dpg_ref[r] = dz * change * (1.0 - g)
-        z_out_ref[r] = (zm_ref[r].astype(F32) + change).T.astype(BF16)
-        spread(d_st, post_back_row(unit, inv, g, dz, mln_ref, wo_ref, acc_ref, x_hat), r)
-
-    @pl.when(step == STEPS - 1)
-    def _():
-        put_post(grad_ref, acc_ref)
-
-    send_rows(step, [(d_st, d_send, dx_ref, d_ss, rs.at[0])])
+        channel_part(IN_FWD, (a_in, b_in), jobs)
+
+    @pl.when(step > 0)
+    def _():
+        t = step - 1
+        arrive(t, jobs)
+        x_ref = la0.at[t]
+
+        @rows_loop
+        def _(r):
+            dz = dot(eye_ref[...], dz_ref[r], 1, 1)
+            g = g_ref[r]
+            unit, inv = norm(x_ref[r].astype(F32))
+            x_hat = (unit * mln_ref[0] + mln_ref[1]).astype(BF16)
+            change = g * (dot(wo_t_ref[...], x_hat, 1, 0) + bo_ref[...])
+            dpg_ref[r] = dz * change * (1.0 - g)
+            z_out_ref[r] = (zm_ref[r].astype(F32) + change).T.astype(BF16)
+            spread(d_st, post_back_row(unit, inv, g, dz, mln_ref, wo_ref, acc_ref, x_hat), r)
+
+        @pl.when(t == STEPS - 1)
+        def _():
+            put_post(grad_ref, acc_ref)
+
+        send_rows(t, [(d_st, d_send, dx_ref, d_ss, rs.at[0])])
 
 
 def pre_back_row(unit, inv, keep, da, db, d_pg, ln_ref, w_ref, w_acc, b_acc, l_acc):
@@ -307,10 +377,12 @@
         set_column(ref.at[k], ln[block, k:k + 1, :])
 
 
-def back_kernel(da_ref, db_ref, dpg1_ref, keep_ref, unit_ref, inv_ref, dz_ref, munit_ref, minv_ref, g_ref, gu_ref, ln_in, w_proj, ln_mid, w_out,
+def back_kernel(a_in, b_in, dx_in, dpg1_ref, keep_ref, unit_ref, inv_ref, dz_ref, munit_ref, minv_ref, g_ref, gu_ref, ln_in, w_proj, ln_mid, w_out,
                 dx_ref, dzm_ref, dpg_ref, grad1_ref, grad0_ref, d_st, d_send,
-                eye_ref, ln_ref, mln_ref, w_acc, b_acc, l_acc, acc_ref, d_ss, rs):
+                eye_ref, ln_ref, mln_ref, w_acc, b_acc, l_acc, acc_ref, d_ss, rs,
+               st0, st1, se0, se1, la0, la1, ss0, ss1, rv0, rv1):
     step = pl.program_id(0)
+    jobs = [(st0, se0, la0, ss0, rv0), (st1, se1, la1, ss1, rv1)]
     w_ref, wo_ref = w_proj.at[1], w_out.at[0]
 
     @pl.when(step == 0)
@@ -321,113 +393,64 @@
         set_gains(mln_ref, ln_mid, 0)
         for ref in (w_acc, b_acc, l_acc, acc_ref):
             ref[...] = jnp.zeros_like(ref)
-
-    @rows_loop
-    def _(r):
-        at = pl.ds(r, 1)
-        dzn = pre_back_row(unit_ref[r], inv_ref[0, at, :], keep_ref.at[r], da_ref[r].astype(F32), db_ref[r].astype(F32), dpg1_ref[r],
-                           ln_ref, w_ref, w_acc, b_acc, l_acc)
-        dzm = (dot(eye_ref[...], dz_ref[r], 1, 1) + dzn).astype(BF16)
-        dzm_ref[r] = dzm
-        dzm = dzm.astype(F32)
-        dpg_ref[r] = dzm * gu_ref[r]
-        spread(d_st, post_back_row(munit_ref[r], minv_ref[0, at, :], g_ref[r], dzm, mln_ref, wo_ref, acc_ref), r)
-
-    @pl.when(step == STEPS - 1)
-    def _():
-        put_pre(grad1_ref, w_acc, b_acc, l_acc)
-        put_post(grad0_ref, acc_ref)
-
-    send_rows(step, [(d_st, d_send, dx_ref, d_ss, rs.at[0])])
-
-
-def last_kernel(da_ref, db_ref, dpg_ref, keep_ref, unit_ref, inv_ref, dzm_ref, ln_in, w_proj,
-                dz_ref, grad_ref, ln_ref, w_acc, b_acc, l_acc):
+        channel_part(IN_BWD, (a_in, b_in, dx_in), jobs)
+
+    @pl.when(step > 0)
+    def _():
+        t = step - 1
+        arrive(t, jobs)
+        da_ref, db_ref = la0.at[t], la1.at[t]
+
+        @rows_loop
+        def _(r):
+            at = pl.ds(r, 1)
+            dzn = pre_back_row(unit_ref[r], inv_ref[0, at, :], keep_ref.at[r], da_ref[r].astype(F32), db_ref[r].astype(F32), dpg1_ref[r],
+                               ln_ref, w_ref, w_acc, b_acc, l_acc)
+            dzm = (dot(eye_ref[...], dz_ref[r], 1, 1) + dzn).astype(BF16)
+            dzm_ref[r] = dzm
+            dzm = dzm.astype(F32)
+            dpg_ref[r] = dzm * gu_ref[r]
+            spread(d_st, post_back_row(munit_ref[r], minv_ref[0, at, :], g_ref[r], dzm, mln_ref, wo_ref, acc_ref), r)
+
+        @pl.when(t == STEPS - 1)
+        def _():
+            put_pre(grad1_ref, w_acc, b_acc, l_acc)
+            put_post(grad0_ref, acc_ref)
+
+        send_rows(t, [(d_st, d_send, dx_ref, d_ss, rs.at[0])])
+
+
+def last_kernel(a_in, b_in, dx_in, dpg_ref, keep_ref, unit_ref, inv_ref, dzm_ref, ln_in, w_proj,
+                dz_ref, grad_ref, ln_ref, w_acc, b_acc, l_acc,
+               st0, st1, se0, se1, la0, la1, ss0, ss1, rv0, rv1):
     step = pl.program_id(0)
+    jobs = [(st0, se0, la0, ss0, rv0), (st1, se1, la1, ss1, rv1)]
     w_ref = w_proj.at[0]
 
     @pl.when(step == 0)
     def _():
+        enter()
         set_gains(ln_ref, ln_in, 0)
         for ref in (w_acc, b_acc, l_acc):
             ref[...] = jnp.zeros_like(ref)
-
-    @rows_loop
-    def _(r):
-        dzn = pre_back_row(unit_ref[r], inv_ref[0, pl.ds(r, 1), :], keep_ref.at[r], da_ref[r].astype(F32), db_ref[r].astype(F32), dpg_ref[r],
-                           ln_ref, w_ref, w_acc, b_acc, l_acc)
-        dz_ref[r] = (dzm_ref[r].astype(F32) + dzn).T.astype(BF16)
-
-    @pl.when(step == STEPS - 1)
-    def _():
-        put_pre(grad_ref, w_acc, b_acc, l_acc)
-
-
-HALF = N // 2
-
-
-def spread_channel(stage, value, c):
-    for h in range(2):
-        stage[pl.ds((h * 2 + c // 8) * HALF * 8 + c % 8, HALF, stride=8), :] = value[:, h * C:(h + 1) * C]
-
-
-def pack_channels(stage, send_ref, slot):
-    for h in range(2):
-        for q in range(4):
-            lo = stage[pl.ds((h * 2) * HALF * 8 + q * 256, 256), :].reshape(32, 8, C)
-            hi = stage[pl.ds((h * 2 + 1) * HALF * 8 + q * 256, 256), :].reshape(32, 8, C)
-            send_ref[slot, q * 32:(q + 1) * 32, :, h * C:(h + 1) * C] = jnp.concatenate([lo, hi], axis=1).astype(BF16)
-
-
-def channel_copies(send_ref, out_ref, send_sem, recv_sem, slot, top):
-    me, cy, cx, core = place()
-    out = []
-    k = 0
-    for dx in (1, 0):
-        for dc in (1, 0):
-            within = ((cx + dx) % 2) * 2 + (core + dc) % 2
-            out.append(move(send_ref.at[slot, pl.ds(pl.multiple_of(within * ROWS, ROWS), ROWS)],
-                            out_ref.at[:, pl.ds(pl.multiple_of(me * CH, CH), CH), :],
-                            send_sem.at[slot, k], recv_sem, top * 4 + within, slot == 1 and k == 3))
-            k += 1
-    return out
-
-
-def channel_kernel(products, n_in, n_out, *refs):
-    ins, outs = refs[:n_in], refs[n_in:n_in + n_out]
-    stages = refs[n_in + n_out:n_in + 2 * n_out]
-    sends = refs[n_in + 2 * n_out:n_in + 3 * n_out]
-    sems = refs[n_in + 3 * n_out:n_in + 4 * n_out]
-    rs = refs[-1]
-    step = pl.program_id(0)
-    pl.when(step == 0)(enter)
-    _, cy, _, _ = place()
-    top = (cy + 1 + step) % 2
-    rows = pl.ds(pl.multiple_of(top * HALF, HALF), HALF)
-    for j in range(n_out):
-        for c in range(CH):
-            spread_channel(stages[j], products[j](ins, c, rows), c)
-        for slot in range(2):
-            @pl.when(step == slot)
-            def _():
-                pack_channels(stages[j], sends[j], slot)
-                if slot == 0 and j == 0:
-                    all_in()
-                for copy in channel_copies(sends[j], outs[j], sems[j], rs.at[j], slot, top):
-                    copy.start()
-
-    @pl.when(step == 1)
-    def _():
-        for j in range(n_out):
-            for slot in range(2):
-                wait_sends(channel_copies(sends[j], outs[j], sems[j], rs.at[j], slot, (cy + 1 + slot) % 2))
-            pltpu.make_async_copy(outs[j], outs[j], rs.at[j]).wait()
-
-
-OUT_FWD = (lambda r, c, rows: dot(r[0][c, rows, :], r[1][c], 1, 1),)
-IN_FWD = (lambda r, c, rows: dot(r[0][c, :, rows], r[1][c], 0, 0),)
-IN_BWD = (lambda r, c, rows: dot(r[1][c, rows, :], r[2][c], 1, 1), lambda r, c, rows: dot(r[0][c, rows, :], r[2][c], 1, 0))
-OUT_BWD = (lambda r, c, rows: dot(r[2][c, rows, :], r[1][c], 1, 0), lambda r, c, rows: dot(r[2][c, :, rows], r[0][c], 0, 0))
+        channel_part(OUT_BWD, (a_in, b_in, dx_in), jobs)
+
+    @pl.when(step > 0)
+    def _():
+        t = step - 1
+        arrive(t, jobs)
+        da_ref, db_ref = la0.at[t], la1.at[t]
+
+        @rows_loop
+        def _(r):
+            dzn = pre_back_row(unit_ref[r], inv_ref[0, pl.ds(r, 1), :], keep_ref.at[r], da_ref[r].astype(F32), db_ref[r].astype(F32), dpg_ref[r],
+                               ln_ref, w_ref, w_acc, b_acc, l_acc)
+            dz_ref[r] = (dzm_ref[r].astype(F32) + dzn).T.astype(BF16)
+
+        @pl.when(t == STEPS - 1)
+        def _():
+            put_pre(grad_ref, w_acc, b_acc, l_acc)
+
 
 ALL = 16
 SHARE = 112
@@ -502,7 +525,7 @@
         out_specs=vmem,
         out_shape=jax.ShapeDtypeStruct((ALL * SHARE, C), F32),
         scratch_shapes=[pltpu.VMEM((ALL * SHARE, C), BF16), pltpu.VMEM((ALL, SHARE, C), BF16), pltpu.VMEM((SHARE, C), F32), dma, dma, dma, dma],
-        compiler_params=pltpu.CompilerParams(vmem_limit_bytes=VMEM_LIMIT, collective_id=8, has_side_effects=True),
+        compiler_params=pltpu.CompilerParams(vmem_limit_bytes=VMEM_LIMIT, collective_id=5, has_side_effects=True),
         name="sum",
     )(*packs)
     shapes = ((2, 2, C), (2, C, 5 * C), (2, 5 * C), (2, 2, C), (2, C, C), (2, C))
@@ -515,7 +538,6 @@
     )(total)
 
 
-ANY = pl.BlockSpec(memory_space=pl.ANY)
 TRI = jax.ShapeDtypeStruct((CH, N, N), BF16)
 ROW = jax.ShapeDtypeStruct((ROWS, C, N), BF16)
 ROW32 = jax.ShapeDtypeStruct((ROWS, C, N), F32)
@@ -526,49 +548,42 @@
 INV = jax.ShapeDtypeStruct((STEPS, STEP, N), F32)
 
 
-def by_row(array):
+def by_row(array, lead=0):
     tail = array.shape[1:]
-    return pl.BlockSpec((array.shape[0] // STEPS,) + tail, lambda t: (t,) + (0,) * len(tail))
+    return pl.BlockSpec((array.shape[0] // STEPS,) + tail, lambda s: ((s * STEPS) // (STEPS + lead),) + (0,) * len(tail))
 
 
 def whole(array):
     zeros = (0,) * len(array.shape)
-    return pl.BlockSpec(array.shape, lambda t: zeros)
-
-
-def params(collective_id):
-    if collective_id is None:
-        return pltpu.CompilerParams(dimension_semantics=("arbitrary",), vmem_limit_bytes=VMEM_LIMIT)
-    return pltpu.CompilerParams(dimension_semantics=("arbitrary",), vmem_limit_bytes=VMEM_LIMIT, collective_id=collective_id, has_side_effects=True)
-
-
-def row_call(kernel, name, collective_id, ins, consts, outs, specs, n_send, scratch):
+    return pl.BlockSpec(array.shape, lambda t: zeros, pipeline_mode=pl.Buffered(1))
+
+
+def out_spec(array, lead):
+    if array is TRI:
+        return pl.BlockSpec(memory_space=pl.ANY)
+    if array in (PRE, POST):
+        return pl.BlockSpec(array.shape, lambda t: (0, 0))
+    return by_row(array, lead)
+
+
+def row_call(kernel, name, collective_id, tris, ins, consts, outs, n_back, scratch):
+    lead = 1 if tris else 0
+    n_send = sum(out is TRI for out in outs)
+    dma = pltpu.SemaphoreType.DMA
     sent = [pltpu.VMEM((2 * C * STEP, C), F32)] * n_send + [pltpu.VMEM((STEPS, C, STEP, N), BF16)] * n_send
-    sems = [pltpu.SemaphoreType.DMA((STEPS, GROUP))] * n_send + ([pltpu.SemaphoreType.DMA((n_send,))] if n_send else [])
+    sems = [dma((STEPS, GROUP))] * n_send + ([dma((n_send,))] if n_send else [])
+    back = [pltpu.VMEM((4 * N * 8, C), F32)] * n_back + [pltpu.VMEM((STEPS, GROUP, STEP, CH, N), BF16)] * n_back
+    back += [pltpu.VMEM((STEPS, STEP, C, N), BF16)] * n_back + [dma((STEPS, GROUP))] * (2 * n_back)
     return pl.pallas_call(
         kernel,
-        grid=(STEPS,),
-        in_specs=[by_row(x) for x in ins] + [whole(x) for x in consts],
-        out_specs=specs,
+        grid=(STEPS + lead,),
+        in_specs=[whole(x) for x in tris] + [by_row(x, lead) for x in ins] + [whole(x) for x in consts],
+        out_specs=[out_spec(out, lead) for out in outs],
         out_shape=outs,
-        scratch_shapes=sent + scratch + sems,
-        compiler_params=params(collective_id),
+        scratch_shapes=sent + scratch + sems + back,
+        compiler_params=pltpu.CompilerParams(dimension_semantics=("arbitrary",), vmem_limit_bytes=VMEM_LIMIT, collective_id=collective_id, has_side_effects=True),
         name=name,
-    )(*ins, *consts)
-
-
-def channel_call(products, name, collective_id, ins, n_out):
-    return pl.pallas_call(
-        functools.partial(channel_kernel, products, len(ins), n_out),
-        grid=(2,),
-        in_specs=[whole(x) for x in ins],
-        out_specs=[ANY] * n_out,
-        out_shape=[ROW] * n_out,
-        scratch_shapes=[pltpu.VMEM((4 * HALF * 8, C), F32)] * n_out + [pltpu.VMEM((2, HALF, CH, N), BF16)] * n_out
-        + [pltpu.SemaphoreType.DMA((2, 4))] * n_out + [pltpu.SemaphoreType.DMA((n_out,))],
-        compiler_params=params(collective_id),
-        name=name,
-    )(*ins)
+    )(*tris, *ins, *consts)
 
 
 def local_step(z_pair, pair_mask, dz_out, ln_in, w_proj, b_proj, ln_mid, w_out, b_out):
@@ -581,24 +596,18 @@
     post_acc = [pltpu.VMEM((4, C, C), F32)]
     pre_acc = [pltpu.VMEM((5 * C, C), F32), pltpu.VMEM((5 * C, C), F32), pltpu.VMEM((2, C, C), F32)]
 
-    kept = [by_row(ROW32), by_row(KEEP), by_row(ROW32), by_row(INV)]
-    a0, b0, g0, keep0, unit0, inv0 = row_call(pre_kernel, "pre0", 0, [z, mask], pre, [TRI, TRI, ROW32, KEEP, ROW32, INV],
-                                              [ANY, ANY, *kept], 2, eye + pre_c)
-    x0, = channel_call(OUT_FWD, "tri0", 1, [a0, b0], 1)
+    gains = [pltpu.VMEM((2, C, N), F32)]
+    kept = [TRI, TRI, ROW32, KEEP, ROW32, INV]
+    a0, b0, g0, keep0, unit0, inv0 = row_call(pre_kernel, "pre0", 0, [], [z, mask], pre, kept, 0, eye + pre_c)
     a1, b1, g1, keep1, unit1, inv1, zm, gu0, munit0, minv0 = row_call(
-        mid_kernel, "mid", 2, [x0, z, g0, mask], post + pre, [TRI, TRI, ROW32, KEEP, ROW32, INV, ROW, ROW32, ROW32, INV],
-        [ANY, ANY, *kept, by_row(ROW), by_row(ROW32), by_row(ROW32), by_row(INV)], 2, eye + pre_c + post_c)
-    x1, = channel_call(IN_FWD, "tri1", 3, [a1, b1], 1)
-    dx1, z_new, dpg1, post_g1 = row_call(turn_kernel, "turn", 4, [x1, zm, g1, dz], post, [TRI, NATIVE, ROW32, POST],
-                                         [ANY, by_row(NATIVE), by_row(ROW32), whole(POST)], 1, eye + post_c + post_acc)
-    da1, db1 = channel_call(IN_BWD, "trib1", 5, [a1, b1, dx1], 2)
-    gains = [pltpu.VMEM((2, C, N), F32)]
+        mid_kernel, "mid", 1, [a0, b0], [z, g0, mask], post + pre, kept + [ROW, ROW32, ROW32, INV], 1, eye + pre_c + post_c)
+    dx1, z_new, dpg1, post_g1 = row_call(
+        turn_kernel, "turn", 2, [a1, b1], [zm, g1, dz], post, [TRI, NATIVE, ROW32, POST], 1, eye + post_c + post_acc)
     dx0, dzm, dpg0, pre_g1, post_g0 = row_call(
-        back_kernel, "back", 6, [da1, db1, dpg1, keep1, unit1, inv1, dz, munit0, minv0, g0, gu0], [ln_in, w_proj, ln_mid, w_out],
-        [TRI, ROW, ROW32, PRE, POST], [ANY, by_row(ROW), by_row(ROW32), whole(PRE), whole(POST)], 1, eye + gains * 2 + pre_acc + post_acc)
-    da0, db0 = channel_call(OUT_BWD, "trib0", 7, [a0, b0, dx0], 2)
-    dz_new, pre_g0 = row_call(last_kernel, "last", None, [da0, db0, dpg0, keep0, unit0, inv0, dzm], [ln_in, w_proj], [NATIVE, PRE],
-                              [by_row(NATIVE), whole(PRE)], 0, gains + pre_acc)
+        back_kernel, "back", 3, [a1, b1, dx1], [dpg1, keep1, unit1, inv1, dz, munit0, minv0, g0, gu0], [ln_in, w_proj, ln_mid, w_out],
+        [TRI, ROW, ROW32, PRE, POST], 2, eye + gains * 2 + pre_acc + post_acc)
+    dz_new, pre_g0 = row_call(
+        last_kernel, "last", 4, [a0, b0, dx0], [dpg0, keep0, unit0, inv0, dzm], [ln_in, w_proj], [NATIVE, PRE], 2, gains + pre_acc)
     return (z_new[None], dz_new[None], *sum_grads([post_g0, post_g1, pre_g0, pre_g1]))
 
 

time: 385 us -> 363 us (0.943)
  Pallas kernels: 381 us -> 357 us
    pallas_call x9 -> x5, Pallas kernels: 353 us -> 329 us  [row_call(): pl.pallas_call(kernel, grid=(STEPS + lead,), in_specs=[whole(x) for x in...]
where the time goes in v4:
time: 363 us; the launch traced here: 362 us
  Pallas kernels  357 us (98%)
  local copies, waits for them, and re-layouts  4.61 us (1%)
    pallas_call x5, Pallas kernels, row_call(): pl.pallas_call(kernel, grid=(STEPS + lead,), in_specs=[whole(x) for x in...  329 us
    pallas_call x1, Pallas kernels, sum_grads(): pl.pallas_call(sum_kernel, in_specs=[vmem] * 4, out_specs=vmem, out_shape...  25.8 us

profile of v4, /device:TPU:0, one launch (start us, length us, event | category | flops | bytes accessed | tf_op | source)
XLA Modules:
  0.0 362.4 jit_solution(9714993226270135620)
XLA Ops:
  0.6 55.9 %pre0.1 = (bf16[16,256,256]{2,1,0:T(8,128)(2,1)}, bf16[16,256,256]{2,1,0:T(8,128)(2,1)}, f32[32,128,256]{2,1,0:T(8,128)}, f32[32,4,128,256]{3,2,1,0:T(8,128)}, f...) custom-call(bf16[32,256,128]{2,1,0:T(8,128)(2,1)} %bitcast.7, s32[4,8,256]{2,1,0:T(8,128)} %bitcast.11, ...), custom_call_target="tpu_custom_call" | custom-call | tf_op jit(solution)/shard_map/pre0/pallas_call | solution.py:577
  56.6 79.3 %mid.1 = (bf16[16,256,256]{2,1,0:T(8,128)(2,1)}, bf16[16,256,256]{2,1,0:T(8,128)(2,1)}, f32[32,128,256]{2,1,0:T(8,128)}, f32[32,4,128,256]{3,2,1,0:T(8,128)}, f3...) custom-call(bf16[16,256,256]{2,1,0:T(8,128)(2,1)} %get-tuple-element, ...), custom_call_target="tpu_custom_call" | custom-call | tf_op jit(solution)/shard_map/mid/pallas_call | solution.py:577
  135.9 53.1 %turn.1 = (bf16[16,256,256]{2,1,0:T(8,128)(2,1)}, bf16[32,256,128]{2,1,0:T(8,128)(2,1)}, f32[32,128,256]{2,1,0:T(8,128)}, f32[144,128]{1,0:T(8,128)}) custom-call(bf16[16,256,256]{2,1,0:T(8,128)(2,1)} %get-tuple-element.44.a_in, bf16[16,256,256]{2,1,0:T(8,128)(2,1)} %get-tuple-element.45.b_in, bf16[32,128,256]{2,1,0:T(8,128)(2,1)} %get-tuple-element.46.zm_ref, ...), custom_call_target="tpu_custom_call" | custom-call | tf_op jit(solution)/shard_map/turn/pallas_call | solution.py:577
  189.0 82.2 %back.1 = (bf16[16,256,256]{2,1,0:T(8,128)(2,1)}, bf16[32,128,256]{2,1,0:T(8,128)(2,1)}, f32[32,128,256]{2,1,0:T(8,128)}, f32[656,128]{1,0:T(8,128)}, f32[144,128]{1,0:T(8,128)}) custom-call(bf16[16,256,256]{2,1,0:T(8,128)(2,1)} %get-tuple-element.44.a_in, bf16[16,256,256]{2,1,0:T(8,128)(2,1)} %get-tuple-element.45.b_in, ...), custom_call_target="tpu_custom_call" | custom-call | tf_op jit(solution)/shard_map/back/pallas_call | solution.py:577
  271.2 58.5 %last.1 = (bf16[32,256,128]{2,1,0:T(8,128)(2,1)}, f32[656,128]{1,0:T(8,128)}) custom-call(bf16[16,256,256]{2,1,0:T(8,128)(2,1)} %get-tuple-element.41.a_in, bf16[16,256,256]{2,1,0:T(8,128)(2,1)} %get-tuple-element.42.b_in, bf16[16,256,256]{2,1,0:T(8,128)(2,1)} %get-tuple-element.57.dx_in, f32[32,128,256]{2,1,0:T(8,128)} %get-tuple-element.58.dpg_ref, ...), custom_call_target="tpu_custom_call" | custom-call | tf_op jit(solution)/shard_map/last/pallas_call | solution.py:577
  329.7 25.8 %sum.1.tot = f32[1792,128]{1,0:T(8,128)} custom-call(f32[144,128]{1,0:T(8,128)} %get-tuple-element.64.p0, f32[144,128]{1,0:T(8,128)} %get-tuple-element.65.p1, f32[656,128]{1,0:T(8,128)} %get-tuple-element.66.p2, f32[656,128]{1,0:T(8,128)} %get-tuple-element.67.p3), custom_call_target="tpu_custom_call" | custom-call | tf_op jit(solution)/shard_map/sum/pallas_call | solution.py:522
  355.5 2.3 split.1
  357.8 0.0 copy-start
  357.8 3.3 copy.19
  361.0 0.0 copy-done
  361.0 1.3 copy.20
Async XLA Ops:
  357.8 3.3 copy-start

commit v5 on v4

--- a/solution.py
+++ b/solution.py
@@ -170,20 +170,38 @@
         device_id={"dap": dest}, device_id_type=pl.DeviceIdType.MESH)
 
 
+GROUPS = 4
+
+
+class Piecewise:
+    def __init__(self, source, ref, sems):
+        self.source, self.ref, self.sems = source, ref, sems
+
+    def load(self, g):
+        part = pl.ds(g * (CH // GROUPS), CH // GROUPS)
+        return pltpu.make_async_copy(self.source.at[part], self.ref.at[part], self.sems.at[g])
+
+
 def channel_part(products, ins, jobs):
-    for product, job in zip(products, jobs):
+    me, dests = peers()
+    refs = [x.ref for x in ins]
+    for j, (product, job) in enumerate(zip(products, jobs)):
+        stage, send_ref, land_ref = job[:3]
+
         def body(c, carry):
-            value = product(ins, c)
+            value = product(refs, c)
             for h in range(2):
-                job[0][pl.ds((h * 2 + c // 8) * N * 8 + c % 8, N, stride=8), :] = value[:, h * C:(h + 1) * C]
+                stage[pl.ds((h * 2 + c // 8) * N * 8 + c % 8, N, stride=8), :] = value[:, h * C:(h + 1) * C]
             return carry
 
-        lax.fori_loop(0, CH, body, 0, unroll=4)
-    all_in()
-    me, dests = peers()
-    for t in range(STEPS):
-        for job in jobs:
-            stage, send_ref, land_ref = job[:3]
+        for g in range(GROUPS):
+            if j == 0:
+                for x in ins:
+                    x.load(g).wait()
+            lax.fori_loop(g * (CH // GROUPS), (g + 1) * (CH // GROUPS), body, 0, unroll=True)
+        if j == 0:
+            all_in()
+        for t in range(STEPS):
             for dest in range(GROUP):
                 for h in range(2):
                     at = h * 2 * N * 8 + (dest * ROWS + t * STEP) * 8
@@ -193,6 +211,43 @@
             for k, dest in enumerate(dests[:-1]):
                 back_copy(job, t, k, dest, me).start()
             land_ref[t, :, pl.ds(pl.multiple_of(me * CH, CH), CH), :] = send_ref[t, me]
+
+
+def staged_kernel(inner, n_tri, n_in, *refs):
+    far, refs = refs[:n_tri + n_in], refs[n_tri + n_in:]
+    near, refs = refs[-2 - n_tri - n_in:-2], refs[:-2 - n_tri - n_in] + refs[-2:]
+    refs, (tri_sem, row_sem) = refs[:-2], refs[-2:]
+    step = pl.program_id(0)
+    tris = [Piecewise(far[k], near[k], tri_sem.at[k]) for k in range(n_tri)]
+
+    def fetch(t, slot):
+        out = []
+        for k in range(n_in):
+            size = far[n_tri + k].shape[0] // STEPS
+            out.append(pltpu.make_async_copy(far[n_tri + k].at[pl.ds(t * size, size)], near[n_tri + k].at[slot], row_sem.at[slot, k]))
+        return out
+
+    @pl.when(step == 0)
+    def _():
+        for g in range(GROUPS):
+            for x in tris:
+                x.load(g).start()
+        for copy in fetch(0, 0):
+            copy.start()
+
+    slot = (step + 1) % 2
+
+    @pl.when(step > 0)
+    def _():
+        for copy in fetch(step - 1, slot):
+            copy.wait()
+
+    @pl.when((step > 0) & (step < STEPS))
+    def _():
+        for copy in fetch(step, 1 - slot):
+            copy.start()
+
+    inner(*tris, *[ref.at[slot] for ref in near[n_tri:]], *refs)
 
 
 def arrive(t, jobs):
@@ -337,7 +392,7 @@
             x_hat = (unit * mln_ref[0] + mln_ref[1]).astype(BF16)
             change = g * (dot(wo_t_ref[...], x_hat, 1, 0) + bo_ref[...])
             dpg_ref[r] = dz * change * (1.0 - g)
-            z_out_ref[r] = (zm_ref[r].astype(F32) + change).T.astype(BF16)
+            z_out_ref[r] = (zm_ref[r].astype(F32) + change).astype(BF16)
             spread(d_st, post_back_row(unit, inv, g, dz, mln_ref, wo_ref, acc_ref, x_hat), r)
 
         @pl.when(t == STEPS - 1)
@@ -445,7 +500,7 @@
         def _(r):
             dzn = pre_back_row(unit_ref[r], inv_ref[0, pl.ds(r, 1), :], keep_ref.at[r], da_ref[r].astype(F32), db_ref[r].astype(F32), dpg_ref[r],
                                ln_ref, w_ref, w_acc, b_acc, l_acc)
-            dz_ref[r] = (dzm_ref[r].astype(F32) + dzn).T.astype(BF16)
+            dz_ref[r] = (dzm_ref[r].astype(F32) + dzn).astype(BF16)
 
         @pl.when(t == STEPS - 1)
         def _():
@@ -501,7 +556,14 @@
         second(to, k, me).wait_send()
 
 
-def split_kernel(tot, d_ln_in, d_w_proj, d_b_proj, d_ln_mid, d_w_out, d_b_out):
+def split_kernel(z_t, dz_t, tot, z_out, dz_out, *grads):
+    for r in range(STEP):
+        z_out[r] = z_t[r].astype(F32).T.astype(BF16)
+        dz_out[r] = dz_t[r].astype(F32).T.astype(BF16)
+    pl.when(pl.program_id(0) == 0)(lambda: split_grads(tot, *grads))
+
+
+def split_grads(tot, d_ln_in, d_w_proj, d_b_proj, d_ln_mid, d_w_out, d_b_out):
     at = 0
     for k in range(2):
         d_w_out[k] = tot[at:at + C, :]
@@ -516,7 +578,7 @@
         at += 5 * C + 16
 
 
-def sum_grads(packs):
+def finish(z_t, dz_t, packs):
     vmem = pl.BlockSpec(memory_space=pltpu.VMEM)
     dma = pltpu.SemaphoreType.DMA((ALL,))
     total = pl.pallas_call(
@@ -529,13 +591,16 @@
         name="sum",
     )(*packs)
     shapes = ((2, 2, C), (2, C, 5 * C), (2, 5 * C), (2, 2, C), (2, C, C), (2, C))
+    grads = [jax.ShapeDtypeStruct(shape, F32) for shape in shapes]
     return pl.pallas_call(
         split_kernel,
-        in_specs=[vmem],
-        out_specs=[vmem] * 6,
-        out_shape=[jax.ShapeDtypeStruct(shape, F32) for shape in shapes],
+        grid=(STEPS,),
+        in_specs=[by_row(z_t), by_row(dz_t), whole(total)],
+        out_specs=[by_row(NATIVE)] * 2 + [pl.BlockSpec(x.shape, lambda t, n=len(x.shape): (0,) * n) for x in grads],
+        out_shape=[NATIVE] * 2 + grads,
+        compiler_params=pltpu.CompilerParams(dimension_semantics=("arbitrary",)),
         name="split",
-    )(total)
+    )(z_t, dz_t, total)
 
 
 TRI = jax.ShapeDtypeStruct((CH, N, N), BF16)
@@ -574,13 +639,19 @@
     sems = [dma((STEPS, GROUP))] * n_send + ([dma((n_send,))] if n_send else [])
     back = [pltpu.VMEM((4 * N * 8, C), F32)] * n_back + [pltpu.VMEM((STEPS, GROUP, STEP, CH, N), BF16)] * n_back
     back += [pltpu.VMEM((STEPS, STEP, C, N), BF16)] * n_back + [dma((STEPS, GROUP))] * (2 * n_back)
+    far = pl.BlockSpec(memory_space=pl.ANY)
+    near = []
+    if tris:
+        near = [pltpu.VMEM(x.shape, x.dtype) for x in tris] + [pltpu.VMEM((2, x.shape[0] // STEPS) + x.shape[1:], x.dtype) for x in ins]
+        near += [dma((len(tris), GROUPS)), dma((2, len(ins)))]
+        kernel = functools.partial(staged_kernel, kernel, len(tris), len(ins))
     return pl.pallas_call(
         kernel,
         grid=(STEPS + lead,),
-        in_specs=[whole(x) for x in tris] + [by_row(x, lead) for x in ins] + [whole(x) for x in consts],
+        in_specs=[far if tris else by_row(x) for x in [*tris, *ins]] + [whole(x) for x in consts],
         out_specs=[out_spec(out, lead) for out in outs],
         out_shape=outs,
-        scratch_shapes=sent + scratch + sems + back,
+        scratch_shapes=sent + scratch + sems + back + near,
         compiler_params=pltpu.CompilerParams(dimension_semantics=("arbitrary",), vmem_limit_bytes=VMEM_LIMIT, collective_id=collective_id, has_side_effects=True),
         name=name,
     )(*tris, *ins, *consts)
@@ -602,13 +673,14 @@
     a1, b1, g1, keep1, unit1, inv1, zm, gu0, munit0, minv0 = row_call(
         mid_kernel, "mid", 1, [a0, b0], [z, g0, mask], post + pre, kept + [ROW, ROW32, ROW32, INV], 1, eye + pre_c + post_c)
     dx1, z_new, dpg1, post_g1 = row_call(
-        turn_kernel, "turn", 2, [a1, b1], [zm, g1, dz], post, [TRI, NATIVE, ROW32, POST], 1, eye + post_c + post_acc)
+        turn_kernel, "turn", 2, [a1, b1], [zm, g1, dz], post, [TRI, ROW, ROW32, POST], 1, eye + post_c + post_acc)
     dx0, dzm, dpg0, pre_g1, post_g0 = row_call(
         back_kernel, "back", 3, [a1, b1, dx1], [dpg1, keep1, unit1, inv1, dz, munit0, minv0, g0, gu0], [ln_in, w_proj, ln_mid, w_out],
         [TRI, ROW, ROW32, PRE, POST], 2, eye + gains * 2 + pre_acc + post_acc)
     dz_new, pre_g0 = row_call(
-        last_kernel, "last", 4, [a0, b0, dx0], [dpg0, keep0, unit0, inv0, dzm], [ln_in, w_proj], [NATIVE, PRE], 2, gains + pre_acc)
-    return (z_new[None], dz_new[None], *sum_grads([post_g0, post_g1, pre_g0, pre_g1]))
+        last_kernel, "last", 4, [a0, b0, dx0], [dpg0, keep0, unit0, inv0, dzm], [ln_in, w_proj], [ROW, PRE], 2, gains + pre_acc)
+    z_out, dz_pair, *grads = finish(z_new, dz_new, [post_g0, post_g1, pre_g0, pre_g1])
+    return z_out[None], dz_pair[None], *grads
 
 
 def solution(mesh):

time: 363 us -> 355 us (0.978)
  local copies, waits for them, and re-layouts: 4.61 us -> 0 us
    unnamed x4 -> x0, local copies, waits for them, and re-layouts: 4.61 us -> none
where the time goes in v5:
time: 355 us; the launch traced here: 354 us
  Pallas kernels  354 us (100%)
    pallas_call x5, Pallas kernels, row_call(): pl.pallas_call(kernel, grid=(STEPS + lead,), in_specs=[far if tris else b...  321 us
    pallas_call x1, Pallas kernels, finish(): pl.pallas_call(sum_kernel, in_specs=[vmem] * 4, out_specs=vmem, out_shape...  26.1 us

profile of v5, /device:TPU:0, one launch (start us, length us, event | category | flops | bytes accessed | tf_op | source)
XLA Modules:
  0.0 354.4 jit_solution(15951051384860889549)
XLA Ops:
  0.6 56.0 %pre0.1 = (bf16[16,256,256]{2,1,0:T(8,128)(2,1)}, bf16[16,256,256]{2,1,0:T(8,128)(2,1)}, f32[32,128,256]{2,1,0:T(8,128)}, f32[32,4,128,256]{3,2,1,0:T(8,128)}, f...) custom-call(bf16[32,256,128]{2,1,0:T(8,128)(2,1)} %bitcast.7, s32[4,8,256]{2,1,0:T(8,128)} %bitcast.9, ...), custom_call_target="tpu_custom_call" | custom-call | tf_op jit(solution)/shard_map/pre0/pallas_call | solution.py:648
  56.6 78.2 %mid.1 = (bf16[16,256,256]{2,1,0:T(8,128)(2,1)}, bf16[16,256,256]{2,1,0:T(8,128)(2,1)}, f32[32,128,256]{2,1,0:T(8,128)}, f32[32,4,128,256]{3,2,1,0:T(8,128)}, f3...) custom-call(bf16[16,256,256]{2,1,0:T(8,128)(2,1)} %get-tuple-element, ...), custom_call_target="tpu_custom_call" | custom-call | tf_op jit(solution)/shard_map/mid/pallas_call | solution.py:648
  134.8 52.2 %turn.1 = (bf16[16,256,256]{2,1,0:T(8,128)(2,1)}, bf16[32,128,256]{2,1,0:T(8,128)(2,1)}, f32[32,128,256]{2,1,0:T(8,128)}, f32[144,128]{1,0:T(8,128)}) custom-call(bf16[16,256,256]{2,1,0:T(8,128)(2,1)} %get-tuple-element.46.refs_0_, bf16[16,256,256]{2,1,0:T(8,128)(2,1)} %get-tuple-element.47.refs_1_, bf16[32,128,256]{2,1,0:T(8,128)(2,1)} %get-tuple-element.48.refs_2_, ...), custom_call_target="tpu_custom_call" | custom-call | tf_op jit(solution)/shard_map/turn/pallas_call | solution.py:648
  187.0 79.1 %back.1 = (bf16[16,256,256]{2,1,0:T(8,128)(2,1)}, bf16[32,128,256]{2,1,0:T(8,128)(2,1)}, f32[32,128,256]{2,1,0:T(8,128)}, f32[656,128]{1,0:T(8,128)}, f32[144,128]{1,0:T(8,128)}) custom-call(bf16[16,256,256]{2,1,0:T(8,128)(2,1)} %get-tuple-element.46.refs_0_, bf16[16,256,256]{2,1,0:T(8,128)(2,1)} %get-tuple-element.47.refs_1_, ...), custom_call_target="tpu_custom_call" | custom-call | tf_op jit(solution)/shard_map/back/pallas_call | solution.py:648
  266.1 56.0 %last.1 = (bf16[32,128,256]{2,1,0:T(8,128)(2,1)}, f32[656,128]{1,0:T(8,128)}) custom-call(bf16[16,256,256]{2,1,0:T(8,128)(2,1)} %get-tuple-element.43.refs_0_, bf16[16,256,256]{2,1,0:T(8,128)(2,1)} %get-tuple-element.44.refs_1_, bf16[16,256,256]{2,1,0:T(8,128)(2,1)} %get-tuple-element.59.refs_2_, f32[32,128,256]{2,1,0:T(8,128)} %get-tuple-element.60.refs_3_, ...), custom_call_target="tpu_custom_call" | custom-call | tf_op jit(solution)/shard_map/last/pallas_call | solution.py:648
  322.1 26.1 %sum.1.tot = f32[1792,128]{1,0:T(8,128)} custom-call(f32[144,128]{1,0:T(8,128)} %get-tuple-element.66.p0, f32[144,128]{1,0:T(8,128)} %get-tuple-element.67.p1, f32[656,128]{1,0:T(8,128)} %get-tuple-element.68.p2, f32[656,128]{1,0:T(8,128)} %get-tuple-element.69.p3), custom_call_target="tpu_custom_call" | custom-call | tf_op jit(solution)/shard_map/sum/pallas_call | solution.py:584
  348.2 6.0 %split.1 = (bf16[32,256,128]{2,1,0:T(8,128)(2,1)}, bf16[32,256,128]{2,1,0:T(8,128)(2,1)}, f32[2,2,128]{2,1,0:T(2,128)}, f32[2,128,640]{2,1,0:T(8,128)}, f32[2,64...) custom-call(bf16[32,128,256]{2,1,0:T(8,128)(2,1)} %get-tuple-element.50.z_t, ...), custom_call_target="tpu_custom_call" | custom-call | tf_op jit(solution)/shard_map/split/pallas_call | solution.py:595

commit v6 on v5

--- a/solution.py
+++ b/solution.py
@@ -392,7 +392,7 @@
             x_hat = (unit * mln_ref[0] + mln_ref[1]).astype(BF16)
             change = g * (dot(wo_t_ref[...], x_hat, 1, 0) + bo_ref[...])
             dpg_ref[r] = dz * change * (1.0 - g)
-            z_out_ref[r] = (zm_ref[r].astype(F32) + change).astype(BF16)
+            z_out_ref[r] = (zm_ref[r].astype(F32) + change).T.astype(BF16)
             spread(d_st, post_back_row(unit, inv, g, dz, mln_ref, wo_ref, acc_ref, x_hat), r)
 
         @pl.when(t == STEPS - 1)
@@ -500,7 +500,7 @@
         def _(r):
             dzn = pre_back_row(unit_ref[r], inv_ref[0, pl.ds(r, 1), :], keep_ref.at[r], da_ref[r].astype(F32), db_ref[r].astype(F32), dpg_ref[r],
                                ln_ref, w_ref, w_acc, b_acc, l_acc)
-            dz_ref[r] = (dzm_ref[r].astype(F32) + dzn).astype(BF16)
+            dz_ref[r] = (dzm_ref[r].astype(F32) + dzn).T.astype(BF16)
 
         @pl.when(t == STEPS - 1)
         def _():
@@ -516,14 +516,23 @@
     return pl.ds(pl.multiple_of(k * SHARE, SHARE), SHARE)
 
 
-def sum_kernel(p0, p1, p2, p3, tot_ref, send_ref, got_ref, part_ref, ss, rs, ss2, rs2):
+def sum_kernel(p0, p1, p2, p3, tot_ref, send_ref, got_ref, part_ref, ss, rs, ss2, rs2, ss3, rs3):
     dp, dap = lax.axis_index("dp"), lax.axis_index("dap")
     me = dp * GROUP + dap
+    core = dap % 2
+    twin = me + 1 - 2 * core
     others = [(me + k) % ALL for k in range(1, ALL)]
-    ids = [{"dp": o // GROUP, "dap": o % GROUP} for o in others]
+    chips = [(me + 2 * k) % ALL for k in range(1, ALL // 2)]
+
+    def device(o):
+        return {"dp": o // GROUP, "dap": o % GROUP}
+
+    def remote(src, dst, send_sem, recv_sem, to):
+        return pltpu.make_async_remote_copy(src, dst, send_sem, recv_sem, device_id=device(to), device_id_type=pl.DeviceIdType.MESH)
+
     sem = pltpu.get_barrier_semaphore()
-    for to in ids:
-        pl.semaphore_signal(sem, inc=1, device_id=to, device_id_type=pl.DeviceIdType.MESH)
+    for to in others:
+        pl.semaphore_signal(sem, inc=1, device_id=device(to), device_id_type=pl.DeviceIdType.MESH)
     at = 0
     for ref, rows in zip((p0, p1, p2, p3), PACKS):
         send_ref[at:at + rows, :] = ref[...].astype(BF16)
@@ -531,35 +540,47 @@
     send_ref[at:, :] = jnp.zeros((ALL * SHARE - at, C), BF16)
     pl.semaphore_wait(sem, ALL - 1)
 
-    def first(to, k, frm):
-        return pltpu.make_async_remote_copy(send_ref.at[share(others[k])], got_ref.at[frm], ss.at[k], rs.at[frm], device_id=to, device_id_type=pl.DeviceIdType.MESH)
-
-    def second(to, k, frm):
-        return pltpu.make_async_remote_copy(part_ref, tot_ref.at[share(frm)], ss2.at[k], rs2.at[frm], device_id=to, device_id_type=pl.DeviceIdType.MESH)
-
-    for k, to in enumerate(ids):
-        first(to, k, me).start()
+    def first(k, frm):
+        return remote(send_ref.at[share(others[k])], got_ref.at[frm], ss.at[k], rs.at[frm], others[k])
+
+    def second(k, frm):
+        return remote(part_ref, tot_ref.at[share(frm)], ss2.at[k], rs2.at[frm], chips[k])
+
+    def third(k, block):
+        return remote(tot_ref.at[share(block)], tot_ref.at[share(block)], ss3.at[k], rs3.at[k], twin)
+
+    for k in range(ALL - 1):
+        first(k, me).start()
     got_ref[me] = send_ref[share(me), :]
-    for k, to in enumerate(ids):
-        first(to, k, others[k]).wait_recv()
+    for k in range(ALL - 1):
+        first(k, others[k]).wait_recv()
     total = got_ref[0].astype(F32)
     for k in range(1, ALL):
         total = total + got_ref[k].astype(F32)
     part_ref[...] = total
-    for k, to in enumerate(ids):
-        second(to, k, me).start()
+    for k in range(ALL // 2 - 1):
+        second(k, me).start()
+    own = remote(part_ref, tot_ref.at[share(me)], ss3.at[7], rs3.at[7], twin)
+    own.start()
     tot_ref[share(me), :] = total
-    for k, to in enumerate(ids):
-        second(to, k, others[k]).wait_recv()
-    for k, to in enumerate(ids):
-        first(to, k, me).wait_send()
-        second(to, k, me).wait_send()
-
-
-def split_kernel(z_t, dz_t, tot, z_out, dz_out, *grads):
-    for r in range(STEP):
-        z_out[r] = z_t[r].astype(F32).T.astype(BF16)
-        dz_out[r] = dz_t[r].astype(F32).T.astype(BF16)
+    for k in range(ALL // 2 - 2, -1, -1):
+        back = (me + ALL - 2 * (k + 1)) % ALL
+        second(k, back).wait_recv()
+        third(k, back).start()
+    for k in range(ALL // 2 - 1):
+        third(k, (twin + ALL - 2 * (k + 1)) % ALL).wait_recv()
+    remote(part_ref, tot_ref.at[share(twin)], ss3.at[7], rs3.at[7], twin).wait_recv()
+    own.wait_send()
+    for k in range(ALL - 1):
+        first(k, me).wait_send()
+    for k in range(ALL // 2 - 1):
+        second(k, me).wait_send()
+        third(k, (me + ALL - 2 * (k + 1)) % ALL).wait_send()
+
+
+def split_kernel(z_in, dz_in, tot, z_out, dz_out, *grads):
+    z_out[...] = z_in[...]
+    dz_out[...] = dz_in[...]
     pl.when(pl.program_id(0) == 0)(lambda: split_grads(tot, *grads))
 
 
@@ -578,7 +599,7 @@
         at += 5 * C + 16
 
 
-def finish(z_t, dz_t, packs):
+def finish(z_new, dz_new, packs):
     vmem = pl.BlockSpec(memory_space=pltpu.VMEM)
     dma = pltpu.SemaphoreType.DMA((ALL,))
     total = pl.pallas_call(
@@ -586,7 +607,7 @@
         in_specs=[vmem] * 4,
         out_specs=vmem,
         out_shape=jax.ShapeDtypeStruct((ALL * SHARE, C), F32),
-        scratch_shapes=[pltpu.VMEM((ALL * SHARE, C), BF16), pltpu.VMEM((ALL, SHARE, C), BF16), pltpu.VMEM((SHARE, C), F32), dma, dma, dma, dma],
+        scratch_shapes=[pltpu.VMEM((ALL * SHARE, C), BF16), pltpu.VMEM((ALL, SHARE, C), BF16), pltpu.VMEM((SHARE, C), F32), dma, dma, dma, dma, dma, dma],
         compiler_params=pltpu.CompilerParams(vmem_limit_bytes=VMEM_LIMIT, collective_id=5, has_side_effects=True),
         name="sum",
     )(*packs)
@@ -595,12 +616,12 @@
     return pl.pallas_call(
         split_kernel,
         grid=(STEPS,),
-        in_specs=[by_row(z_t), by_row(dz_t), whole(total)],
+        in_specs=[by_row(z_new), by_row(dz_new), whole(total)],
         out_specs=[by_row(NATIVE)] * 2 + [pl.BlockSpec(x.shape, lambda t, n=len(x.shape): (0,) * n) for x in grads],
         out_shape=[NATIVE] * 2 + grads,
         compiler_params=pltpu.CompilerParams(dimension_semantics=("arbitrary",)),
         name="split",
-    )(z_t, dz_t, total)
+    )(z_new, dz_new, total)
 
 
 TRI = jax.ShapeDtypeStruct((CH, N, N), BF16)
@@ -673,12 +694,12 @@
     a1, b1, g1, keep1, unit1, inv1, zm, gu0, munit0, minv0 = row_call(
         mid_kernel, "mid", 1, [a0, b0], [z, g0, mask], post + pre, kept + [ROW, ROW32, ROW32, INV], 1, eye + pre_c + post_c)
     dx1, z_new, dpg1, post_g1 = row_call(
-        turn_kernel, "turn", 2, [a1, b1], [zm, g1, dz], post, [TRI, ROW, ROW32, POST], 1, eye + post_c + post_acc)
+        turn_kernel, "turn", 2, [a1, b1], [zm, g1, dz], post, [TRI, NATIVE, ROW32, POST], 1, eye + post_c + post_acc)
     dx0, dzm, dpg0, pre_g1, post_g0 = row_call(
         back_kernel, "back", 3, [a1, b1, dx1], [dpg1, keep1, unit1, inv1, dz, munit0, minv0, g0, gu0], [ln_in, w_proj, ln_mid, w_out],
         [TRI, ROW, ROW32, PRE, POST], 2, eye + gains * 2 + pre_acc + post_acc)
     dz_new, pre_g0 = row_call(
-        last_kernel, "last", 4, [a0, b0, dx0], [dpg0, keep0, unit0, inv0, dzm], [ln_in, w_proj], [ROW, PRE], 2, gains + pre_acc)
+        last_kernel, "last", 4, [a0, b0, dx0], [dpg0, keep0, unit0, inv0, dzm], [ln_in, w_proj], [NATIVE, PRE], 2, gains + pre_acc)
     z_out, dz_pair, *grads = finish(z_new, dz_new, [post_g0, post_g1, pre_g0, pre_g1])
     return z_out[None], dz_pair[None], *grads
 

time: 355 us -> 350 us (0.986)
  Pallas kernels: 354 us -> 349 us
    pallas_call x1, Pallas kernels: 26.1 us -> 22.2 us  [finish(): pl.pallas_call(sum_kernel, in_specs=[vmem] * 4, out_specs=vmem, out_shape...]
where the time goes in v6:
time: 350 us
  Pallas kernels  349 us (100%)
    pallas_call x5, Pallas kernels, row_call(): pl.pallas_call(kernel, grid=(STEPS + lead,), in_specs=[far if tris else b...  321 us
    pallas_call x1, Pallas kernels, finish(): pl.pallas_call(sum_kernel, in_specs=[vmem] * 4, out_specs=vmem, out_shape...  22.2 us

profile of v6, /device:TPU:0, one launch (start us, length us, event | category | flops | bytes accessed | tf_op | source)
XLA Modules:
  0.0 350.0 jit_solution(1586322508119521814)
XLA Ops:
  0.6 56.0 %pre0.1 = (bf16[16,256,256]{2,1,0:T(8,128)(2,1)}, bf16[16,256,256]{2,1,0:T(8,128)(2,1)}, f32[32,128,256]{2,1,0:T(8,128)}, f32[32,4,128,256]{3,2,1,0:T(8,128)}, f...) custom-call(bf16[32,256,128]{2,1,0:T(8,128)(2,1)} %bitcast.7, s32[4,8,256]{2,1,0:T(8,128)} %bitcast.9, ...), custom_call_target="tpu_custom_call" | custom-call | tf_op jit(solution)/shard_map/pre0/pallas_call | solution.py:669
  56.6 78.2 %mid.1 = (bf16[16,256,256]{2,1,0:T(8,128)(2,1)}, bf16[16,256,256]{2,1,0:T(8,128)(2,1)}, f32[32,128,256]{2,1,0:T(8,128)}, f32[32,4,128,256]{3,2,1,0:T(8,128)}, f3...) custom-call(bf16[16,256,256]{2,1,0:T(8,128)(2,1)} %get-tuple-element, ...), custom_call_target="tpu_custom_call" | custom-call | tf_op jit(solution)/shard_map/mid/pallas_call | solution.py:669
  134.8 52.2 %turn.1 = (bf16[16,256,256]{2,1,0:T(8,128)(2,1)}, bf16[32,256,128]{2,1,0:T(8,128)(2,1)}, f32[32,128,256]{2,1,0:T(8,128)}, f32[144,128]{1,0:T(8,128)}) custom-call(bf16[16,256,256]{2,1,0:T(8,128)(2,1)} %get-tuple-element.46.refs_0_, bf16[16,256,256]{2,1,0:T(8,128)(2,1)} %get-tuple-element.47.refs_1_, bf16[32,128,256]{2,1,0:T(8,128)(2,1)} %get-tuple-element.48.refs_2_, ...), custom_call_target="tpu_custom_call" | custom-call | tf_op jit(solution)/shard_map/turn/pallas_call | solution.py:669
  187.0 79.1 %back.1 = (bf16[16,256,256]{2,1,0:T(8,128)(2,1)}, bf16[32,128,256]{2,1,0:T(8,128)(2,1)}, f32[32,128,256]{2,1,0:T(8,128)}, f32[656,128]{1,0:T(8,128)}, f32[144,128]{1,0:T(8,128)}) custom-call(bf16[16,256,256]{2,1,0:T(8,128)(2,1)} %get-tuple-element.46.refs_0_, bf16[16,256,256]{2,1,0:T(8,128)(2,1)} %get-tuple-element.47.refs_1_, ...), custom_call_target="tpu_custom_call" | custom-call | tf_op jit(solution)/shard_map/back/pallas_call | solution.py:669
  266.1 56.0 %last.1 = (bf16[32,256,128]{2,1,0:T(8,128)(2,1)}, f32[656,128]{1,0:T(8,128)}) custom-call(bf16[16,256,256]{2,1,0:T(8,128)(2,1)} %get-tuple-element.43.refs_0_, bf16[16,256,256]{2,1,0:T(8,128)(2,1)} %get-tuple-element.44.refs_1_, bf16[16,256,256]{2,1,0:T(8,128)(2,1)} %get-tuple-element.59.refs_2_, f32[32,128,256]{2,1,0:T(8,128)} %get-tuple-element.60.refs_3_, ...), custom_call_target="tpu_custom_call" | custom-call | tf_op jit(solution)/shard_map/last/pallas_call | solution.py:669
  322.1 22.2 %sum.1.tot = f32[1792,128]{1,0:T(8,128)} custom-call(f32[144,128]{1,0:T(8,128)} %get-tuple-element.66.p0, f32[144,128]{1,0:T(8,128)} %get-tuple-element.67.p1, f32[656,128]{1,0:T(8,128)} %get-tuple-element.68.p2, f32[656,128]{1,0:T(8,128)} %get-tuple-element.69.p3), custom_call_target="tpu_custom_call" | custom-call | tf_op jit(solution)/shard_map/sum/pallas_call | solution.py:605
  344.3 5.5 %split.1 = (bf16[32,256,128]{2,1,0:T(8,128)(2,1)}, bf16[32,256,128]{2,1,0:T(8,128)(2,1)}, f32[2,2,128]{2,1,0:T(2,128)}, f32[2,128,640]{2,1,0:T(8,128)}, f32[2,64...) custom-call(bf16[32,256,128]{2,1,0:T(8,128)(2,1)} %get-tuple-element.50.z_in, ...), custom_call_target="tpu_custom_call" | custom-call | tf_op jit(solution)/shard_map/split/pallas_call | solution.py:616

commit v7 on v6

--- a/solution.py
+++ b/solution.py
@@ -16,6 +16,8 @@
 STEP = 8
 UNROLL = 4
 STEPS = ROWS // STEP
+PROJ = 5 * C
+HAT = 16
 F32 = jnp.float32
 BF16 = jnp.bfloat16
 VMEM_LIMIT = 62 * 1024 * 1024
@@ -25,17 +27,29 @@
     return lax.dot_general(lhs, rhs, (((lhs_dim,), (rhs_dim,)), ((), ())), preferred_element_type=F32)
 
 
+nn = functools.partial(dot, lhs_dim=1, rhs_dim=0)
+nt = functools.partial(dot, lhs_dim=1, rhs_dim=1)
+tn = functools.partial(dot, lhs_dim=0, rhs_dim=0)
+
+
+def step_now():
+    return pl.program_id(0)
+
+
+def mean(values):
+    return jnp.mean(values, axis=0, keepdims=True)
+
+
 def norm(values):
-    mean = jnp.mean(values, axis=0, keepdims=True)
-    cen = values - mean
-    inv = lax.rsqrt(jnp.mean(cen * cen, axis=0, keepdims=True) + LN_EPS)
+    cen = values - mean(values)
+    inv = lax.rsqrt(mean(cen * cen) + LN_EPS)
     return cen * inv, inv
 
 
 def norm_back(d_hat, unit, inv, gain):
     d_unit = d_hat * gain
-    mean_d = jnp.mean(d_unit, axis=0, keepdims=True)
-    mean_du = jnp.mean(d_unit * unit, axis=0, keepdims=True)
+    mean_d = mean(d_unit)
+    mean_du = mean(d_unit * unit)
     return inv * (d_unit - mean_d - unit * mean_du)
 
 
@@ -54,7 +68,7 @@
 def project(z_t, ln, w_t, bias):
     unit, inv = norm(z_t)
     z_hat = (unit * ln[0] + ln[1]).astype(BF16)
-    return unit, inv, z_hat, dot(w_t[...], z_hat, 1, 0) + bias[...]
+    return unit, inv, z_hat, nn(w_t[...], z_hat) + bias[...]
 
 
 def set_eye(eye):
@@ -143,24 +157,77 @@
     ]
 
 
+BCH = C // 2
+BLOCK = N // 2
+
+
+def by_column(kind, core):
+    return core if kind else 1 - core
+
+
+def pick(column, on_column, on_row):
+    return column * on_column + (1 - column) * on_row
+
+
+def channels(core):
+    return pl.ds(pl.multiple_of(core * BCH, BCH), BCH)
+
+
+def swap(lo, hi):
+    first = lax.broadcasted_iota(jnp.int32, lo.shape, 1) < BLOCK // 2
+    return jnp.where(first, lo, pltpu.roll(hi, BLOCK // 2, 1)), jnp.where(first, pltpu.roll(lo, BLOCK // 2, 1), hi)
+
+
+def swap_core1(value):
+    lo, hi = swap(value[BCH:, :BLOCK], value[BCH:, BLOCK:])
+    return jnp.concatenate([value[:BCH], jnp.concatenate([lo, hi], axis=1)], axis=0)
+
+
+def block_copies(kind, halves, send_ref, out_ref, send_sem, recv_sem, slot):
+    me, cy, cx, core = place()
+    out = []
+    for k, (to, far) in enumerate(((0, 1), (1, 1), (1 - core, 0), (core, 0))):
+        column = by_column(kind, to)
+        y, x = cy, cx
+        if far:
+            y, x = (1 - cy, cx) if column else (cy, 1 - cx)
+        start = pick(column, cy, cx) * 2 * ROWS + core * ROWS + slot * STEP
+        src = send_ref.at[slot, pick(column, y, x), channels(to)] if halves else send_ref.at[slot, channels(to)]
+        out.append(move(src, out_ref.at[:, pl.ds(pl.multiple_of(start, STEP), STEP), :], send_sem.at[slot, k], recv_sem, (y * 2 + x) * 2 + to, k == 3))
+    return out
+
+
+def pack_halves(stage, send_ref, slot):
+    for h in range(2):
+        for q in range(4):
+            rows = stage[pl.ds((h * C + q * 32) * STEP, 32 * STEP), :].reshape(32, STEP, C)
+            send_ref[slot, h, q * 32:(q + 1) * 32] = rows.astype(BF16)
+
+
+A_ROWS = (pack_rows, functools.partial(block_copies, 0, False))
+B_ROWS = (pack_rows, functools.partial(block_copies, 1, False))
+ROWS_ALL = (pack_rows, row_copies)
+DX_ROWS = (pack_halves, functools.partial(block_copies, 0, True))
+
+
 def send_rows(step, jobs):
-    for stage, send_ref, out_ref, send_sem, recv_sem in jobs:
-        pack_rows(stage, send_ref, step)
-        for copy in row_copies(send_ref, out_ref, send_sem, recv_sem, step):
+    for (pack, copies), stage, send_ref, out_ref, send_sem, recv_sem in jobs:
+        pack(stage, send_ref, step)
+        for copy in copies(send_ref, out_ref, send_sem, recv_sem, step):
             copy.start()
 
     @pl.when(step == STEPS - 1)
     def _():
-        for stage, send_ref, out_ref, send_sem, recv_sem in jobs:
+        for (pack, copies), stage, send_ref, out_ref, send_sem, recv_sem in jobs:
             for slot in range(STEPS):
-                wait_sends(row_copies(send_ref, out_ref, send_sem, recv_sem, slot))
+                wait_sends(copies(send_ref, out_ref, send_sem, recv_sem, slot))
             pltpu.make_async_copy(out_ref, out_ref, recv_sem).wait()
 
 
-OUT_FWD = (lambda r, c: dot(r[0][c], r[1][c], 1, 1),)
-IN_FWD = (lambda r, c: dot(r[0][c], r[1][c], 0, 0),)
-IN_BWD = (lambda r, c: dot(r[1][c], r[2][c], 1, 1), lambda r, c: dot(r[0][c], r[2][c], 1, 0))
-OUT_BWD = (lambda r, c: dot(r[2][c], r[1][c], 1, 0), lambda r, c: dot(r[2][c], r[0][c], 0, 0))
+OUT_FWD = (lambda c, a, b: nt(a[c], b[c]),)
+IN_FWD = (lambda c, a, b: tn(a[c], b[c]),)
+IN_BWD = (lambda c, a, b, dx: nt(b[c], dx[c]), lambda c, a, b, dx: nn(a[c], dx[c]))
+OUT_BWD = (lambda c, a, b, dx: nn(dx[c], b[c]), lambda c, a, b, dx: tn(dx[c], a[c]))
 
 
 def back_copy(job, t, k, dest, frm):
@@ -178,7 +245,8 @@
         self.source, self.ref, self.sems = source, ref, sems
 
     def load(self, g):
-        part = pl.ds(g * (CH // GROUPS), CH // GROUPS)
+        size = self.ref.shape[0] // GROUPS
+        part = pl.ds(g * size, size)
         return pltpu.make_async_copy(self.source.at[part], self.ref.at[part], self.sems.at[g])
 
 
@@ -189,7 +257,7 @@
         stage, send_ref, land_ref = job[:3]
 
         def body(c, carry):
-            value = product(refs, c)
+            value = product(c, *refs)
             for h in range(2):
                 stage[pl.ds((h * 2 + c // 8) * N * 8 + c % 8, N, stride=8), :] = value[:, h * C:(h + 1) * C]
             return carry
@@ -213,11 +281,95 @@
             land_ref[t, :, pl.ds(pl.multiple_of(me * CH, CH), CH), :] = send_ref[t, me]
 
 
+def block_sends(kind, job, t):
+    stage, send_ref, land_ref, send_sem, recv_sem = job
+    me, cy, cx, core = place()
+    column = by_column(kind, core)
+    mine = pick(column, cy, cx)
+    y, x = cy + column * (1 - 2 * cy), cx + (1 - column) * (1 - 2 * cx)
+    land = land_ref.at[t, mine, :, channels(core), :]
+    out = []
+    for k, (dest, member, slot) in enumerate((((y * 2 + x) * 2, pick(column, y, x) * 2, core), ((y * 2 + x) * 2 + 1, pick(column, y, x) * 2 + 1, core),
+                                              (me + 1 - 2 * core, mine * 2 + 1 - core, 2))):
+        out.append(pltpu.make_async_remote_copy(send_ref.at[t, member], land, send_sem.at[t, k], recv_sem.at[t, slot],
+                                                device_id={"dap": dest}, device_id_type=pl.DeviceIdType.MESH))
+    return out
+
+
+def block_receives(kind, job, t):
+    stage, send_ref, land_ref, send_sem, recv_sem = job
+    me, cy, cx, core = place()
+    out = []
+    for slot, (frm, far) in enumerate(((0, 1), (1, 1), (1 - core, 0))):
+        column = by_column(kind, frm)
+        y, x = cy, cx
+        if far:
+            y, x = (1 - cy, cx) if column else (cy, 1 - cx)
+        out.append(pltpu.make_async_remote_copy(send_ref.at[t, 0], land_ref.at[t, pick(column, y, x), :, channels(frm), :], send_sem.at[t, slot],
+                                                recv_sem.at[t, slot], device_id={"dap": (y * 2 + x) * 2 + frm}, device_id_type=pl.DeviceIdType.MESH))
+    return out
+
+
+def block_part(products, kinds, ins, jobs):
+    me, cy, cx, core = place()
+    refs = [x.ref for x in ins]
+    for j, (product, kind, job) in enumerate(zip(products, kinds, jobs)):
+        stage, send_ref, land_ref = job[:3]
+        tiles = send_ref.shape[-1] // C
+
+        def body(c, carry):
+            value = product(c, *refs)
+            for h in range(tiles):
+                stage[pl.ds((h * (BCH // 8) + c // 8) * BLOCK * 8 + c % 8, BLOCK, stride=8), :] = value[:, h * C:(h + 1) * C]
+            return carry
+
+        for g in range(GROUPS):
+            if j == 0:
+                for x in ins:
+                    x.load(g).wait()
+            lax.fori_loop(g * (BCH // GROUPS), (g + 1) * (BCH // GROUPS), body, 0, unroll=4)
+        if j == 0:
+            all_in()
+        mine = pick(by_column(kind, core), cy, cx)
+
+        def turn(t, carry):
+            for member in range(4):
+                for h in range(tiles):
+                    for q in range(BCH // 16):
+                        at = (h * (BCH // 8) + 2 * q) * BLOCK * 8 + (member * ROWS + t * STEP) * 8
+                        lo = stage[pl.ds(pl.multiple_of(at, 64), 64), :].reshape(STEP, 8, C)
+                        hi = stage[pl.ds(pl.multiple_of(at + BLOCK * 8, 64), 64), :].reshape(STEP, 8, C)
+                        send_ref[t, member, :, q * 16:(q + 1) * 16, h * C:(h + 1) * C] = jnp.concatenate([lo, hi], axis=1).astype(BF16)
+            for copy in block_sends(kind, job, t):
+                copy.start()
+            land_ref[t, mine, :, channels(core), :] = send_ref[t, mine * 2 + core]
+            return carry
+
+        lax.fori_loop(0, STEPS, turn, 0)
+
+
+def block_arrive(t, kinds, jobs):
+    for kind, job in zip(kinds, jobs):
+        for copy in block_receives(kind, job, t):
+            copy.wait_recv()
+
+    @pl.when(t == STEPS - 1)
+    def _():
+        for kind, job in zip(kinds, jobs):
+            for slot in range(STEPS):
+                for copy in block_sends(kind, job, slot):
+                    copy.wait_send()
+
+
+def both(land_ref, t, r):
+    return land_ref[t, 0, r].astype(F32) + land_ref[t, 1, r].astype(F32)
+
+
 def staged_kernel(inner, n_tri, n_in, *refs):
     far, refs = refs[:n_tri + n_in], refs[n_tri + n_in:]
     near, refs = refs[-2 - n_tri - n_in:-2], refs[:-2 - n_tri - n_in] + refs[-2:]
     refs, (tri_sem, row_sem) = refs[:-2], refs[-2:]
-    step = pl.program_id(0)
+    step = step_now()
     tris = [Piecewise(far[k], near[k], tri_sem.at[k]) for k in range(n_tri)]
 
     def fetch(t, slot):
@@ -289,7 +441,7 @@
 
 def pre_kernel(z_ref, mask_ref, ln_in, w_proj, b_proj, a_ref, b_ref, g_ref, keep_ref, unit_ref, inv_ref, a_st, b_st, a_send, b_send,
                eye_ref, ln_ref, w_t_ref, bias_ref, a_ss, b_ss, rs):
-    step = pl.program_id(0)
+    step = step_now()
 
     @pl.when(step == 0)
     def _():
@@ -299,18 +451,18 @@
 
     @rows_loop
     def _(r):
-        z_t = dot(eye_ref[...], z_ref[r], 1, 1)
+        z_t = nt(eye_ref[...], z_ref[r])
         pre_row(r, z_t, mask_ref, ln_ref, w_t_ref, bias_ref, g_ref, keep_ref, unit_ref, inv_ref, a_st, b_st)
 
     pl.when(step == 0)(all_in)
-    send_rows(step, [(a_st, a_send, a_ref, a_ss, rs.at[0]), (b_st, b_send, b_ref, b_ss, rs.at[1])])
+    send_rows(step, [(A_ROWS, a_st, a_send, a_ref, a_ss, rs.at[0]), (B_ROWS, b_st, b_send, b_ref, b_ss, rs.at[1])])
 
 
 def mid_kernel(a_in, b_in, z_ref, g0_ref, mask_ref, ln_mid, w_out, b_out, ln_in, w_proj, b_proj,
                a_ref, b_ref, g_ref, keep_ref, unit_ref, inv_ref, zm_ref, gu_ref, munit_ref, minv_ref, a_st, b_st, a_send, b_send,
                eye_ref, ln_ref, w_t_ref, bias_ref, mln_ref, wo_t_ref, bo_ref, a_ss, b_ss, rs,
                st0, se0, la0, ss0, rv0):
-    step = pl.program_id(0)
+    step = step_now()
     jobs = [(st0, se0, la0, ss0, rv0)]
 
     @pl.when(step == 0)
@@ -319,29 +471,28 @@
         set_eye(eye_ref)
         set_pre(1, ln_in, w_proj, b_proj, ln_ref, w_t_ref, bias_ref)
         set_post(0, ln_mid, w_out, b_out, mln_ref, wo_t_ref, bo_ref)
-        channel_part(OUT_FWD, (a_in, b_in), jobs)
+        block_part(OUT_FWD, (0,), (a_in, b_in), jobs)
 
     @pl.when(step > 0)
     def _():
         t = step - 1
-        arrive(t, jobs)
-        x_ref = la0.at[t]
+        block_arrive(t, (0,), jobs)
 
         @rows_loop
         def _(r):
-            unit, inv = norm(x_ref[r].astype(F32))
+            unit, inv = norm(swap_core1(jnp.concatenate([la0[t, 0, r], la0[t, 1, r]], axis=1).astype(F32)))
             munit_ref[r] = unit
             minv_ref[0, pl.ds(r, 1), :] = inv
             x_hat = (unit * mln_ref[0] + mln_ref[1]).astype(BF16)
-            update = dot(wo_t_ref[...], x_hat, 1, 0) + bo_ref[...]
+            update = nn(wo_t_ref[...], x_hat) + bo_ref[...]
             g = g0_ref[r]
             change = g * update
             gu_ref[r] = change * (1.0 - g)
-            z_new = (dot(eye_ref[...], z_ref[r], 1, 1) + change).astype(BF16)
+            z_new = (nt(eye_ref[...], z_ref[r]) + change).astype(BF16)
             zm_ref[r] = z_new
             pre_row(r, z_new.astype(F32), mask_ref, ln_ref, w_t_ref, bias_ref, g_ref, keep_ref, unit_ref, inv_ref, a_st, b_st)
 
-        send_rows(t, [(a_st, a_send, a_ref, a_ss, rs.at[0]), (b_st, b_send, b_ref, b_ss, rs.at[1])])
+        send_rows(t, [(ROWS_ALL, a_st, a_send, a_ref, a_ss, rs.at[0]), (ROWS_ALL, b_st, b_send, b_ref, b_ss, rs.at[1])])
 
 
 def post_back_row(unit, inv, g, dz, mln_ref, wo_ref, acc_ref, x_hat=None):
@@ -349,9 +500,9 @@
         x_hat = (unit * mln_ref[0] + mln_ref[1]).astype(BF16)
     d_up = dz * g
     d_up_bf = d_up.astype(BF16)
-    acc_ref[0] += dot(x_hat, d_up_bf, 1, 1)
+    acc_ref[0] += nt(x_hat, d_up_bf)
     acc_ref[3] += fold(d_up)
-    d_hat = dot(wo_ref[...], d_up_bf, 1, 0).astype(BF16).astype(F32)
+    d_hat = nn(wo_ref[...], d_up_bf).astype(BF16).astype(F32)
     acc_ref[1] += fold(d_hat * unit)
     acc_ref[2] += fold(d_hat)
     return norm_back(d_hat, unit, inv, mln_ref[0])
@@ -360,13 +511,13 @@
 def put_post(grad_ref, acc_ref):
     grad_ref[0:C, :] = acc_ref[0]
     grad_ref[C:C + 8, :] = jnp.concatenate([row_sums(acc_ref[1]), row_sums(acc_ref[2]), row_sums(acc_ref[3]), jnp.zeros((5, C), F32)], axis=0)
-    grad_ref[C + 8:C + 16, :] = jnp.zeros((8, C), F32)
+    grad_ref[C + 8:C + HAT, :] = jnp.zeros((8, C), F32)
 
 
 def turn_kernel(a_in, b_in, zm_ref, g_ref, dz_ref, ln_mid, w_out, b_out,
                 dx_ref, z_out_ref, dpg_ref, grad_ref, d_st, d_send, eye_ref, mln_ref, wo_t_ref, bo_ref, acc_ref, d_ss, rs,
                st0, se0, la0, ss0, rv0):
-    step = pl.program_id(0)
+    step = step_now()
     jobs = [(st0, se0, la0, ss0, rv0)]
     wo_ref = w_out.at[1]
 
@@ -386,11 +537,11 @@
 
         @rows_loop
         def _(r):
-            dz = dot(eye_ref[...], dz_ref[r], 1, 1)
+            dz = nt(eye_ref[...], dz_ref[r])
             g = g_ref[r]
             unit, inv = norm(x_ref[r].astype(F32))
             x_hat = (unit * mln_ref[0] + mln_ref[1]).astype(BF16)
-            change = g * (dot(wo_t_ref[...], x_hat, 1, 0) + bo_ref[...])
+            change = g * (nn(wo_t_ref[...], x_hat) + bo_ref[...])
             dpg_ref[r] = dz * change * (1.0 - g)
             z_out_ref[r] = (zm_ref[r].astype(F32) + change).T.astype(BF16)
             spread(d_st, post_back_row(unit, inv, g, dz, mln_ref, wo_ref, acc_ref, x_hat), r)
@@ -399,7 +550,7 @@
         def _():
             put_post(grad_ref, acc_ref)
 
-        send_rows(t, [(d_st, d_send, dx_ref, d_ss, rs.at[0])])
+        send_rows(t, [(ROWS_ALL, d_st, d_send, dx_ref, d_ss, rs.at[0])])
 
 
 def pre_back_row(unit, inv, keep, da, db, d_pg, ln_ref, w_ref, w_acc, b_acc, l_acc):
@@ -412,19 +563,19 @@
     for k, part in enumerate(parts):
         b_acc[k * C:(k + 1) * C, :] += fold(part)
     d_p = jnp.concatenate([part.astype(BF16) for part in parts], axis=0)
-    w_acc[...] += dot(d_p, z_hat, 1, 1)
-    d_hat = dot(w_ref[...], d_p, 1, 0).astype(BF16).astype(F32)
+    w_acc[...] += nt(d_p, z_hat)
+    d_hat = nn(w_ref[...], d_p).astype(BF16).astype(F32)
     l_acc[0] += fold(d_hat * unit)
     l_acc[1] += fold(d_hat)
     return norm_back(d_hat, unit, inv, ln_ref[0])
 
 
 def put_pre(grad_ref, w_acc, b_acc, l_acc):
-    grad_ref[0:5 * C, :] = w_acc[...]
+    grad_ref[0:PROJ, :] = w_acc[...]
     rows = [row_sums(b_acc[k * C:(k + 1) * C, :]) for k in range(5)]
     rows += [row_sums(l_acc[0]), row_sums(l_acc[1]), jnp.zeros((1, C), F32)]
-    grad_ref[5 * C:5 * C + 8, :] = jnp.concatenate(rows, axis=0)
-    grad_ref[5 * C + 8:5 * C + 16, :] = jnp.zeros((8, C), F32)
+    grad_ref[PROJ:PROJ + 8, :] = jnp.concatenate(rows, axis=0)
+    grad_ref[PROJ + 8:PROJ + HAT, :] = jnp.zeros((8, C), F32)
 
 
 def set_gains(ref, ln, block):
@@ -436,7 +587,7 @@
                 dx_ref, dzm_ref, dpg_ref, grad1_ref, grad0_ref, d_st, d_send,
                 eye_ref, ln_ref, mln_ref, w_acc, b_acc, l_acc, acc_ref, d_ss, rs,
                st0, st1, se0, se1, la0, la1, ss0, ss1, rv0, rv1):
-    step = pl.program_id(0)
+    step = step_now()
     jobs = [(st0, se0, la0, ss0, rv0), (st1, se1, la1, ss1, rv1)]
     w_ref, wo_ref = w_proj.at[1], w_out.at[0]
 
@@ -461,25 +612,25 @@
             at = pl.ds(r, 1)
             dzn = pre_back_row(unit_ref[r], inv_ref[0, at, :], keep_ref.at[r], da_ref[r].astype(F32), db_ref[r].astype(F32), dpg1_ref[r],
                                ln_ref, w_ref, w_acc, b_acc, l_acc)
-            dzm = (dot(eye_ref[...], dz_ref[r], 1, 1) + dzn).astype(BF16)
+            dzm = (nt(eye_ref[...], dz_ref[r]) + dzn).astype(BF16)
             dzm_ref[r] = dzm
             dzm = dzm.astype(F32)
             dpg_ref[r] = dzm * gu_ref[r]
-            spread(d_st, post_back_row(munit_ref[r], minv_ref[0, at, :], g_ref[r], dzm, mln_ref, wo_ref, acc_ref), r)
+            spread(d_st, swap_core1(post_back_row(munit_ref[r], minv_ref[0, at, :], g_ref[r], dzm, mln_ref, wo_ref, acc_ref)), r)
 
         @pl.when(t == STEPS - 1)
         def _():
             put_pre(grad1_ref, w_acc, b_acc, l_acc)
             put_post(grad0_ref, acc_ref)
 
-        send_rows(t, [(d_st, d_send, dx_ref, d_ss, rs.at[0])])
+        send_rows(t, [(DX_ROWS, d_st, d_send, dx_ref, d_ss, rs.at[0])])
 
 
 def last_kernel(a_in, b_in, dx_in, dpg_ref, keep_ref, unit_ref, inv_ref, dzm_ref, ln_in, w_proj,
                 dz_ref, grad_ref, ln_ref, w_acc, b_acc, l_acc,
                st0, st1, se0, se1, la0, la1, ss0, ss1, rv0, rv1):
-    step = pl.program_id(0)
-    jobs = [(st0, se0, la0, ss0, rv0), (st1, se1, la1, ss1, rv1)]
+    step = step_now()
+    jobs = [(st0, se0, la0, ss0, rv0), (st0, se1, la1, ss1, rv1)]
     w_ref = w_proj.at[0]
 
     @pl.when(step == 0)
@@ -488,17 +639,16 @@
         set_gains(ln_ref, ln_in, 0)
         for ref in (w_acc, b_acc, l_acc):
             ref[...] = jnp.zeros_like(ref)
-        channel_part(OUT_BWD, (a_in, b_in, dx_in), jobs)
+        block_part(OUT_BWD, (0, 1), (a_in, b_in, dx_in), jobs)
 
     @pl.when(step > 0)
     def _():
         t = step - 1
-        arrive(t, jobs)
-        da_ref, db_ref = la0.at[t], la1.at[t]
+        block_arrive(t, (0, 1), jobs)
 
         @rows_loop
         def _(r):
-            dzn = pre_back_row(unit_ref[r], inv_ref[0, pl.ds(r, 1), :], keep_ref.at[r], da_ref[r].astype(F32), db_ref[r].astype(F32), dpg_ref[r],
+            dzn = pre_back_row(unit_ref[r], inv_ref[0, pl.ds(r, 1), :], keep_ref.at[r], both(la0, t, r), both(la1, t, r), dpg_ref[r],
                                ln_ref, w_ref, w_acc, b_acc, l_acc)
             dz_ref[r] = (dzm_ref[r].astype(F32) + dzn).T.astype(BF16)
 
@@ -509,7 +659,7 @@
 
 ALL = 16
 SHARE = 112
-PACKS = (C + 16, C + 16, 5 * C + 16, 5 * C + 16)
+PACKS = (C + HAT, C + HAT, PROJ + HAT, PROJ + HAT)
 
 
 def share(k):
@@ -581,7 +731,7 @@
 def split_kernel(z_in, dz_in, tot, z_out, dz_out, *grads):
     z_out[...] = z_in[...]
     dz_out[...] = dz_in[...]
-    pl.when(pl.program_id(0) == 0)(lambda: split_grads(tot, *grads))
+    pl.when(step_now() == 0)(lambda: split_grads(tot, *grads))
 
 
 def split_grads(tot, d_ln_in, d_w_proj, d_b_proj, d_ln_mid, d_w_out, d_b_out):
@@ -590,13 +740,13 @@
         d_w_out[k] = tot[at:at + C, :]
         d_ln_mid[k] = tot[at + C:at + C + 2, :]
         d_b_out[k:k + 1, :] = tot[at + C + 2:at + C + 3, :]
-        at += C + 16
+        at += C + HAT
     for k in range(2):
         for j in range(5):
             d_w_proj[k, :, j * C:(j + 1) * C] = tot[at + j * C:at + (j + 1) * C, :].T
-            d_b_proj[k:k + 1, j * C:(j + 1) * C] = tot[at + 5 * C + j:at + 5 * C + j + 1, :]
-        d_ln_in[k] = tot[at + 5 * C + 5:at + 5 * C + 7, :]
-        at += 5 * C + 16
+            d_b_proj[k:k + 1, j * C:(j + 1) * C] = tot[at + PROJ + j:at + PROJ + j + 1, :]
+        d_ln_in[k] = tot[at + PROJ + 5:at + PROJ + 7, :]
+        at += PROJ + HAT
 
 
 def finish(z_new, dz_new, packs):
@@ -611,7 +761,7 @@
         compiler_params=pltpu.CompilerParams(vmem_limit_bytes=VMEM_LIMIT, collective_id=5, has_side_effects=True),
         name="sum",
     )(*packs)
-    shapes = ((2, 2, C), (2, C, 5 * C), (2, 5 * C), (2, 2, C), (2, C, C), (2, C))
+    shapes = ((2, 2, C), (2, C, PROJ), (2, PROJ), (2, 2, C), (2, C, C), (2, C))
     grads = [jax.ShapeDtypeStruct(shape, F32) for shape in shapes]
     return pl.pallas_call(
         split_kernel,
@@ -625,11 +775,14 @@
 
 
 TRI = jax.ShapeDtypeStruct((CH, N, N), BF16)
+BTRI = jax.ShapeDtypeStruct((BCH, BLOCK, N), BF16)
+BDX = jax.ShapeDtypeStruct((BCH, BLOCK, BLOCK), BF16)
+SENT = (TRI, BTRI, BDX)
 ROW = jax.ShapeDtypeStruct((ROWS, C, N), BF16)
 ROW32 = jax.ShapeDtypeStruct((ROWS, C, N), F32)
 NATIVE = jax.ShapeDtypeStruct((ROWS, N, C), BF16)
-POST = jax.ShapeDtypeStruct((C + 16, C), F32)
-PRE = jax.ShapeDtypeStruct((5 * C + 16, C), F32)
+POST = jax.ShapeDtypeStruct((C + HAT, C), F32)
+PRE = jax.ShapeDtypeStruct((PROJ + HAT, C), F32)
 KEEP = jax.ShapeDtypeStruct((ROWS, 4, C, N), F32)
 INV = jax.ShapeDtypeStruct((STEPS, STEP, N), F32)
 
@@ -645,21 +798,26 @@
 
 
 def out_spec(array, lead):
-    if array is TRI:
+    if array in SENT:
         return pl.BlockSpec(memory_space=pl.ANY)
     if array in (PRE, POST):
         return pl.BlockSpec(array.shape, lambda t: (0, 0))
     return by_row(array, lead)
 
 
-def row_call(kernel, name, collective_id, tris, ins, consts, outs, n_back, scratch):
+def row_call(kernel, name, collective_id, tris, ins, consts, outs, n_back, scratch, width=0):
     lead = 1 if tris else 0
-    n_send = sum(out is TRI for out in outs)
+    n_send = sum(out in SENT for out in outs)
+    packed = (STEPS, 2, C, STEP, BLOCK) if BDX in outs else (STEPS, C, STEP, N)
     dma = pltpu.SemaphoreType.DMA
-    sent = [pltpu.VMEM((2 * C * STEP, C), F32)] * n_send + [pltpu.VMEM((STEPS, C, STEP, N), BF16)] * n_send
+    sent = [pltpu.VMEM((2 * C * STEP, C), F32)] * n_send + [pltpu.VMEM(packed, BF16)] * n_send
     sems = [dma((STEPS, GROUP))] * n_send + ([dma((n_send,))] if n_send else [])
     back = [pltpu.VMEM((4 * N * 8, C), F32)] * n_back + [pltpu.VMEM((STEPS, GROUP, STEP, CH, N), BF16)] * n_back
-    back += [pltpu.VMEM((STEPS, STEP, C, N), BF16)] * n_back + [dma((STEPS, GROUP))] * (2 * n_back)
+    back += [pltpu.VMEM((STEPS, STEP, C, N), BF16)] * n_back
+    if width:
+        back = [pltpu.VMEM((BCH * BLOCK * width // C if k == 0 else 8, C), F32) for k in range(n_back)]
+        back += [pltpu.VMEM((STEPS, 4, STEP, BCH, width), BF16)] * n_back + [pltpu.VMEM((STEPS, 2, STEP, C, width), BF16)] * n_back
+    back += [dma((STEPS, GROUP))] * (2 * n_back)
     far = pl.BlockSpec(memory_space=pl.ANY)
     near = []
     if tris:
@@ -683,23 +841,23 @@
     mask = pair_mask.reshape(STEPS, STEP, N)
     pre, post = [ln_in, w_proj, b_proj], [ln_mid, w_out, b_out]
     eye = [pltpu.VMEM((C, C), BF16)]
-    pre_c = [pltpu.VMEM((2, C, N), F32), pltpu.VMEM((5 * C, C), BF16), pltpu.VMEM((5 * C, N), F32)]
+    pre_c = [pltpu.VMEM((2, C, N), F32), pltpu.VMEM((PROJ, C), BF16), pltpu.VMEM((PROJ, N), F32)]
     post_c = [pltpu.VMEM((2, C, N), F32), pltpu.VMEM((C, C), BF16), pltpu.VMEM((C, N), F32)]
     post_acc = [pltpu.VMEM((4, C, C), F32)]
-    pre_acc = [pltpu.VMEM((5 * C, C), F32), pltpu.VMEM((5 * C, C), F32), pltpu.VMEM((2, C, C), F32)]
+    pre_acc = [pltpu.VMEM((PROJ, C), F32), pltpu.VMEM((PROJ, C), F32), pltpu.VMEM((2, C, C), F32)]
 
     gains = [pltpu.VMEM((2, C, N), F32)]
     kept = [TRI, TRI, ROW32, KEEP, ROW32, INV]
-    a0, b0, g0, keep0, unit0, inv0 = row_call(pre_kernel, "pre0", 0, [], [z, mask], pre, kept, 0, eye + pre_c)
+    a0, b0, g0, keep0, unit0, inv0 = row_call(pre_kernel, "pre0", 0, [], [z, mask], pre, [BTRI, BTRI] + kept[2:], 0, eye + pre_c)
     a1, b1, g1, keep1, unit1, inv1, zm, gu0, munit0, minv0 = row_call(
-        mid_kernel, "mid", 1, [a0, b0], [z, g0, mask], post + pre, kept + [ROW, ROW32, ROW32, INV], 1, eye + pre_c + post_c)
+        mid_kernel, "mid", 1, [a0, b0], [z, g0, mask], post + pre, kept + [ROW, ROW32, ROW32, INV], 1, eye + pre_c + post_c, BLOCK)
     dx1, z_new, dpg1, post_g1 = row_call(
         turn_kernel, "turn", 2, [a1, b1], [zm, g1, dz], post, [TRI, NATIVE, ROW32, POST], 1, eye + post_c + post_acc)
     dx0, dzm, dpg0, pre_g1, post_g0 = row_call(
         back_kernel, "back", 3, [a1, b1, dx1], [dpg1, keep1, unit1, inv1, dz, munit0, minv0, g0, gu0], [ln_in, w_proj, ln_mid, w_out],
-        [TRI, ROW, ROW32, PRE, POST], 2, eye + gains * 2 + pre_acc + post_acc)
+        [BDX, ROW, ROW32, PRE, POST], 2, eye + gains * 2 + pre_acc + post_acc)
     dz_new, pre_g0 = row_call(
-        last_kernel, "last", 4, [a0, b0, dx0], [dpg0, keep0, unit0, inv0, dzm], [ln_in, w_proj], [NATIVE, PRE], 2, gains + pre_acc)
+        last_kernel, "last", 4, [a0, b0, dx0], [dpg0, keep0, unit0, inv0, dzm], [ln_in, w_proj], [NATIVE, PRE], 2, gains + pre_acc, N)
     z_out, dz_pair, *grads = finish(z_new, dz_new, [post_g0, post_g1, pre_g0, pre_g1])
     return z_out[None], dz_pair[None], *grads
 

time: 350 us -> 333 us (0.951)
  Pallas kernels: 349 us -> 332 us
    pallas_call x5, Pallas kernels: 321 us -> 303 us  [row_call(): pl.pallas_call(kernel, grid=(STEPS + lead,), in_specs=[far if tris else b...]
where the time goes in v7:
time: 333 us
  Pallas kernels  332 us (100%)
    pallas_call x5, Pallas kernels, row_call(): pl.pallas_call(kernel, grid=(STEPS + lead,), in_specs=[far if tris else b...  303 us
    pallas_call x1, Pallas kernels, finish(): pl.pallas_call(sum_kernel, in_specs=[vmem] * 4, out_specs=vmem, out_shape...  23.4 us

profile of v7, /device:TPU:0, one launch (start us, length us, event | category | flops | bytes accessed | tf_op | source)
XLA Modules:
  0.0 333.1 jit_solution(2111631977352912378)
XLA Ops:
  0.6 55.9 %pre0.1 = (bf16[64,128,256]{2,1,0:T(8,128)(2,1)}, bf16[64,128,256]{2,1,0:T(8,128)(2,1)}, f32[32,128,256]{2,1,0:T(8,128)}, f32[32,4,128,256]{3,2,1,0:T(8,128)}, f...) custom-call(bf16[32,256,128]{2,1,0:T(8,128)(2,1)} %bitcast.7, s32[4,8,256]{2,1,0:T(8,128)} %bitcast.9, ...), custom_call_target="tpu_custom_call" | custom-call | tf_op jit(solution)/shard_map/pre0/pallas_call | solution.py:827
  56.5 70.6 %mid.1 = (bf16[16,256,256]{2,1,0:T(8,128)(2,1)}, bf16[16,256,256]{2,1,0:T(8,128)(2,1)}, f32[32,128,256]{2,1,0:T(8,128)}, f32[32,4,128,256]{3,2,1,0:T(8,128)}, f3...) custom-call(bf16[64,128,256]{2,1,0:T(8,128)(2,1)} %get-tuple-element, ...), custom_call_target="tpu_custom_call" | custom-call | tf_op jit(solution)/shard_map/mid/pallas_call | solution.py:827
  127.1 52.3 %turn.1 = (bf16[16,256,256]{2,1,0:T(8,128)(2,1)}, bf16[32,256,128]{2,1,0:T(8,128)(2,1)}, f32[32,128,256]{2,1,0:T(8,128)}, f32[144,128]{1,0:T(8,128)}) custom-call(bf16[16,256,256]{2,1,0:T(8,128)(2,1)} %get-tuple-element.46.refs_0_, bf16[16,256,256]{2,1,0:T(8,128)(2,1)} %get-tuple-element.47.refs_1_, bf16[32,128,256]{2,1,0:T(8,128)(2,1)} %get-tuple-element.48.refs_2_, ...), custom_call_target="tpu_custom_call" | custom-call | tf_op jit(solution)/shard_map/turn/pallas_call | solution.py:827
  179.4 66.7 %back.1 = (bf16[64,128,128]{2,1,0:T(8,128)(2,1)}, bf16[32,128,256]{2,1,0:T(8,128)(2,1)}, f32[32,128,256]{2,1,0:T(8,128)}, f32[656,128]{1,0:T(8,128)}, f32[144,128]{1,0:T(8,128)}) custom-call(bf16[16,256,256]{2,1,0:T(8,128)(2,1)} %get-tuple-element.46.refs_0_, bf16[16,256,256]{2,1,0:T(8,128)(2,1)} %get-tuple-element.47.refs_1_, ...), custom_call_target="tpu_custom_call" | custom-call | tf_op jit(solution)/shard_map/back/pallas_call | solution.py:827
  246.1 58.0 %last.1 = (bf16[32,256,128]{2,1,0:T(8,128)(2,1)}, f32[656,128]{1,0:T(8,128)}) custom-call(bf16[64,128,256]{2,1,0:T(8,128)(2,1)} %get-tuple-element.43.refs_0_, bf16[64,128,256]{2,1,0:T(8,128)(2,1)} %get-tuple-element.44.refs_1_, bf16[64,128,128]{2,1,0:T(8,128)(2,1)} %get-tuple-element.59.refs_2_, f32[32,128,256]{2,1,0:T(8,128)} %get-tuple-element.60.refs_3_, ...), custom_call_target="tpu_custom_call" | custom-call | tf_op jit(solution)/shard_map/last/pallas_call | solution.py:827
  304.0 23.4 %sum.1.tot = f32[1792,128]{1,0:T(8,128)} custom-call(f32[144,128]{1,0:T(8,128)} %get-tuple-element.66.p0, f32[144,128]{1,0:T(8,128)} %get-tuple-element.67.p1, f32[656,128]{1,0:T(8,128)} %get-tuple-element.68.p2, f32[656,128]{1,0:T(8,128)} %get-tuple-element.69.p3), custom_call_target="tpu_custom_call" | custom-call | tf_op jit(solution)/shard_map/sum/pallas_call | solution.py:755
  327.4 5.5 %split.1 = (bf16[32,256,128]{2,1,0:T(8,128)(2,1)}, bf16[32,256,128]{2,1,0:T(8,128)(2,1)}, f32[2,2,128]{2,1,0:T(2,128)}, f32[2,128,640]{2,1,0:T(8,128)}, f32[2,64...) custom-call(bf16[32,256,128]{2,1,0:T(8,128)(2,1)} %get-tuple-element.50.z_in, ...), custom_call_target="tpu_custom_call" | custom-call | tf_op jit(solution)/shard_map/split/pallas_call | solution.py:766

commit v8 on v7

--- a/solution.py
+++ b/solution.py
@@ -237,6 +237,7 @@
         device_id={"dap": dest}, device_id_type=pl.DeviceIdType.MESH)
 
 
+EARLY = 2
 GROUPS = 4
 
 
@@ -281,17 +282,19 @@
             land_ref[t, :, pl.ds(pl.multiple_of(me * CH, CH), CH), :] = send_ref[t, me]
 
 
-def block_sends(kind, job, t):
+def block_sends(kind, job, t, piece=None):
     stage, send_ref, land_ref, send_sem, recv_sem = job
     me, cy, cx, core = place()
     column = by_column(kind, core)
     mine = pick(column, cy, cx)
     y, x = cy + column * (1 - 2 * cy), cx + (1 - column) * (1 - 2 * cx)
-    land = land_ref.at[t, mine, :, channels(core), :]
+    size = BCH if piece is None else BCH // GROUPS
+    at = (piece or 0) * size
+    land = land_ref.at[t, mine, :, pl.ds(pl.multiple_of(core * BCH + at, size), size), :]
     out = []
     for k, (dest, member, slot) in enumerate((((y * 2 + x) * 2, pick(column, y, x) * 2, core), ((y * 2 + x) * 2 + 1, pick(column, y, x) * 2 + 1, core),
                                               (me + 1 - 2 * core, mine * 2 + 1 - core, 2))):
-        out.append(pltpu.make_async_remote_copy(send_ref.at[t, member], land, send_sem.at[t, k], recv_sem.at[t, slot],
+        out.append(pltpu.make_async_remote_copy(send_ref.at[t, member, :, pl.ds(at, size), :], land, send_sem.at[t, k], recv_sem.at[t, slot],
                                                 device_id={"dap": dest}, device_id_type=pl.DeviceIdType.MESH))
     return out
 
@@ -323,29 +326,37 @@
                 stage[pl.ds((h * (BCH // 8) + c // 8) * BLOCK * 8 + c % 8, BLOCK, stride=8), :] = value[:, h * C:(h + 1) * C]
             return carry
 
+        mine = pick(by_column(kind, core), cy, cx)
+
+        def pack(t, q):
+            for member in range(4):
+                for h in range(tiles):
+                    at = (h * (BCH // 8) + q * 2) * BLOCK * 8 + (member * ROWS + t * STEP) * 8
+                    lo = stage[pl.ds(at, 64), :].reshape(STEP, 8, C)
+                    hi = stage[pl.ds(at + BLOCK * 8, 64), :].reshape(STEP, 8, C)
+                    send_ref[t, member, :, q * CH:(q + 1) * CH, h * C:(h + 1) * C] = jnp.concatenate([lo, hi], axis=1).astype(BF16)
+
+        def keep(t):
+            land_ref[t, mine, :, channels(core), :] = send_ref[t, mine * 2 + core]
+
         for g in range(GROUPS):
             if j == 0:
                 for x in ins:
                     x.load(g).wait()
-            lax.fori_loop(g * (BCH // GROUPS), (g + 1) * (BCH // GROUPS), body, 0, unroll=4)
-        if j == 0:
-            all_in()
-        mine = pick(by_column(kind, core), cy, cx)
-
-        def turn(t, carry):
-            for member in range(4):
-                for h in range(tiles):
-                    for q in range(BCH // 16):
-                        at = (h * (BCH // 8) + 2 * q) * BLOCK * 8 + (member * ROWS + t * STEP) * 8
-                        lo = stage[pl.ds(pl.multiple_of(at, 64), 64), :].reshape(STEP, 8, C)
-                        hi = stage[pl.ds(pl.multiple_of(at + BLOCK * 8, 64), 64), :].reshape(STEP, 8, C)
-                        send_ref[t, member, :, q * 16:(q + 1) * 16, h * C:(h + 1) * C] = jnp.concatenate([lo, hi], axis=1).astype(BF16)
+            lax.fori_loop(g * CH, (g + 1) * CH, body, 0, unroll=4)
+            if g == j == 0:
+                all_in()
+            for t in range(EARLY):
+                pack(t, g)
+                for copy in block_sends(kind, job, t, g):
+                    copy.start()
+        for t in range(EARLY, STEPS):
+            for g in range(GROUPS):
+                pack(t, g)
             for copy in block_sends(kind, job, t):
                 copy.start()
-            land_ref[t, mine, :, channels(core), :] = send_ref[t, mine * 2 + core]
-            return carry
-
-        lax.fori_loop(0, STEPS, turn, 0)
+        for t in range(STEPS):
+            keep(t)
 
 
 def block_arrive(t, kinds, jobs):

time: 333 us -> 327 us (0.982)
  Pallas kernels: 332 us -> 326 us
    pallas_call x5, Pallas kernels: 303 us -> 296 us  [row_call(): pl.pallas_call(kernel, grid=(STEPS + lead,), in_specs=[far if tris else b...]
where the time goes in v8:
time: 327 us
  Pallas kernels  326 us (100%)
    pallas_call x5, Pallas kernels, row_call(): pl.pallas_call(kernel, grid=(STEPS + lead,), in_specs=[far if tris else b...  296 us
    pallas_call x1, Pallas kernels, finish(): pl.pallas_call(sum_kernel, in_specs=[vmem] * 4, out_specs=vmem, out_shape...  24 us

profile of v8, /device:TPU:0, one launch (start us, length us, event | category | flops | bytes accessed | tf_op | source)
XLA Modules:
  0.0 326.5 jit_solution(8121863982645479723)
XLA Ops:
  0.6 55.9 %pre0.1 = (bf16[64,128,256]{2,1,0:T(8,128)(2,1)}, bf16[64,128,256]{2,1,0:T(8,128)(2,1)}, f32[32,128,256]{2,1,0:T(8,128)}, f32[32,4,128,256]{3,2,1,0:T(8,128)}, f...) custom-call(bf16[32,256,128]{2,1,0:T(8,128)(2,1)} %bitcast.7, s32[4,8,256]{2,1,0:T(8,128)} %bitcast.9, ...), custom_call_target="tpu_custom_call" | custom-call | tf_op jit(solution)/shard_map/pre0/pallas_call | solution.py:838
  56.5 67.6 %mid.1 = (bf16[16,256,256]{2,1,0:T(8,128)(2,1)}, bf16[16,256,256]{2,1,0:T(8,128)(2,1)}, f32[32,128,256]{2,1,0:T(8,128)}, f32[32,4,128,256]{3,2,1,0:T(8,128)}, f3...) custom-call(bf16[64,128,256]{2,1,0:T(8,128)(2,1)} %get-tuple-element, ...), custom_call_target="tpu_custom_call" | custom-call | tf_op jit(solution)/shard_map/mid/pallas_call | solution.py:838
  124.1 52.3 %turn.1 = (bf16[16,256,256]{2,1,0:T(8,128)(2,1)}, bf16[32,256,128]{2,1,0:T(8,128)(2,1)}, f32[32,128,256]{2,1,0:T(8,128)}, f32[144,128]{1,0:T(8,128)}) custom-call(bf16[16,256,256]{2,1,0:T(8,128)(2,1)} %get-tuple-element.46.refs_0_, bf16[16,256,256]{2,1,0:T(8,128)(2,1)} %get-tuple-element.47.refs_1_, bf16[32,128,256]{2,1,0:T(8,128)(2,1)} %get-tuple-element.48.refs_2_, ...), custom_call_target="tpu_custom_call" | custom-call | tf_op jit(solution)/shard_map/turn/pallas_call | solution.py:838
  176.4 66.6 %back.1 = (bf16[64,128,128]{2,1,0:T(8,128)(2,1)}, bf16[32,128,256]{2,1,0:T(8,128)(2,1)}, f32[32,128,256]{2,1,0:T(8,128)}, f32[656,128]{1,0:T(8,128)}, f32[144,128]{1,0:T(8,128)}) custom-call(bf16[16,256,256]{2,1,0:T(8,128)(2,1)} %get-tuple-element.46.refs_0_, bf16[16,256,256]{2,1,0:T(8,128)(2,1)} %get-tuple-element.47.refs_1_, ...), custom_call_target="tpu_custom_call" | custom-call | tf_op jit(solution)/shard_map/back/pallas_call | solution.py:838
  243.1 53.8 %last.1 = (bf16[32,256,128]{2,1,0:T(8,128)(2,1)}, f32[656,128]{1,0:T(8,128)}) custom-call(bf16[64,128,256]{2,1,0:T(8,128)(2,1)} %get-tuple-element.43.refs_0_, bf16[64,128,256]{2,1,0:T(8,128)(2,1)} %get-tuple-element.44.refs_1_, bf16[64,128,128]{2,1,0:T(8,128)(2,1)} %get-tuple-element.59.refs_2_, f32[32,128,256]{2,1,0:T(8,128)} %get-tuple-element.60.refs_3_, ...), custom_call_target="tpu_custom_call" | custom-call | tf_op jit(solution)/shard_map/last/pallas_call | solution.py:838
  296.9 24.0 %sum.1.tot = f32[1792,128]{1,0:T(8,128)} custom-call(f32[144,128]{1,0:T(8,128)} %get-tuple-element.66.p0, f32[144,128]{1,0:T(8,128)} %get-tuple-element.67.p1, f32[656,128]{1,0:T(8,128)} %get-tuple-element.68.p2, f32[656,128]{1,0:T(8,128)} %get-tuple-element.69.p3), custom_call_target="tpu_custom_call" | custom-call | tf_op jit(solution)/shard_map/sum/pallas_call | solution.py:766
  320.9 5.5 %split.1 = (bf16[32,256,128]{2,1,0:T(8,128)(2,1)}, bf16[32,256,128]{2,1,0:T(8,128)(2,1)}, f32[2,2,128]{2,1,0:T(2,128)}, f32[2,128,640]{2,1,0:T(8,128)}, f32[2,64...) custom-call(bf16[32,256,128]{2,1,0:T(8,128)(2,1)} %get-tuple-element.50.z_in, ...), custom_call_target="tpu_custom_call" | custom-call | tf_op jit(solution)/shard_map/split/pallas_call | solution.py:777

commit v9 on v8

--- a/solution.py
+++ b/solution.py
@@ -110,8 +110,8 @@
         pl.semaphore_signal(sem, inc=1, device_id={"dap": (me + k) % GROUP}, device_id_type=pl.DeviceIdType.MESH)
 
 
-def all_in():
-    pl.semaphore_wait(pltpu.get_barrier_semaphore(), GROUP - 1)
+def all_in(others=GROUP - 1):
+    pl.semaphore_wait(pltpu.get_barrier_semaphore(), others)
 
 
 def peers():
@@ -313,7 +313,7 @@
     return out
 
 
-def block_part(products, kinds, ins, jobs):
+def block_part(products, kinds, ins, jobs, others=GROUP - 1):
     me, cy, cx, core = place()
     refs = [x.ref for x in ins]
     for j, (product, kind, job) in enumerate(zip(products, kinds, jobs)):
@@ -345,7 +345,7 @@
                     x.load(g).wait()
             lax.fori_loop(g * CH, (g + 1) * CH, body, 0, unroll=4)
             if g == j == 0:
-                all_in()
+                all_in(others)
             for t in range(EARLY):
                 pack(t, g)
                 for copy in block_sends(kind, job, t, g):
@@ -637,20 +637,120 @@
         send_rows(t, [(DX_ROWS, d_st, d_send, dx_ref, d_ss, rs.at[0])])
 
 
-def last_kernel(a_in, b_in, dx_in, dpg_ref, keep_ref, unit_ref, inv_ref, dzm_ref, ln_in, w_proj,
-                dz_ref, grad_ref, ln_ref, w_acc, b_acc, l_acc,
-               st0, st1, se0, se1, la0, la1, ss0, ss1, rv0, rv1):
+ALL = 16
+EARLY_SHARE, LATE_SHARE = 64, 48
+
+
+def device(o):
+    return {"dp": o // GROUP, "dap": o % GROUP}
+
+
+def everyone():
+    dap = lax.axis_index("dap")
+    me = lax.axis_index("dp") * GROUP + dap
+    twin = me + 1 - dap % 2 * 2
+    return me, twin, [(me + k) % ALL for k in range(1, ALL)], [(me + 2 * k) % ALL for k in range(1, GROUP)]
+
+
+def enter_all():
+    for to in everyone()[2]:
+        pl.semaphore_signal(pltpu.get_barrier_semaphore(), inc=1, device_id=device(to), device_id_type=pl.DeviceIdType.MESH)
+
+
+class Adder:
+    def __init__(self, base, send_ref, got_ref, part_ref, tot_ref, sems):
+        self.base, self.send_ref, self.got_ref, self.part_ref, self.tot_ref, self.sems = base, send_ref, got_ref, part_ref, tot_ref, sems
+        self.size = part_ref.shape[0]
+
+    def share(self, k, base=0):
+        return pl.ds(pl.multiple_of(base + k * self.size, HAT), self.size)
+
+    def sums(self, k):
+        return self.tot_ref.at[self.share(k, self.base)]
+
+    def remote(self, src, dst, phase, k, slot, to):
+        return pltpu.make_async_remote_copy(src, dst, self.sems.at[2 * phase, k], self.sems.at[2 * phase + 1, slot], device_id=device(to),
+                                            device_id_type=pl.DeviceIdType.MESH)
+
+    def first(self, k, frm):
+        other = everyone()[2][k]
+        return self.remote(self.send_ref.at[self.share(other)], self.got_ref.at[frm], 0, k, frm, other)
+
+    def second(self, k, frm):
+        return self.remote(self.part_ref, self.sums(frm), 1, k, frm, everyone()[3][k])
+
+    def third(self, k, block):
+        return self.remote(self.sums(block), self.sums(block), 2, k, k, everyone()[1])
+
+    def own(self, block):
+        return self.remote(self.part_ref, self.sums(block), 2, GROUP, GROUP, everyone()[1])
+
+    def before(self, device_number, k):
+        return (device_number + ALL - 2 * (k + 1)) % ALL
+
+    def fill(self, *packs):
+        at = 0
+        for ref in packs:
+            self.send_ref[at:at + ref.shape[0], :] = ref[...].astype(BF16)
+            at += ref.shape[0]
+        self.send_ref[at:, :] = jnp.zeros((self.send_ref.shape[0] - at, C), BF16)
+
+    def scatter(self):
+        me = everyone()[0]
+        for k in range(ALL - 1):
+            self.first(k, me).start()
+        self.got_ref[me] = self.send_ref[self.share(me), :]
+
+    def add(self):
+        me, twin, others, chips = everyone()
+        for k in range(ALL - 1):
+            self.first(k, others[k]).wait_recv()
+        total = self.got_ref[0].astype(F32)
+        for k in range(1, ALL):
+            total = total + self.got_ref[k].astype(F32)
+        self.part_ref[...] = total
+        for k in range(GROUP - 1):
+            self.second(k, me).start()
+        self.own(me).start()
+        self.tot_ref[self.share(me, self.base), :] = total
+
+    def hand_on(self):
+        me = everyone()[0]
+        for k in range(GROUP - 1):
+            self.second(k, self.before(me, k)).wait_recv()
+            self.third(k, self.before(me, k)).start()
+
+    def finish(self):
+        me, twin, others, chips = everyone()
+        for k in range(GROUP - 1):
+            self.third(k, self.before(twin, k)).wait_recv()
+        self.own(twin).wait_recv()
+        self.own(me).wait_send()
+        for k in range(ALL - 1):
+            self.first(k, me).wait_send()
+        for k in range(GROUP - 1):
+            self.second(k, me).wait_send()
+            self.third(k, self.before(me, k)).wait_send()
+
+
+def last_kernel(a_in, b_in, dx_in, dpg_ref, keep_ref, unit_ref, inv_ref, dzm_ref, ln_in, w_proj, post0, post1, pre1,
+                dz_ref, tot_out, ln_ref, w_acc, b_acc, l_acc, grad_ref, send_e, got_e, part_e, send_l, got_l, part_l, tot_ref, sems,
+                st0, st1, se0, se1, la0, la1, ss0, ss1, rv0, rv1):
     step = step_now()
     jobs = [(st0, se0, la0, ss0, rv0), (st0, se1, la1, ss1, rv1)]
     w_ref = w_proj.at[0]
+    early = Adder(0, send_e, got_e, part_e, tot_ref, sems.at[0])
+    late = Adder(send_e.shape[0], send_l, got_l, part_l, tot_ref, sems.at[1])
 
     @pl.when(step == 0)
     def _():
-        enter()
+        enter_all()
         set_gains(ln_ref, ln_in, 0)
         for ref in (w_acc, b_acc, l_acc):
             ref[...] = jnp.zeros_like(ref)
-        block_part(OUT_BWD, (0, 1), (a_in, b_in, dx_in), jobs)
+        block_part(OUT_BWD, (0, 1), (a_in, b_in, dx_in), jobs, ALL - 1)
+        early.fill(post0, post1, pre1)
+        early.scatter()
 
     @pl.when(step > 0)
     def _():
@@ -666,77 +766,15 @@
         @pl.when(t == STEPS - 1)
         def _():
             put_pre(grad_ref, w_acc, b_acc, l_acc)
-
-
-ALL = 16
-SHARE = 112
-PACKS = (C + HAT, C + HAT, PROJ + HAT, PROJ + HAT)
-
-
-def share(k):
-    return pl.ds(pl.multiple_of(k * SHARE, SHARE), SHARE)
-
-
-def sum_kernel(p0, p1, p2, p3, tot_ref, send_ref, got_ref, part_ref, ss, rs, ss2, rs2, ss3, rs3):
-    dp, dap = lax.axis_index("dp"), lax.axis_index("dap")
-    me = dp * GROUP + dap
-    core = dap % 2
-    twin = me + 1 - 2 * core
-    others = [(me + k) % ALL for k in range(1, ALL)]
-    chips = [(me + 2 * k) % ALL for k in range(1, ALL // 2)]
-
-    def device(o):
-        return {"dp": o // GROUP, "dap": o % GROUP}
-
-    def remote(src, dst, send_sem, recv_sem, to):
-        return pltpu.make_async_remote_copy(src, dst, send_sem, recv_sem, device_id=device(to), device_id_type=pl.DeviceIdType.MESH)
-
-    sem = pltpu.get_barrier_semaphore()
-    for to in others:
-        pl.semaphore_signal(sem, inc=1, device_id=device(to), device_id_type=pl.DeviceIdType.MESH)
-    at = 0
-    for ref, rows in zip((p0, p1, p2, p3), PACKS):
-        send_ref[at:at + rows, :] = ref[...].astype(BF16)
-        at += rows
-    send_ref[at:, :] = jnp.zeros((ALL * SHARE - at, C), BF16)
-    pl.semaphore_wait(sem, ALL - 1)
-
-    def first(k, frm):
-        return remote(send_ref.at[share(others[k])], got_ref.at[frm], ss.at[k], rs.at[frm], others[k])
-
-    def second(k, frm):
-        return remote(part_ref, tot_ref.at[share(frm)], ss2.at[k], rs2.at[frm], chips[k])
-
-    def third(k, block):
-        return remote(tot_ref.at[share(block)], tot_ref.at[share(block)], ss3.at[k], rs3.at[k], twin)
-
-    for k in range(ALL - 1):
-        first(k, me).start()
-    got_ref[me] = send_ref[share(me), :]
-    for k in range(ALL - 1):
-        first(k, others[k]).wait_recv()
-    total = got_ref[0].astype(F32)
-    for k in range(1, ALL):
-        total = total + got_ref[k].astype(F32)
-    part_ref[...] = total
-    for k in range(ALL // 2 - 1):
-        second(k, me).start()
-    own = remote(part_ref, tot_ref.at[share(me)], ss3.at[7], rs3.at[7], twin)
-    own.start()
-    tot_ref[share(me), :] = total
-    for k in range(ALL // 2 - 2, -1, -1):
-        back = (me + ALL - 2 * (k + 1)) % ALL
-        second(k, back).wait_recv()
-        third(k, back).start()
-    for k in range(ALL // 2 - 1):
-        third(k, (twin + ALL - 2 * (k + 1)) % ALL).wait_recv()
-    remote(part_ref, tot_ref.at[share(twin)], ss3.at[7], rs3.at[7], twin).wait_recv()
-    own.wait_send()
-    for k in range(ALL - 1):
-        first(k, me).wait_send()
-    for k in range(ALL // 2 - 1):
-        second(k, me).wait_send()
-        third(k, (me + ALL - 2 * (k + 1)) % ALL).wait_send()
+            late.fill(grad_ref)
+            late.scatter()
+            early.add()
+            late.add()
+            early.hand_on()
+            late.hand_on()
+            early.finish()
+            late.finish()
+            tot_out[...] = tot_ref[...]
 
 
 def split_kernel(z_in, dz_in, tot, z_out, dz_out, *grads):
@@ -752,26 +790,14 @@
         d_ln_mid[k] = tot[at + C:at + C + 2, :]
         d_b_out[k:k + 1, :] = tot[at + C + 2:at + C + 3, :]
         at += C + HAT
-    for k in range(2):
+    for k, at in enumerate((ALL * EARLY_SHARE, at)):
         for j in range(5):
             d_w_proj[k, :, j * C:(j + 1) * C] = tot[at + j * C:at + (j + 1) * C, :].T
             d_b_proj[k:k + 1, j * C:(j + 1) * C] = tot[at + PROJ + j:at + PROJ + j + 1, :]
         d_ln_in[k] = tot[at + PROJ + 5:at + PROJ + 7, :]
-        at += PROJ + HAT
-
-
-def finish(z_new, dz_new, packs):
-    vmem = pl.BlockSpec(memory_space=pltpu.VMEM)
-    dma = pltpu.SemaphoreType.DMA((ALL,))
-    total = pl.pallas_call(
-        sum_kernel,
-        in_specs=[vmem] * 4,
-        out_specs=vmem,
-        out_shape=jax.ShapeDtypeStruct((ALL * SHARE, C), F32),
-        scratch_shapes=[pltpu.VMEM((ALL * SHARE, C), BF16), pltpu.VMEM((ALL, SHARE, C), BF16), pltpu.VMEM((SHARE, C), F32), dma, dma, dma, dma, dma, dma],
-        compiler_params=pltpu.CompilerParams(vmem_limit_bytes=VMEM_LIMIT, collective_id=5, has_side_effects=True),
-        name="sum",
-    )(*packs)
+
+
+def finish(z_new, dz_new, total):
     shapes = ((2, 2, C), (2, C, PROJ), (2, PROJ), (2, 2, C), (2, C, C), (2, C))
     grads = [jax.ShapeDtypeStruct(shape, F32) for shape in shapes]
     return pl.pallas_call(
@@ -794,6 +820,7 @@
 NATIVE = jax.ShapeDtypeStruct((ROWS, N, C), BF16)
 POST = jax.ShapeDtypeStruct((C + HAT, C), F32)
 PRE = jax.ShapeDtypeStruct((PROJ + HAT, C), F32)
+TOT = jax.ShapeDtypeStruct((ALL * (EARLY_SHARE + LATE_SHARE), C), F32)
 KEEP = jax.ShapeDtypeStruct((ROWS, 4, C, N), F32)
 INV = jax.ShapeDtypeStruct((STEPS, STEP, N), F32)
 
@@ -811,7 +838,7 @@
 def out_spec(array, lead):
     if array in SENT:
         return pl.BlockSpec(memory_space=pl.ANY)
-    if array in (PRE, POST):
+    if array in (PRE, POST, TOT):
         return pl.BlockSpec(array.shape, lambda t: (0, 0))
     return by_row(array, lead)
 
@@ -867,9 +894,14 @@
     dx0, dzm, dpg0, pre_g1, post_g0 = row_call(
         back_kernel, "back", 3, [a1, b1, dx1], [dpg1, keep1, unit1, inv1, dz, munit0, minv0, g0, gu0], [ln_in, w_proj, ln_mid, w_out],
         [BDX, ROW, ROW32, PRE, POST], 2, eye + gains * 2 + pre_acc + post_acc)
-    dz_new, pre_g0 = row_call(
-        last_kernel, "last", 4, [a0, b0, dx0], [dpg0, keep0, unit0, inv0, dzm], [ln_in, w_proj], [NATIVE, PRE], 2, gains + pre_acc, N)
-    z_out, dz_pair, *grads = finish(z_new, dz_new, [post_g0, post_g1, pre_g0, pre_g1])
+    adders = [pltpu.VMEM(PRE.shape, F32)]
+    for size in (EARLY_SHARE, LATE_SHARE):
+        adders += [pltpu.VMEM((ALL * size, C), BF16), pltpu.VMEM((ALL, size, C), BF16), pltpu.VMEM((size, C), F32)]
+    adders += [pltpu.VMEM(TOT.shape, F32), pltpu.SemaphoreType.DMA((2, 6, ALL))]
+    dz_new, total = row_call(
+        last_kernel, "last", 4, [a0, b0, dx0], [dpg0, keep0, unit0, inv0, dzm], [ln_in, w_proj, post_g0, post_g1, pre_g1],
+        [NATIVE, TOT], 2, gains + pre_acc + adders, N)
+    z_out, dz_pair, *grads = finish(z_new, dz_new, total)
     return z_out[None], dz_pair[None], *grads
 
 

time: 327 us -> 320 us (0.979)
  Pallas kernels: 326 us -> 319 us
    pallas_call x1 -> x0, Pallas kernels: 24 us -> none  [finish(): pl.pallas_call(sum_kernel, in_specs=[vmem] * 4, out_specs=vmem, out_shape...]
    pallas_call x5, Pallas kernels: 296 us -> 313 us  [row_call(): pl.pallas_call(kernel, grid=(STEPS + lead,), in_specs=[far if tris else b...]
where the time goes in v9:
time: 320 us
  Pallas kernels  319 us (100%)
    pallas_call x5, Pallas kernels, row_call(): pl.pallas_call(kernel, grid=(STEPS + lead,), in_specs=[far if tris else b...  313 us

profile of v9, /device:TPU:0, one launch (start us, length us, event | category | flops | bytes accessed | tf_op | source)
XLA Modules:
  0.0 319.6 jit_solution(17651691621594870444)
XLA Ops:
  0.6 55.9 %pre0.1 = (bf16[64,128,256]{2,1,0:T(8,128)(2,1)}, bf16[64,128,256]{2,1,0:T(8,128)(2,1)}, f32[32,128,256]{2,1,0:T(8,128)}, f32[32,4,128,256]{3,2,1,0:T(8,128)}, f...) custom-call(bf16[32,256,128]{2,1,0:T(8,128)(2,1)} %bitcast.7, s32[4,8,256]{2,1,0:T(8,128)} %bitcast.9, ...), custom_call_target="tpu_custom_call" | custom-call | tf_op jit(solution)/shard_map/pre0/pallas_call | solution.py:865
  56.5 67.6 %mid.1 = (bf16[16,256,256]{2,1,0:T(8,128)(2,1)}, bf16[16,256,256]{2,1,0:T(8,128)(2,1)}, f32[32,128,256]{2,1,0:T(8,128)}, f32[32,4,128,256]{3,2,1,0:T(8,128)}, f3...) custom-call(bf16[64,128,256]{2,1,0:T(8,128)(2,1)} %get-tuple-element, ...), custom_call_target="tpu_custom_call" | custom-call | tf_op jit(solution)/shard_map/mid/pallas_call | solution.py:865
  124.1 52.3 %turn.1 = (bf16[16,256,256]{2,1,0:T(8,128)(2,1)}, bf16[32,256,128]{2,1,0:T(8,128)(2,1)}, f32[32,128,256]{2,1,0:T(8,128)}, f32[144,128]{1,0:T(8,128)}) custom-call(bf16[16,256,256]{2,1,0:T(8,128)(2,1)} %get-tuple-element.46.refs_0_, bf16[16,256,256]{2,1,0:T(8,128)(2,1)} %get-tuple-element.47.refs_1_, bf16[32,128,256]{2,1,0:T(8,128)(2,1)} %get-tuple-element.48.refs_2_, ...), custom_call_target="tpu_custom_call" | custom-call | tf_op jit(solution)/shard_map/turn/pallas_call | solution.py:865
  176.4 66.6 %back.1 = (bf16[64,128,128]{2,1,0:T(8,128)(2,1)}, bf16[32,128,256]{2,1,0:T(8,128)(2,1)}, f32[32,128,256]{2,1,0:T(8,128)}, f32[656,128]{1,0:T(8,128)}, f32[144,128]{1,0:T(8,128)}) custom-call(bf16[16,256,256]{2,1,0:T(8,128)(2,1)} %get-tuple-element.46.refs_0_, bf16[16,256,256]{2,1,0:T(8,128)(2,1)} %get-tuple-element.47.refs_1_, ...), custom_call_target="tpu_custom_call" | custom-call | tf_op jit(solution)/shard_map/back/pallas_call | solution.py:865
  243.1 70.8 %last.1 = (bf16[32,256,128]{2,1,0:T(8,128)(2,1)}, f32[1792,128]{1,0:T(8,128)}) custom-call(bf16[64,128,256]{2,1,0:T(8,128)(2,1)} %get-tuple-element.43.refs_0_, bf16[64,128,256]{2,1,0:T(8,128)(2,1)} %get-tuple-element.44.refs_1_, bf16[64,128,128]{2,1,0:T(8,128)(2,1)} %get-tuple-element.59.refs_2_, f32[32,128,256]{2,1,0:T(8,128)} %get-tuple-element.60.refs_3_, ...), custom_call_target="tpu_custom_call" | custom-call | tf_op jit(solution)/shard_map/last/pallas_call | solution.py:865
  313.9 5.5 %split.1 = (bf16[32,256,128]{2,1,0:T(8,128)(2,1)}, bf16[32,256,128]{2,1,0:T(8,128)(2,1)}, f32[2,2,128]{2,1,0:T(2,128)}, f32[2,128,640]{2,1,0:T(8,128)}, f32[2,64...) custom-call(bf16[32,256,128]{2,1,0:T(8,128)(2,1)} %get-tuple-element.50.z_in, ...), custom_call_target="tpu_custom_call" | custom-call | tf_op jit(solution)/shard_map/split/pallas_call | solution.py:803

commit v10 on v9

--- a/solution.py
+++ b/solution.py
@@ -211,17 +211,21 @@
 
 
 def send_rows(step, jobs):
-    for (pack, copies), stage, send_ref, out_ref, send_sem, recv_sem in jobs:
+    for (pack, copies), stage, send_ref, out_ref, send_sem, recv_sems, k in jobs:
         pack(stage, send_ref, step)
-        for copy in copies(send_ref, out_ref, send_sem, recv_sem, step):
+        for copy in copies(send_ref, out_ref, send_sem, recv_sems.at[k], step):
             copy.start()
-
-    @pl.when(step == STEPS - 1)
-    def _():
-        for (pack, copies), stage, send_ref, out_ref, send_sem, recv_sem in jobs:
-            for slot in range(STEPS):
-                wait_sends(copies(send_ref, out_ref, send_sem, recv_sem, slot))
-            pltpu.make_async_copy(out_ref, out_ref, recv_sem).wait()
+    PENDING.extend(jobs)
+
+
+PENDING = []
+
+
+def finish_rows(jobs):
+    for (pack, copies), stage, send_ref, out_ref, send_sem, recv_sems, k in jobs:
+        for slot in range(STEPS):
+            wait_sends(copies(send_ref, out_ref, send_sem, recv_sems.at[k], slot))
+        pltpu.make_async_copy(out_ref, out_ref, recv_sems.at[k]).wait()
 
 
 OUT_FWD = (lambda c, a, b: nt(a[c], b[c]),)
@@ -376,19 +380,28 @@
     return land_ref[t, 0, r].astype(F32) + land_ref[t, 1, r].astype(F32)
 
 
-def staged_kernel(inner, n_tri, n_in, *refs):
-    far, refs = refs[:n_tri + n_in], refs[n_tri + n_in:]
-    near, refs = refs[-2 - n_tri - n_in:-2], refs[:-2 - n_tri - n_in] + refs[-2:]
-    refs, (tri_sem, row_sem) = refs[:-2], refs[-2:]
+def staged_kernel(inner, n_tri, n_in, n_const, outs, *refs):
+    n_far = n_tri + n_in
+    far, consts, refs = refs[:n_far], refs[n_far:n_far + n_const], refs[n_far + n_const:]
+    results, refs = list(refs[:len(outs)]), refs[len(outs):]
+    tri_sem, row_sem, out_sem = refs[-3:]
+    rows_out = [k for k, out in enumerate(outs) if is_rows(out)]
+    n_near = n_far + len(rows_out)
+    refs, near = refs[:-3 - n_near], refs[-3 - n_near:-3]
     step = step_now()
+    slot = (step + 1) % 2
     tris = [Piecewise(far[k], near[k], tri_sem.at[k]) for k in range(n_tri)]
+    targets = [results[k] for k in rows_out]
+    for k, ref in zip(rows_out, near[n_far:]):
+        results[k] = ref.at[slot]
 
     def fetch(t, slot):
-        out = []
-        for k in range(n_in):
-            size = far[n_tri + k].shape[0] // STEPS
-            out.append(pltpu.make_async_copy(far[n_tri + k].at[pl.ds(t * size, size)], near[n_tri + k].at[slot], row_sem.at[slot, k]))
-        return out
+        return [pltpu.make_async_copy(block_of(whole_ref, t), ref.at[slot], row_sem.at[slot, k])
+                for k, (whole_ref, ref) in enumerate(zip(far[n_tri:], near[n_tri:n_far]))]
+
+    def store(t, slot):
+        return [pltpu.make_async_copy(ref.at[slot], block_of(whole_ref, t), out_sem.at[slot, k])
+                for k, (whole_ref, ref) in enumerate(zip(targets, near[n_far:]))]
 
     @pl.when(step == 0)
     def _():
@@ -398,8 +411,6 @@
         for copy in fetch(0, 0):
             copy.start()
 
-    slot = (step + 1) % 2
-
     @pl.when(step > 0)
     def _():
         for copy in fetch(step - 1, slot):
@@ -410,7 +421,34 @@
         for copy in fetch(step, 1 - slot):
             copy.start()
 
-    inner(*tris, *[ref.at[slot] for ref in near[n_tri:]], *refs)
+    @pl.when(step > 2)
+    def _():
+        for copy in store(step - 3, slot):
+            copy.wait()
+
+    PENDING.clear()
+    inner(*tris, *[ref.at[slot] for ref in near[n_tri:n_far]], *consts, *results, *refs)
+    jobs = list(PENDING)
+
+    @pl.when(step > 0)
+    def _():
+        for copy in store(step - 1, slot):
+            copy.start()
+
+    @pl.when(step == STEPS)
+    def _():
+        finish_rows(jobs)
+        for copy in store(step - 2, 1 - slot) + store(step - 1, slot):
+            copy.wait()
+
+
+def block_of(ref, t):
+    size = ref.shape[0] // STEPS
+    return ref.at[pl.ds(t * size, size)]
+
+
+def is_rows(out):
+    return out not in (PRE, POST, TOT, *SENT)
 
 
 def arrive(t, jobs):
@@ -459,14 +497,18 @@
         enter()
         set_eye(eye_ref)
         set_pre(0, ln_in, w_proj, b_proj, ln_ref, w_t_ref, bias_ref)
-
-    @rows_loop
-    def _(r):
-        z_t = nt(eye_ref[...], z_ref[r])
-        pre_row(r, z_t, mask_ref, ln_ref, w_t_ref, bias_ref, g_ref, keep_ref, unit_ref, inv_ref, a_st, b_st)
-
-    pl.when(step == 0)(all_in)
-    send_rows(step, [(A_ROWS, a_st, a_send, a_ref, a_ss, rs.at[0]), (B_ROWS, b_st, b_send, b_ref, b_ss, rs.at[1])])
+        all_in()
+
+    @pl.when(step > 0)
+    def _():
+        t = step - 1
+
+        @rows_loop
+        def _(r):
+            z_t = nt(eye_ref[...], z_ref[r])
+            pre_row(r, z_t, mask_ref, ln_ref, w_t_ref, bias_ref, g_ref, keep_ref, unit_ref, inv_ref, a_st, b_st)
+
+        send_rows(t, [(A_ROWS, a_st, a_send, a_ref, a_ss, rs, 0), (B_ROWS, b_st, b_send, b_ref, b_ss, rs, 1)])
 
 
 def mid_kernel(a_in, b_in, z_ref, g0_ref, mask_ref, ln_mid, w_out, b_out, ln_in, w_proj, b_proj,
@@ -503,7 +545,7 @@
             zm_ref[r] = z_new
             pre_row(r, z_new.astype(F32), mask_ref, ln_ref, w_t_ref, bias_ref, g_ref, keep_ref, unit_ref, inv_ref, a_st, b_st)
 
-        send_rows(t, [(ROWS_ALL, a_st, a_send, a_ref, a_ss, rs.at[0]), (ROWS_ALL, b_st, b_send, b_ref, b_ss, rs.at[1])])
+        send_rows(t, [(ROWS_ALL, a_st, a_send, a_ref, a_ss, rs, 0), (ROWS_ALL, b_st, b_send, b_ref, b_ss, rs, 1)])
 
 
 def post_back_row(unit, inv, g, dz, mln_ref, wo_ref, acc_ref, x_hat=None):
@@ -561,7 +603,7 @@
         def _():
             put_post(grad_ref, acc_ref)
 
-        send_rows(t, [(ROWS_ALL, d_st, d_send, dx_ref, d_ss, rs.at[0])])
+        send_rows(t, [(ROWS_ALL, d_st, d_send, dx_ref, d_ss, rs, 0)])
 
 
 def pre_back_row(unit, inv, keep, da, db, d_pg, ln_ref, w_ref, w_acc, b_acc, l_acc):
@@ -634,7 +676,7 @@
             put_pre(grad1_ref, w_acc, b_acc, l_acc)
             put_post(grad0_ref, acc_ref)
 
-        send_rows(t, [(DX_ROWS, d_st, d_send, dx_ref, d_ss, rs.at[0])])
+        send_rows(t, [(DX_ROWS, d_st, d_send, dx_ref, d_ss, rs, 0)])
 
 
 ALL = 16
@@ -825,9 +867,9 @@
 INV = jax.ShapeDtypeStruct((STEPS, STEP, N), F32)
 
 
-def by_row(array, lead=0):
+def by_row(array):
     tail = array.shape[1:]
-    return pl.BlockSpec((array.shape[0] // STEPS,) + tail, lambda s: ((s * STEPS) // (STEPS + lead),) + (0,) * len(tail))
+    return pl.BlockSpec((array.shape[0] // STEPS,) + tail, lambda t: (t,) + (0,) * len(tail))
 
 
 def whole(array):
@@ -835,16 +877,7 @@
     return pl.BlockSpec(array.shape, lambda t: zeros, pipeline_mode=pl.Buffered(1))
 
 
-def out_spec(array, lead):
-    if array in SENT:
-        return pl.BlockSpec(memory_space=pl.ANY)
-    if array in (PRE, POST, TOT):
-        return pl.BlockSpec(array.shape, lambda t: (0, 0))
-    return by_row(array, lead)
-
-
 def row_call(kernel, name, collective_id, tris, ins, consts, outs, n_back, scratch, width=0):
-    lead = 1 if tris else 0
     n_send = sum(out in SENT for out in outs)
     packed = (STEPS, 2, C, STEP, BLOCK) if BDX in outs else (STEPS, C, STEP, N)
     dma = pltpu.SemaphoreType.DMA
@@ -857,16 +890,15 @@
         back += [pltpu.VMEM((STEPS, 4, STEP, BCH, width), BF16)] * n_back + [pltpu.VMEM((STEPS, 2, STEP, C, width), BF16)] * n_back
     back += [dma((STEPS, GROUP))] * (2 * n_back)
     far = pl.BlockSpec(memory_space=pl.ANY)
-    near = []
-    if tris:
-        near = [pltpu.VMEM(x.shape, x.dtype) for x in tris] + [pltpu.VMEM((2, x.shape[0] // STEPS) + x.shape[1:], x.dtype) for x in ins]
-        near += [dma((len(tris), GROUPS)), dma((2, len(ins)))]
-        kernel = functools.partial(staged_kernel, kernel, len(tris), len(ins))
+    rows_out = [out for out in outs if is_rows(out)]
+    near = [pltpu.VMEM(x.shape, x.dtype) for x in tris]
+    near += [pltpu.VMEM((2, x.shape[0] // STEPS) + x.shape[1:], x.dtype) for x in [*ins, *rows_out]]
+    near += [dma((max(len(tris), 1), GROUPS)), dma((2, len(ins))), dma((2, len(rows_out)))]
     return pl.pallas_call(
-        kernel,
-        grid=(STEPS + lead,),
-        in_specs=[far if tris else by_row(x) for x in [*tris, *ins]] + [whole(x) for x in consts],
-        out_specs=[out_spec(out, lead) for out in outs],
+        functools.partial(staged_kernel, kernel, len(tris), len(ins), len(consts), outs),
+        grid=(STEPS + 1,),
+        in_specs=[far] * (len(tris) + len(ins)) + [whole(x) for x in consts],
+        out_specs=[pl.BlockSpec(out.shape, lambda t: (0, 0)) if out in (PRE, POST, TOT) else far for out in outs],
         out_shape=outs,
         scratch_shapes=sent + scratch + sems + back + near,
         compiler_params=pltpu.CompilerParams(dimension_semantics=("arbitrary",), vmem_limit_bytes=VMEM_LIMIT, collective_id=collective_id, has_side_effects=True),

time: 320 us -> 315 us (0.984)
  Pallas kernels: 319 us -> 314 us
    pallas_call x5, Pallas kernels: 313 us -> 309 us  [row_call(): pl.pallas_call(functools.partial(staged_kernel, kernel, len(tris), len(in...]
where the time goes in v10:
time: 315 us
  Pallas kernels  314 us (100%)
    pallas_call x5, Pallas kernels, row_call(): pl.pallas_call(functools.partial(staged_kernel, kernel, len(tris), len(in...  309 us

profile of v10, /device:TPU:0, one launch (start us, length us, event | category | flops | bytes accessed | tf_op | source)
XLA Modules:
  0.0 314.8 jit_solution(1689995758253589118)
XLA Ops:
  0.6 54.9 %pre0.1 = (bf16[64,128,256]{2,1,0:T(8,128)(2,1)}, bf16[64,128,256]{2,1,0:T(8,128)(2,1)}, f32[32,128,256]{2,1,0:T(8,128)}, f32[32,4,128,256]{3,2,1,0:T(8,128)}, f...) custom-call(bf16[32,256,128]{2,1,0:T(8,128)(2,1)} %bitcast.7, s32[4,8,256]{2,1,0:T(8,128)} %bitcast.9, ...), custom_call_target="tpu_custom_call" | custom-call | tf_op jit(solution)/shard_map/pre0/pallas_call | solution.py:897
  55.5 63.6 %mid.1 = (bf16[16,256,256]{2,1,0:T(8,128)(2,1)}, bf16[16,256,256]{2,1,0:T(8,128)(2,1)}, f32[32,128,256]{2,1,0:T(8,128)}, f32[32,4,128,256]{3,2,1,0:T(8,128)}, f3...) custom-call(bf16[64,128,256]{2,1,0:T(8,128)(2,1)} %get-tuple-element, ...), custom_call_target="tpu_custom_call" | custom-call | tf_op jit(solution)/shard_map/mid/pallas_call | solution.py:897
  119.1 52.5 %turn.1 = (bf16[16,256,256]{2,1,0:T(8,128)(2,1)}, bf16[32,256,128]{2,1,0:T(8,128)(2,1)}, f32[32,128,256]{2,1,0:T(8,128)}, f32[144,128]{1,0:T(8,128)}) custom-call(bf16[16,256,256]{2,1,0:T(8,128)(2,1)} %get-tuple-element.46.refs_0_, bf16[16,256,256]{2,1,0:T(8,128)(2,1)} %get-tuple-element.47.refs_1_, bf16[32,128,256]{2,1,0:T(8,128)(2,1)} %get-tuple-element.48.refs_2_, ...), custom_call_target="tpu_custom_call" | custom-call | tf_op jit(solution)/shard_map/turn/pallas_call | solution.py:897
  171.6 66.3 %back.1 = (bf16[64,128,128]{2,1,0:T(8,128)(2,1)}, bf16[32,128,256]{2,1,0:T(8,128)(2,1)}, f32[32,128,256]{2,1,0:T(8,128)}, f32[656,128]{1,0:T(8,128)}, f32[144,128]{1,0:T(8,128)}) custom-call(bf16[16,256,256]{2,1,0:T(8,128)(2,1)} %get-tuple-element.46.refs_0_, bf16[16,256,256]{2,1,0:T(8,128)(2,1)} %get-tuple-element.47.refs_1_, ...), custom_call_target="tpu_custom_call" | custom-call | tf_op jit(solution)/shard_map/back/pallas_call | solution.py:897
  237.9 71.3 %last.1 = (bf16[32,256,128]{2,1,0:T(8,128)(2,1)}, f32[1792,128]{1,0:T(8,128)}) custom-call(bf16[64,128,256]{2,1,0:T(8,128)(2,1)} %get-tuple-element.43.refs_0_, bf16[64,128,256]{2,1,0:T(8,128)(2,1)} %get-tuple-element.44.refs_1_, bf16[64,128,128]{2,1,0:T(8,128)(2,1)} %get-tuple-element.59.refs_2_, f32[32,128,256]{2,1,0:T(8,128)} %get-tuple-element.60.refs_3_, ...), custom_call_target="tpu_custom_call" | custom-call | tf_op jit(solution)/shard_map/last/pallas_call | solution.py:897
  309.2 5.5 %split.1 = (bf16[32,256,128]{2,1,0:T(8,128)(2,1)}, bf16[32,256,128]{2,1,0:T(8,128)(2,1)}, f32[2,2,128]{2,1,0:T(2,128)}, f32[2,128,640]{2,1,0:T(8,128)}, f32[2,64...) custom-call(bf16[32,256,128]{2,1,0:T(8,128)(2,1)} %get-tuple-element.50.z_in, ...), custom_call_target="tpu_custom_call" | custom-call | tf_op jit(solution)/shard_map/split/pallas_call | solution.py:845

commit v11 on v10

--- a/solution.py
+++ b/solution.py
@@ -819,10 +819,21 @@
             tot_out[...] = tot_ref[...]
 
 
-def split_kernel(z_in, dz_in, tot, z_out, dz_out, *grads):
-    z_out[...] = z_in[...]
-    dz_out[...] = dz_in[...]
-    pl.when(step_now() == 0)(lambda: split_grads(tot, *grads))
+def split_kernel(z_in, dz_in, tot_in, z_out, dz_out, *refs):
+    grads, (tot, buf, sems, tot_sem) = refs[:6], refs[6:]
+    pairs = [(k, t, *pair) for t in range(STEPS) for k, pair in enumerate(((z_in, z_out), (dz_in, dz_out)))]
+    loads = [pltpu.make_async_copy(block_of(src, t), buf.at[k, t], sems.at[0, k, t]) for k, t, src, dst in pairs]
+    stores = [pltpu.make_async_copy(buf.at[k, t], block_of(dst, t), sems.at[1, k, t]) for k, t, src, dst in pairs]
+    load_tot = pltpu.make_async_copy(tot_in, tot, tot_sem)
+    for copy in [load_tot, *loads]:
+        copy.start()
+    load_tot.wait()
+    split_grads(tot, *grads)
+    for load, store in zip(loads, stores):
+        load.wait()
+        store.start()
+    for store in stores:
+        store.wait()
 
 
 def split_grads(tot, d_ln_in, d_w_proj, d_b_proj, d_ln_mid, d_w_out, d_b_out):
@@ -842,13 +853,15 @@
 def finish(z_new, dz_new, total):
     shapes = ((2, 2, C), (2, C, PROJ), (2, PROJ), (2, 2, C), (2, C, C), (2, C))
     grads = [jax.ShapeDtypeStruct(shape, F32) for shape in shapes]
+    far, near = pl.BlockSpec(memory_space=pl.ANY), pl.BlockSpec(memory_space=pltpu.VMEM)
+    dma = pltpu.SemaphoreType.DMA
     return pl.pallas_call(
         split_kernel,
-        grid=(STEPS,),
-        in_specs=[by_row(z_new), by_row(dz_new), whole(total)],
-        out_specs=[by_row(NATIVE)] * 2 + [pl.BlockSpec(x.shape, lambda t, n=len(x.shape): (0,) * n) for x in grads],
+        in_specs=[far] * 3,
+        out_specs=[far] * 2 + [near] * len(grads),
         out_shape=[NATIVE] * 2 + grads,
-        compiler_params=pltpu.CompilerParams(dimension_semantics=("arbitrary",)),
+        scratch_shapes=[pltpu.VMEM(TOT.shape, F32), pltpu.VMEM((2, STEPS, STEP, N, C), BF16), dma((2, 2, STEPS)), dma],
+        compiler_params=pltpu.CompilerParams(vmem_limit_bytes=VMEM_LIMIT),
         name="split",
     )(z_new, dz_new, total)
 
@@ -865,11 +878,6 @@
 TOT = jax.ShapeDtypeStruct((ALL * (EARLY_SHARE + LATE_SHARE), C), F32)
 KEEP = jax.ShapeDtypeStruct((ROWS, 4, C, N), F32)
 INV = jax.ShapeDtypeStruct((STEPS, STEP, N), F32)
-
-
-def by_row(array):
-    tail = array.shape[1:]
-    return pl.BlockSpec((array.shape[0] // STEPS,) + tail, lambda t: (t,) + (0,) * len(tail))
 
 
 def whole(array):

time: 315 us -> 315 us (level)
  no operation moved by 1% of the time
where the time goes in v11:
time: 315 us
  Pallas kernels  314 us (100%)
    pallas_call x5, Pallas kernels, row_call(): pl.pallas_call(functools.partial(staged_kernel, kernel, len(tris), len(in...  309 us

profile of v11, /device:TPU:0, one launch (start us, length us, event | category | flops | bytes accessed | tf_op | source)
XLA Modules:
  0.0 314.9 jit_solution(8520072255145940265)
XLA Ops:
  0.6 54.9 %pre0.1 = (bf16[64,128,256]{2,1,0:T(8,128)(2,1)}, bf16[64,128,256]{2,1,0:T(8,128)(2,1)}, f32[32,128,256]{2,1,0:T(8,128)}, f32[32,4,128,256]{3,2,1,0:T(8,128)}, f...) custom-call(bf16[32,256,128]{2,1,0:T(8,128)(2,1)} %bitcast.7, s32[4,8,256]{2,1,0:T(8,128)} %bitcast.9, ...), custom_call_target="tpu_custom_call" | custom-call | tf_op jit(solution)/shard_map/pre0/pallas_call | solution.py:905
  55.5 63.6 %mid.1 = (bf16[16,256,256]{2,1,0:T(8,128)(2,1)}, bf16[16,256,256]{2,1,0:T(8,128)(2,1)}, f32[32,128,256]{2,1,0:T(8,128)}, f32[32,4,128,256]{3,2,1,0:T(8,128)}, f3...) custom-call(bf16[64,128,256]{2,1,0:T(8,128)(2,1)} %get-tuple-element, ...), custom_call_target="tpu_custom_call" | custom-call | tf_op jit(solution)/shard_map/mid/pallas_call | solution.py:905
  119.1 52.5 %turn.1 = (bf16[16,256,256]{2,1,0:T(8,128)(2,1)}, bf16[32,256,128]{2,1,0:T(8,128)(2,1)}, f32[32,128,256]{2,1,0:T(8,128)}, f32[144,128]{1,0:T(8,128)}) custom-call(bf16[16,256,256]{2,1,0:T(8,128)(2,1)} %get-tuple-element.46.refs_0_, bf16[16,256,256]{2,1,0:T(8,128)(2,1)} %get-tuple-element.47.refs_1_, bf16[32,128,256]{2,1,0:T(8,128)(2,1)} %get-tuple-element.48.refs_2_, ...), custom_call_target="tpu_custom_call" | custom-call | tf_op jit(solution)/shard_map/turn/pallas_call | solution.py:905
  171.6 66.3 %back.1 = (bf16[64,128,128]{2,1,0:T(8,128)(2,1)}, bf16[32,128,256]{2,1,0:T(8,128)(2,1)}, f32[32,128,256]{2,1,0:T(8,128)}, f32[656,128]{1,0:T(8,128)}, f32[144,128]{1,0:T(8,128)}) custom-call(bf16[16,256,256]{2,1,0:T(8,128)(2,1)} %get-tuple-element.46.refs_0_, bf16[16,256,256]{2,1,0:T(8,128)(2,1)} %get-tuple-element.47.refs_1_, ...), custom_call_target="tpu_custom_call" | custom-call | tf_op jit(solution)/shard_map/back/pallas_call | solution.py:905
  237.9 71.3 %last.1 = (bf16[32,256,128]{2,1,0:T(8,128)(2,1)}, f32[1792,128]{1,0:T(8,128)}) custom-call(bf16[64,128,256]{2,1,0:T(8,128)(2,1)} %get-tuple-element.43.refs_0_, bf16[64,128,256]{2,1,0:T(8,128)(2,1)} %get-tuple-element.44.refs_1_, bf16[64,128,128]{2,1,0:T(8,128)(2,1)} %get-tuple-element.59.refs_2_, f32[32,128,256]{2,1,0:T(8,128)} %get-tuple-element.60.refs_3_, ...), custom_call_target="tpu_custom_call" | custom-call | tf_op jit(solution)/shard_map/last/pallas_call | solution.py:905
  309.2 5.6 %split.1 = (bf16[32,256,128]{2,1,0:T(8,128)(2,1)}, bf16[32,256,128]{2,1,0:T(8,128)(2,1)}, f32[2,2,128]{2,1,0:T(2,128)}, f32[2,128,640]{2,1,0:T(8,128)}, f32[2,64...) custom-call(bf16[32,256,128]{2,1,0:T(8,128)(2,1)} %get-tuple-element.50.z_in, ...), custom_call_target="tpu_custom_call" | custom-call | tf_op jit(solution)/shard_map/split/pallas_call | solution.py:858

commit v12 on v11

--- a/solution.py
+++ b/solution.py
@@ -241,7 +241,7 @@
         device_id={"dap": dest}, device_id_type=pl.DeviceIdType.MESH)
 
 
-EARLY = 2
+EARLY = 1
 GROUPS = 4
 
 

time: 315 us -> 316 us (level)
  no operation moved by 1% of the time
where the time goes in v12:
time: 316 us
  Pallas kernels  315 us (100%)
    pallas_call x5, Pallas kernels, row_call(): pl.pallas_call(functools.partial(staged_kernel, kernel, len(tris), len(in...  309 us

profile of v12, /device:TPU:0, one launch (start us, length us, event | category | flops | bytes accessed | tf_op | source)
XLA Modules:
  0.0 315.7 jit_solution(3575818097356369397)
XLA Ops:
  0.6 54.9 %pre0.1 = (bf16[64,128,256]{2,1,0:T(8,128)(2,1)}, bf16[64,128,256]{2,1,0:T(8,128)(2,1)}, f32[32,128,256]{2,1,0:T(8,128)}, f32[32,4,128,256]{3,2,1,0:T(8,128)}, f...) custom-call(bf16[32,256,128]{2,1,0:T(8,128)(2,1)} %bitcast.7, s32[4,8,256]{2,1,0:T(8,128)} %bitcast.9, ...), custom_call_target="tpu_custom_call" | custom-call | tf_op jit(solution)/shard_map/pre0/pallas_call | solution.py:905
  55.5 64.7 %mid.1 = (bf16[16,256,256]{2,1,0:T(8,128)(2,1)}, bf16[16,256,256]{2,1,0:T(8,128)(2,1)}, f32[32,128,256]{2,1,0:T(8,128)}, f32[32,4,128,256]{3,2,1,0:T(8,128)}, f3...) custom-call(bf16[64,128,256]{2,1,0:T(8,128)(2,1)} %get-tuple-element, ...), custom_call_target="tpu_custom_call" | custom-call | tf_op jit(solution)/shard_map/mid/pallas_call | solution.py:905
  120.2 52.3 %turn.1 = (bf16[16,256,256]{2,1,0:T(8,128)(2,1)}, bf16[32,256,128]{2,1,0:T(8,128)(2,1)}, f32[32,128,256]{2,1,0:T(8,128)}, f32[144,128]{1,0:T(8,128)}) custom-call(bf16[16,256,256]{2,1,0:T(8,128)(2,1)} %get-tuple-element.46.refs_0_, bf16[16,256,256]{2,1,0:T(8,128)(2,1)} %get-tuple-element.47.refs_1_, bf16[32,128,256]{2,1,0:T(8,128)(2,1)} %get-tuple-element.48.refs_2_, ...), custom_call_target="tpu_custom_call" | custom-call | tf_op jit(solution)/shard_map/turn/pallas_call | solution.py:905
  172.5 66.2 %back.1 = (bf16[64,128,128]{2,1,0:T(8,128)(2,1)}, bf16[32,128,256]{2,1,0:T(8,128)(2,1)}, f32[32,128,256]{2,1,0:T(8,128)}, f32[656,128]{1,0:T(8,128)}, f32[144,128]{1,0:T(8,128)}) custom-call(bf16[16,256,256]{2,1,0:T(8,128)(2,1)} %get-tuple-element.46.refs_0_, bf16[16,256,256]{2,1,0:T(8,128)(2,1)} %get-tuple-element.47.refs_1_, ...), custom_call_target="tpu_custom_call" | custom-call | tf_op jit(solution)/shard_map/back/pallas_call | solution.py:905
  238.7 71.3 %last.1 = (bf16[32,256,128]{2,1,0:T(8,128)(2,1)}, f32[1792,128]{1,0:T(8,128)}) custom-call(bf16[64,128,256]{2,1,0:T(8,128)(2,1)} %get-tuple-element.43.refs_0_, bf16[64,128,256]{2,1,0:T(8,128)(2,1)} %get-tuple-element.44.refs_1_, bf16[64,128,128]{2,1,0:T(8,128)(2,1)} %get-tuple-element.59.refs_2_, f32[32,128,256]{2,1,0:T(8,128)} %get-tuple-element.60.refs_3_, ...), custom_call_target="tpu_custom_call" | custom-call | tf_op jit(solution)/shard_map/last/pallas_call | solution.py:905
  310.0 5.6 %split.1 = (bf16[32,256,128]{2,1,0:T(8,128)(2,1)}, bf16[32,256,128]{2,1,0:T(8,128)(2,1)}, f32[2,2,128]{2,1,0:T(2,128)}, f32[2,128,640]{2,1,0:T(8,128)}, f32[2,64...) custom-call(bf16[32,256,128]{2,1,0:T(8,128)(2,1)} %get-tuple-element.50.z_in, ...), custom_call_target="tpu_custom_call" | custom-call | tf_op jit(solution)/shard_map/split/pallas_call | solution.py:858
